TPU v7x, 512 devices: a whole 4x8x8 slice. The times are simulated.
512 devices in a mesh: depth: 2 (over core), lat: 256 (over z, y, x).
Axes of the slice: x: 4, y: 8, z: 8, core: 2. Of those that a mesh axis runs over, the one named last changes fastest.
Arguments:
- temp_old: float32 [256, 1024, 512], P('depth', 'lat'), may hold values from -6 to 6
- source: float32 [256, 1024, 512], P('depth', 'lat'), may hold values from -6 to 6
- lat_couple: float32 [256], P('depth'), may hold values from 0.05 to 0.2
- face_couple: float32 [1], replicated, may hold values from 0.5 to 2
- block_inverse: float32 [256, 128], P('depth'), may hold values from -0.3 to 1.4
Outputs:
- temp_new: float32 [256, 1024, 512], P('depth', 'lat')
All inputs are finite; a program needn't handle non-finite values.
Results may differ from a plain program's by a relative error of at most 0.0001.
Values sent between devices are 32-bit elements; how exact they have to be, the bound alone decides.
No kernel may reach another device: no remote copies, remote signals or barrier semaphores. Data moves between devices by JAX's collectives and lax.ppermute only.
A program may use at most 64 MiB of HBM per device.

v0:
```python
import jax
import jax.numpy as jnp
from jax import lax
from jax.sharding import PartitionSpec as P

SWEEPS = 6


def shifted(value, axis, steps):
    count = lax.axis_size(axis)
    first, last = (max(0, -steps), min(count, count - steps))
    return lax.ppermute(value, axis, [(source, source + steps) for source in range(first, last)])


def extended(block, sides, width):
    for axis, dim in sides:
        count = lax.axis_size(axis)
        forward = [(i, i + 1) for i in range(count - 1)]
        backward = [(target, source) for source, target in forward]
        low = lax.ppermute(
            lax.slice_in_dim(block, block.shape[dim] - width, None, axis=dim), axis, forward
        )
        high = lax.ppermute(lax.slice_in_dim(block, 0, width, axis=dim), axis, backward)
        block = jnp.concatenate([low, block, high], axis=dim)
    return block


def apply_inverse(inverse, values):
    depth_cells = inverse.shape[0]
    flat = values.reshape(depth_cells, -1)
    return jnp.dot(
        inverse, flat, precision=lax.Precision.HIGHEST, preferred_element_type=jnp.float32
    ).reshape(values.shape)


def across_columns(field):
    padded = jnp.pad(field, ((0, 0), (0, 0), (1, 1)))
    return padded[:, :, 2:] + padded[:, :, :-2]


def local(temp_old, source, lat_couple, face_couple, block_inverse):
    depth_count = lax.axis_size("depth")
    slab_index = lax.axis_index("depth")
    depth_cells, row_count, col_count = temp_old.shape
    couple_above = jnp.where(slab_index > 0, face_couple[jnp.maximum(slab_index - 1, 0)], 0.0)
    couple_below = face_couple[jnp.minimum(slab_index, depth_count - 2)]
    tail_gain = block_inverse[depth_cells - 1, 0] * couple_above
    first_column = block_inverse[:, 0] * couple_above
    weights = lat_couple[:, None, None]
    field = temp_old
    for sweep_index in range(SWEEPS):
        under_layer = shifted(field[0], "depth", -1)
        padded = extended(field, (("lat", 1),), 1)
        across_rows = padded[:, 2:] + padded[:, :-2]
        right_side = source + weights * (across_rows + across_columns(field))
        right_side = right_side.at[depth_cells - 1].add(couple_below * under_layer)
        solved = apply_inverse(block_inverse, right_side)
        bottom = solved[depth_cells - 1]
        incoming = jnp.zeros_like(bottom)
        incoming = shifted(bottom + tail_gain * incoming, "depth", 1)
        field = solved + first_column[:, None, None] * incoming[None]
    return field


def solution(mesh):
    return jax.shard_map(
        local,
        mesh=mesh,
        in_specs=(
            P("depth", "lat", None),
            P("depth", "lat", None),
            P("depth"),
            P(),
            P("depth", None),
        ),
        out_specs=P("depth", "lat", None),
        check_vma=False,
    )
```

profile of v0, /device:TPU:257, one launch (start us, length us, event | category | flops | bytes accessed | tf_op | source)
XLA Modules:
  0.0 161.4 jit_solution(7437332650999085548)
XLA Ops:
  0.0 2.1 %fusion.47 = (f32[128,1,512]{2,1,0:T(1,128)S(1)}, f32[128,1,512]{2,1,0:T(1,128)S(1)}) fusion(f32[128,4,512]{2,1,0:T(4,128)} %param.17), kind=kLoop, calls=%fused_computation.96 | loop fusion | bytes 1048576 | tf_op jit(solution)/shard_map/slice | solution.py:23
  2.1 6.4 %collective-permute-start = (f32[128,1,512]{2,1,0:T(1,128)S(1)}, f32[128,1,512]{2,1,0:T(1,128)S(1)}, u32[]{:S(2)}, u32[]{:S(2)}) collective-permute-start(f32[128,1,512]{2,1,0:T(1,128)S(1)} %get-tuple-element.87), channel_id=1, source_target_pairs={{1,0},{2,1},{3,2},{4,3},{5,4},{6,5},{7,6},{8,7},{9,8},{10,9},{11,1... | collective-permute-start | bytes 786440 | tf_op jit(solution)/shard_map/ppermute | solution.py:23
  8.5 1.9 %collective-permute-start.1 = (f32[128,1,512]{2,1,0:T(1,128)S(1)}, f32[128,1,512]{2,1,0:T(1,128)S(1)}, u32[]{:S(2)}, u32[]{:S(2)}) collective-permute-start(f32[128,1,512]{2,1,0:T(1,128)S(1)} %get-tuple-element.88), channel_id=1, source_target_pairs={{0,1},{1,2},{2,3},{3,4},{4,5},{5,6},{6,7},{7,8},{8,9},{9,10},{10,1... | collective-permute-start | bytes 786440 | tf_op jit(solution)/shard_map/ppermute | solution.py:20
  11.1 2.8 %collective-permute-start.2 = (f32[4,512]{1,0:T(4,128)S(1)}, f32[4,512]{1,0:T(4,128)S(1)}, u32[]{:S(2)}, u32[]{:S(2)}) collective-permute-start(f32[4,512]{1,0:T(4,128)S(1)} %slice_bitcast_fusion.5), channel_id=1, source_target_pairs={{256,0},{257,1},{258,2},{259,3},{260,4},{261,5},{262,6},{263,7},{2... | collective-permute-start | bytes 24584 | tf_op jit(solution)/shard_map/ppermute | solution.py:12
  16.5 6.2 %collective-permute-done.1 = f32[128,1,512]{2,1,0:T(1,128)S(1)} collective-permute-done((f32[128,1,512]{2,1,0:T(1,128)S(1)}, f32[128,1,512]{2,1,0:T(1,128)S(1)}, u32[]{:S(2)}, u32[]{:S(2)}) %collective-permute-start.1) | collective-permute-done | bytes 262176 | tf_op jit(solution)/shard_map/ppermute | solution.py:20
  22.7 3.9 %fusion.3 = f32[128,4,512]{2,1,0:T(4,128)S(1)} fusion(f32[128,4,512]{2,1,0:T(4,128)S(1)} %copy-done, f32[128,4,512]{2,1,0:T(4,128)} %param.17, f32[128,1,512]{2,1,0:T(1,128)S(1)} %collective-permute-done.1, f32[128,1,512]{2,1,0:T(1,128)S(1)} %collective-permute-done, f32[128]{0:T(128)S(1)} %copy-done.2), kind=kLoop, calls=%fused_computation.15 | loop fusion | flops 1835008 | bytes 3670528 | tf_op jit(solution)/shard_map/add | solution.py:55
  27.5 1.8 %fusion.48 = f32[2048,128]{1,0:T(8,128)S(1)} fusion(f32[128,2048]{1,0:T(8,128)S(1)} %bitcast.93, f32[128,128]{1,0:T(8,128)S(1)} %copy-done.1), kind=kOutput, calls=%fused_computation.97 | convolution fusion | flops 402653184 | bytes 2162688 | tf_op jit(solution)/shard_map/dot_general | solution.py:31
  30.0 1.3 collective-permute-start.3
  31.9 1.8 %collective-permute-done.3 = f32[4,512]{1,0:T(4,128)S(1)} collective-permute-done((f32[4,512]{1,0:T(4,128)S(1)}, f32[4,512]{1,0:T(4,128)S(1)}, u32[]{:S(2)}, u32[]{:S(2)}) %collective-permute-start.3) | collective-permute-done | bytes 8224 | tf_op jit(solution)/shard_map/ppermute | solution.py:12
  34.4 2.2 %collective-permute-start.4 = (f32[128,1,512]{2,1,0:T(1,128)S(1)}, f32[128,1,512]{2,1,0:T(1,128)S(1)}, u32[]{:S(2)}, u32[]{:S(2)}) collective-permute-start(f32[128,1,512]{2,1,0:T(1,128)S(1)} %get-tuple-element.85), channel_id=1, source_target_pairs={{1,0},{2,1},{3,2},{4,3},{5,4},{6,5},{7,6},{8,7},{9,8},{10,9},{11,1... | collective-permute-start | bytes 786440 | tf_op jit(solution)/shard_map/ppermute | solution.py:23
  36.6 3.1 %collective-permute-start.5 = (f32[128,1,512]{2,1,0:T(1,128)S(1)}, f32[128,1,512]{2,1,0:T(1,128)S(1)}, u32[]{:S(2)}, u32[]{:S(2)}) collective-permute-start(f32[128,1,512]{2,1,0:T(1,128)S(1)} %get-tuple-element.86), channel_id=1, source_target_pairs={{0,1},{1,2},{2,3},{3,4},{4,5},{5,6},{6,7},{7,8},{8,9},{9,10},{10,1... | collective-permute-start | bytes 786440 | tf_op jit(solution)/shard_map/ppermute | solution.py:20
  39.7 2.6 %collective-permute-start.6 = (f32[4,512]{1,0:T(4,128)S(1)}, f32[4,512]{1,0:T(4,128)S(1)}, u32[]{:S(2)}, u32[]{:S(2)}) collective-permute-start(f32[4,512]{1,0:T(4,128)S(1)} %slice_bitcast_fusion.4), channel_id=1, source_target_pairs={{256,0},{257,1},{258,2},{259,3},{260,4},{261,5},{262,6},{263,7},{2... | collective-permute-start | bytes 24584 | tf_op jit(solution)/shard_map/ppermute | solution.py:12
  42.4 1.6 %collective-permute-done.4 = f32[128,1,512]{2,1,0:T(1,128)S(1)} collective-permute-done((f32[128,1,512]{2,1,0:T(1,128)S(1)}, f32[128,1,512]{2,1,0:T(1,128)S(1)}, u32[]{:S(2)}, u32[]{:S(2)}) %collective-permute-start.4) | collective-permute-done | bytes 262176 | tf_op jit(solution)/shard_map/ppermute | solution.py:23
  44.0 7.4 %collective-permute-done.5 = f32[128,1,512]{2,1,0:T(1,128)S(1)} collective-permute-done((f32[128,1,512]{2,1,0:T(1,128)S(1)}, f32[128,1,512]{2,1,0:T(1,128)S(1)}, u32[]{:S(2)}, u32[]{:S(2)}) %collective-permute-start.5) | collective-permute-done | bytes 262176 | tf_op jit(solution)/shard_map/ppermute | solution.py:20
  51.4 1.7 %fusion.7 = f32[128,4,512]{2,1,0:T(4,128)S(1)} fusion(f32[128,4,512]{2,1,0:T(4,128)S(1)} %copy-done, f32[128,4,512]{2,1,0:T(4,128)S(1)} %multiply_add_fusion.5, f32[128,1,512]{2,1,0:T(1,128)S(1)} %collective-permute-done.5, f32[128,1,512]{2,1,0:T(1,128)S(1)} %collective-permute-done.4, f32[128]{0:T(128)S(1)} %copy-done.2), kind=kLoop, calls=%fused_computation.19 | loop fusion | flops 1835008 | bytes 3670528 | tf_op jit(solution)/shard_map/add | solution.py:55
  53.5 1.8 %fusion.49 = f32[2048,128]{1,0:T(8,128)S(1)} fusion(f32[128,2048]{1,0:T(8,128)S(1)} %bitcast.94, f32[128,128]{1,0:T(8,128)S(1)} %copy-done.1), kind=kOutput, calls=%fused_computation.98 | convolution fusion | flops 402653184 | bytes 2162688 | tf_op jit(solution)/shard_map/dot_general | solution.py:31
  55.9 1.3 collective-permute-start.7
  57.7 1.4 collective-permute-done.7
  59.8 1.9 %collective-permute-start.8 = (f32[128,1,512]{2,1,0:T(1,128)S(1)}, f32[128,1,512]{2,1,0:T(1,128)S(1)}, u32[]{:S(2)}, u32[]{:S(2)}) collective-permute-start(f32[128,1,512]{2,1,0:T(1,128)S(1)} %get-tuple-element.83), channel_id=1, source_target_pairs={{1,0},{2,1},{3,2},{4,3},{5,4},{6,5},{7,6},{8,7},{9,8},{10,9},{11,1... | collective-permute-start | bytes 786440 | tf_op jit(solution)/shard_map/ppermute | solution.py:23
  61.8 3.4 %collective-permute-start.9 = (f32[128,1,512]{2,1,0:T(1,128)S(1)}, f32[128,1,512]{2,1,0:T(1,128)S(1)}, u32[]{:S(2)}, u32[]{:S(2)}) collective-permute-start(f32[128,1,512]{2,1,0:T(1,128)S(1)} %get-tuple-element.84), channel_id=1, source_target_pairs={{0,1},{1,2},{2,3},{3,4},{4,5},{5,6},{6,7},{7,8},{8,9},{9,10},{10,1... | collective-permute-start | bytes 786440 | tf_op jit(solution)/shard_map/ppermute | solution.py:20
  65.2 2.8 %collective-permute-start.10 = (f32[4,512]{1,0:T(4,128)S(1)}, f32[4,512]{1,0:T(4,128)S(1)}, u32[]{:S(2)}, u32[]{:S(2)}) collective-permute-start(f32[4,512]{1,0:T(4,128)S(1)} %slice_bitcast_fusion.3), channel_id=1, source_target_pairs={{256,0},{257,1},{258,2},{259,3},{260,4},{261,5},{262,6},{263,7},{2... | collective-permute-start | bytes 24584 | tf_op jit(solution)/shard_map/ppermute | solution.py:12
  68.0 1.5 collective-permute-done.8
  69.4 7.4 %collective-permute-done.9 = f32[128,1,512]{2,1,0:T(1,128)S(1)} collective-permute-done((f32[128,1,512]{2,1,0:T(1,128)S(1)}, f32[128,1,512]{2,1,0:T(1,128)S(1)}, u32[]{:S(2)}, u32[]{:S(2)}) %collective-permute-start.9) | collective-permute-done | bytes 262176 | tf_op jit(solution)/shard_map/ppermute | solution.py:20
  76.8 1.7 %fusion.11 = f32[128,4,512]{2,1,0:T(4,128)S(1)} fusion(f32[128,4,512]{2,1,0:T(4,128)S(1)} %copy-done, f32[128,4,512]{2,1,0:T(4,128)S(1)} %multiply_add_fusion.4, f32[128,1,512]{2,1,0:T(1,128)S(1)} %collective-permute-done.9, f32[128,1,512]{2,1,0:T(1,128)S(1)} %collective-permute-done.8, f32[128]{0:T(128)S(1)} %copy-done.2), kind=kLoop, calls=%fused_computation.23 | loop fusion | flops 1835008 | bytes 3670528 | tf_op jit(solution)/shard_map/add | solution.py:55
  78.9 1.8 %fusion.50 = f32[2048,128]{1,0:T(8,128)S(1)} fusion(f32[128,2048]{1,0:T(8,128)S(1)} %bitcast.95, f32[128,128]{1,0:T(8,128)S(1)} %copy-done.1), kind=kOutput, calls=%fused_computation.99 | convolution fusion | flops 402653184 | bytes 2162688 | tf_op jit(solution)/shard_map/dot_general | solution.py:31
  81.4 1.3 collective-permute-start.11
  85.1 1.9 %collective-permute-start.12 = (f32[128,1,512]{2,1,0:T(1,128)S(1)}, f32[128,1,512]{2,1,0:T(1,128)S(1)}, u32[]{:S(2)}, u32[]{:S(2)}) collective-permute-start(f32[128,1,512]{2,1,0:T(1,128)S(1)} %get-tuple-element.81), channel_id=1, source_target_pairs={{1,0},{2,1},{3,2},{4,3},{5,4},{6,5},{7,6},{8,7},{9,8},{10,9},{11,1... | collective-permute-start | bytes 786440 | tf_op jit(solution)/shard_map/ppermute | solution.py:23
  87.0 3.4 %collective-permute-start.13 = (f32[128,1,512]{2,1,0:T(1,128)S(1)}, f32[128,1,512]{2,1,0:T(1,128)S(1)}, u32[]{:S(2)}, u32[]{:S(2)}) collective-permute-start(f32[128,1,512]{2,1,0:T(1,128)S(1)} %get-tuple-element.82), channel_id=1, source_target_pairs={{0,1},{1,2},{2,3},{3,4},{4,5},{5,6},{6,7},{7,8},{8,9},{9,10},{10,1... | collective-permute-start | bytes 786440 | tf_op jit(solution)/shard_map/ppermute | solution.py:20
  90.4 2.6 %collective-permute-start.14 = (f32[4,512]{1,0:T(4,128)S(1)}, f32[4,512]{1,0:T(4,128)S(1)}, u32[]{:S(2)}, u32[]{:S(2)}) collective-permute-start(f32[4,512]{1,0:T(4,128)S(1)} %slice_bitcast_fusion.2), channel_id=1, source_target_pairs={{256,0},{257,1},{258,2},{259,3},{260,4},{261,5},{262,6},{263,7},{2... | collective-permute-start | bytes 24584 | tf_op jit(solution)/shard_map/ppermute | solution.py:12
  93.0 1.6 %collective-permute-done.12 = f32[128,1,512]{2,1,0:T(1,128)S(1)} collective-permute-done((f32[128,1,512]{2,1,0:T(1,128)S(1)}, f32[128,1,512]{2,1,0:T(1,128)S(1)}, u32[]{:S(2)}, u32[]{:S(2)}) %collective-permute-start.12) | collective-permute-done | bytes 262176 | tf_op jit(solution)/shard_map/ppermute | solution.py:23
  94.7 7.4 %collective-permute-done.13 = f32[128,1,512]{2,1,0:T(1,128)S(1)} collective-permute-done((f32[128,1,512]{2,1,0:T(1,128)S(1)}, f32[128,1,512]{2,1,0:T(1,128)S(1)}, u32[]{:S(2)}, u32[]{:S(2)}) %collective-permute-start.13) | collective-permute-done | bytes 262176 | tf_op jit(solution)/shard_map/ppermute | solution.py:20
  102.0 1.7 %fusion.15 = f32[128,4,512]{2,1,0:T(4,128)S(1)} fusion(f32[128,4,512]{2,1,0:T(4,128)S(1)} %copy-done, f32[128,4,512]{2,1,0:T(4,128)S(1)} %multiply_add_fusion.3, f32[128,1,512]{2,1,0:T(1,128)S(1)} %collective-permute-done.13, f32[128,1,512]{2,1,0:T(1,128)S(1)} %collective-permute-done.12, f32[128]{0:T(128)S(1)} %copy-done.2), kind=kLoop, calls=%fused_computation.27 | loop fusion | flops 1835008 | bytes 3670528 | tf_op jit(solution)/shard_map/add | solution.py:55
  104.1 1.8 %fusion.51 = f32[2048,128]{1,0:T(8,128)S(1)} fusion(f32[128,2048]{1,0:T(8,128)S(1)} %bitcast.96, f32[128,128]{1,0:T(8,128)S(1)} %copy-done.1), kind=kOutput, calls=%fused_computation.100 | convolution fusion | flops 402653184 | bytes 2162688 | tf_op jit(solution)/shard_map/dot_general | solution.py:31
  106.6 1.3 collective-permute-start.15
  110.3 1.9 %collective-permute-start.16 = (f32[128,1,512]{2,1,0:T(1,128)S(1)}, f32[128,1,512]{2,1,0:T(1,128)S(1)}, u32[]{:S(2)}, u32[]{:S(2)}) collective-permute-start(f32[128,1,512]{2,1,0:T(1,128)S(1)} %get-tuple-element.79), channel_id=1, source_target_pairs={{1,0},{2,1},{3,2},{4,3},{5,4},{6,5},{7,6},{8,7},{9,8},{10,9},{11,1... | collective-permute-start | bytes 786440 | tf_op jit(solution)/shard_map/ppermute | solution.py:23
  112.3 3.4 %collective-permute-start.17 = (f32[128,1,512]{2,1,0:T(1,128)S(1)}, f32[128,1,512]{2,1,0:T(1,128)S(1)}, u32[]{:S(2)}, u32[]{:S(2)}) collective-permute-start(f32[128,1,512]{2,1,0:T(1,128)S(1)} %get-tuple-element.80), channel_id=1, source_target_pairs={{0,1},{1,2},{2,3},{3,4},{4,5},{5,6},{6,7},{7,8},{8,9},{9,10},{10,1... | collective-permute-start | bytes 786440 | tf_op jit(solution)/shard_map/ppermute | solution.py:20
  115.7 2.9 %collective-permute-start.18 = (f32[4,512]{1,0:T(4,128)S(1)}, f32[4,512]{1,0:T(4,128)S(1)}, u32[]{:S(2)}, u32[]{:S(2)}) collective-permute-start(f32[4,512]{1,0:T(4,128)S(1)} %slice_bitcast_fusion.1), channel_id=1, source_target_pairs={{256,0},{257,1},{258,2},{259,3},{260,4},{261,5},{262,6},{263,7},{2... | collective-permute-start | bytes 24584 | tf_op jit(solution)/shard_map/ppermute | solution.py:12
  118.5 1.4 collective-permute-done.16
  119.9 7.4 %collective-permute-done.17 = f32[128,1,512]{2,1,0:T(1,128)S(1)} collective-permute-done((f32[128,1,512]{2,1,0:T(1,128)S(1)}, f32[128,1,512]{2,1,0:T(1,128)S(1)}, u32[]{:S(2)}, u32[]{:S(2)}) %collective-permute-start.17) | collective-permute-done | bytes 262176 | tf_op jit(solution)/shard_map/ppermute | solution.py:20
  127.3 1.7 %fusion.19 = f32[128,4,512]{2,1,0:T(4,128)S(1)} fusion(f32[128,4,512]{2,1,0:T(4,128)S(1)} %copy-done, f32[128,4,512]{2,1,0:T(4,128)S(1)} %multiply_add_fusion.2, f32[128,1,512]{2,1,0:T(1,128)S(1)} %collective-permute-done.17, f32[128,1,512]{2,1,0:T(1,128)S(1)} %collective-permute-done.16, f32[128]{0:T(128)S(1)} %copy-done.2), kind=kLoop, calls=%fused_computation.31 | loop fusion | flops 1835008 | bytes 3670528 | tf_op jit(solution)/shard_map/add | solution.py:55
  129.4 1.8 %fusion.52 = f32[2048,128]{1,0:T(8,128)S(1)} fusion(f32[128,2048]{1,0:T(8,128)S(1)} %bitcast.97, f32[128,128]{1,0:T(8,128)S(1)} %copy-done.1), kind=kOutput, calls=%fused_computation.101 | convolution fusion | flops 402653184 | bytes 2162688 | tf_op jit(solution)/shard_map/dot_general | solution.py:31
  135.6 1.9 %collective-permute-start.20 = (f32[128,1,512]{2,1,0:T(1,128)S(1)}, f32[128,1,512]{2,1,0:T(1,128)S(1)}, u32[]{:S(2)}, u32[]{:S(2)}) collective-permute-start(f32[128,1,512]{2,1,0:T(1,128)S(1)} %get-tuple-element.77), channel_id=1, source_target_pairs={{1,0},{2,1},{3,2},{4,3},{5,4},{6,5},{7,6},{8,7},{9,8},{10,9},{11,1... | collective-permute-start | bytes 786440 | tf_op jit(solution)/shard_map/ppermute | solution.py:23
  137.5 3.4 %collective-permute-start.21 = (f32[128,1,512]{2,1,0:T(1,128)S(1)}, f32[128,1,512]{2,1,0:T(1,128)S(1)}, u32[]{:S(2)}, u32[]{:S(2)}) collective-permute-start(f32[128,1,512]{2,1,0:T(1,128)S(1)} %get-tuple-element.78), channel_id=1, source_target_pairs={{0,1},{1,2},{2,3},{3,4},{4,5},{5,6},{6,7},{7,8},{8,9},{9,10},{10,1... | collective-permute-start | bytes 786440 | tf_op jit(solution)/shard_map/ppermute | solution.py:20
  140.9 2.6 %collective-permute-start.22 = (f32[4,512]{1,0:T(4,128)S(1)}, f32[4,512]{1,0:T(4,128)S(1)}, u32[]{:S(2)}, u32[]{:S(2)}) collective-permute-start(f32[4,512]{1,0:T(4,128)S(1)} %slice_bitcast_fusion), channel_id=1, source_target_pairs={{256,0},{257,1},{258,2},{259,3},{260,4},{261,5},{262,6},{263,7},{2... | collective-permute-start | bytes 24584 | tf_op jit(solution)/shard_map/ppermute | solution.py:12
  143.5 1.6 %collective-permute-done.20 = f32[128,1,512]{2,1,0:T(1,128)S(1)} collective-permute-done((f32[128,1,512]{2,1,0:T(1,128)S(1)}, f32[128,1,512]{2,1,0:T(1,128)S(1)}, u32[]{:S(2)}, u32[]{:S(2)}) %collective-permute-start.20) | collective-permute-done | bytes 262176 | tf_op jit(solution)/shard_map/ppermute | solution.py:23
  145.2 7.4 %collective-permute-done.21 = f32[128,1,512]{2,1,0:T(1,128)S(1)} collective-permute-done((f32[128,1,512]{2,1,0:T(1,128)S(1)}, f32[128,1,512]{2,1,0:T(1,128)S(1)}, u32[]{:S(2)}, u32[]{:S(2)}) %collective-permute-start.21) | collective-permute-done | bytes 262176 | tf_op jit(solution)/shard_map/ppermute | solution.py:20
  152.5 1.7 %fusion.23 = f32[128,4,512]{2,1,0:T(4,128)S(1)} fusion(f32[128,4,512]{2,1,0:T(4,128)S(1)} %copy-done, f32[128,4,512]{2,1,0:T(4,128)S(1)} %multiply_add_fusion.1, f32[128,1,512]{2,1,0:T(1,128)S(1)} %collective-permute-done.21, f32[128,1,512]{2,1,0:T(1,128)S(1)} %collective-permute-done.20, f32[128]{0:T(128)S(1)} %copy-done.2), kind=kLoop, calls=%fused_computation.35 | loop fusion | flops 1835008 | bytes 3670528 | tf_op jit(solution)/shard_map/add | solution.py:55
  154.6 1.8 %fusion.53 = f32[2048,128]{1,0:T(8,128)S(1)} fusion(f32[128,2048]{1,0:T(8,128)S(1)} %bitcast.98, f32[128,128]{1,0:T(8,128)S(1)} %copy-done.1), kind=kOutput, calls=%fused_computation.102 | convolution fusion | flops 402653184 | bytes 2162688 | tf_op jit(solution)/shard_map/dot_general | solution.py:31
  (68 shorter events, 23.7 us)
Async XLA Ops:
  0.0 22.7 %copy-start = (f32[128,4,512]{2,1,0:T(4,128)S(1)}, f32[128,4,512]{2,1,0:T(4,128)}, u32[]{:S(2)}) copy-start(f32[128,4,512]{2,1,0:T(4,128)} %param.18) | copy-start | bytes 3145732
  0.0 22.7 %copy-start.2 = (f32[128]{0:T(128)S(1)}, f32[128]{0:T(128)}, u32[]{:S(2)}) copy-start(f32[128]{0:T(128)} %param.19) | copy-start | bytes 1540
  2.1 14.4 %collective-permute-start = (f32[128,1,512]{2,1,0:T(1,128)S(1)}, f32[128,1,512]{2,1,0:T(1,128)S(1)}, u32[]{:S(2)}, u32[]{:S(2)}) collective-permute-start(f32[128,1,512]{2,1,0:T(1,128)S(1)} %get-tuple-element.87), channel_id=1, source_target_pairs={{1,0},{2,1},{3,2},{4,3},{5,4},{6,5},{7,6},{8,7},{9,8},{10,9},{11,1... | collective-permute-start | bytes 786440 | tf_op jit(solution)/shard_map/ppermute | solution.py:23
  8.5 14.2 %collective-permute-start.1 = (f32[128,1,512]{2,1,0:T(1,128)S(1)}, f32[128,1,512]{2,1,0:T(1,128)S(1)}, u32[]{:S(2)}, u32[]{:S(2)}) collective-permute-start(f32[128,1,512]{2,1,0:T(1,128)S(1)} %get-tuple-element.88), channel_id=1, source_target_pairs={{0,1},{1,2},{2,3},{3,4},{4,5},{5,6},{6,7},{7,8},{8,9},{9,10},{10,1... | collective-permute-start | bytes 786440 | tf_op jit(solution)/shard_map/ppermute | solution.py:20
  11.1 15.6 %collective-permute-start.2 = (f32[4,512]{1,0:T(4,128)S(1)}, f32[4,512]{1,0:T(4,128)S(1)}, u32[]{:S(2)}, u32[]{:S(2)}) collective-permute-start(f32[4,512]{1,0:T(4,128)S(1)} %slice_bitcast_fusion.5), channel_id=1, source_target_pairs={{256,0},{257,1},{258,2},{259,3},{260,4},{261,5},{262,6},{263,7},{2... | collective-permute-start | bytes 24584 | tf_op jit(solution)/shard_map/ppermute | solution.py:12
  26.7 0.8 copy-start.1
  30.0 3.8 %collective-permute-start.3 = (f32[4,512]{1,0:T(4,128)S(1)}, f32[4,512]{1,0:T(4,128)S(1)}, u32[]{:S(2)}, u32[]{:S(2)}) collective-permute-start(f32[4,512]{1,0:T(4,128)S(1)} %add.189), channel_id=1, source_target_pairs={{0,256},{1,257},{2,258},{3,259},{4,260},{5,261},{6,262},{7,263},{8... | collective-permute-start | bytes 24584 | tf_op jit(solution)/shard_map/ppermute | solution.py:12
  34.4 9.6 %collective-permute-start.4 = (f32[128,1,512]{2,1,0:T(1,128)S(1)}, f32[128,1,512]{2,1,0:T(1,128)S(1)}, u32[]{:S(2)}, u32[]{:S(2)}) collective-permute-start(f32[128,1,512]{2,1,0:T(1,128)S(1)} %get-tuple-element.85), channel_id=1, source_target_pairs={{1,0},{2,1},{3,2},{4,3},{5,4},{6,5},{7,6},{8,7},{9,8},{10,9},{11,1... | collective-permute-start | bytes 786440 | tf_op jit(solution)/shard_map/ppermute | solution.py:23
  36.6 14.7 %collective-permute-start.5 = (f32[128,1,512]{2,1,0:T(1,128)S(1)}, f32[128,1,512]{2,1,0:T(1,128)S(1)}, u32[]{:S(2)}, u32[]{:S(2)}) collective-permute-start(f32[128,1,512]{2,1,0:T(1,128)S(1)} %get-tuple-element.86), channel_id=1, source_target_pairs={{0,1},{1,2},{2,3},{3,4},{4,5},{5,6},{6,7},{7,8},{8,9},{9,10},{10,1... | collective-permute-start | bytes 786440 | tf_op jit(solution)/shard_map/ppermute | solution.py:20
  39.7 13.4 %collective-permute-start.6 = (f32[4,512]{1,0:T(4,128)S(1)}, f32[4,512]{1,0:T(4,128)S(1)}, u32[]{:S(2)}, u32[]{:S(2)}) collective-permute-start(f32[4,512]{1,0:T(4,128)S(1)} %slice_bitcast_fusion.4), channel_id=1, source_target_pairs={{256,0},{257,1},{258,2},{259,3},{260,4},{261,5},{262,6},{263,7},{2... | collective-permute-start | bytes 24584 | tf_op jit(solution)/shard_map/ppermute | solution.py:12
  55.9 3.2 %collective-permute-start.7 = (f32[4,512]{1,0:T(4,128)S(1)}, f32[4,512]{1,0:T(4,128)S(1)}, u32[]{:S(2)}, u32[]{:S(2)}) collective-permute-start(f32[4,512]{1,0:T(4,128)S(1)} %add.197), channel_id=1, source_target_pairs={{0,256},{1,257},{2,258},{3,259},{4,260},{5,261},{6,262},{7,263},{8... | collective-permute-start | bytes 24584 | tf_op jit(solution)/shard_map/ppermute | solution.py:12
  59.8 9.6 %collective-permute-start.8 = (f32[128,1,512]{2,1,0:T(1,128)S(1)}, f32[128,1,512]{2,1,0:T(1,128)S(1)}, u32[]{:S(2)}, u32[]{:S(2)}) collective-permute-start(f32[128,1,512]{2,1,0:T(1,128)S(1)} %get-tuple-element.83), channel_id=1, source_target_pairs={{1,0},{2,1},{3,2},{4,3},{5,4},{6,5},{7,6},{8,7},{9,8},{10,9},{11,1... | collective-permute-start | bytes 786440 | tf_op jit(solution)/shard_map/ppermute | solution.py:23
  61.8 15.0 %collective-permute-start.9 = (f32[128,1,512]{2,1,0:T(1,128)S(1)}, f32[128,1,512]{2,1,0:T(1,128)S(1)}, u32[]{:S(2)}, u32[]{:S(2)}) collective-permute-start(f32[128,1,512]{2,1,0:T(1,128)S(1)} %get-tuple-element.84), channel_id=1, source_target_pairs={{0,1},{1,2},{2,3},{3,4},{4,5},{5,6},{6,7},{7,8},{8,9},{9,10},{10,1... | collective-permute-start | bytes 786440 | tf_op jit(solution)/shard_map/ppermute | solution.py:20
  65.2 13.4 %collective-permute-start.10 = (f32[4,512]{1,0:T(4,128)S(1)}, f32[4,512]{1,0:T(4,128)S(1)}, u32[]{:S(2)}, u32[]{:S(2)}) collective-permute-start(f32[4,512]{1,0:T(4,128)S(1)} %slice_bitcast_fusion.3), channel_id=1, source_target_pairs={{256,0},{257,1},{258,2},{259,3},{260,4},{261,5},{262,6},{263,7},{2... | collective-permute-start | bytes 24584 | tf_op jit(solution)/shard_map/ppermute | solution.py:12
  81.4 3.1 %collective-permute-start.11 = (f32[4,512]{1,0:T(4,128)S(1)}, f32[4,512]{1,0:T(4,128)S(1)}, u32[]{:S(2)}, u32[]{:S(2)}) collective-permute-start(f32[4,512]{1,0:T(4,128)S(1)} %add.205), channel_id=1, source_target_pairs={{0,256},{1,257},{2,258},{3,259},{4,260},{5,261},{6,262},{7,263},{8... | collective-permute-start | bytes 24584 | tf_op jit(solution)/shard_map/ppermute | solution.py:12
  85.1 9.6 %collective-permute-start.12 = (f32[128,1,512]{2,1,0:T(1,128)S(1)}, f32[128,1,512]{2,1,0:T(1,128)S(1)}, u32[]{:S(2)}, u32[]{:S(2)}) collective-permute-start(f32[128,1,512]{2,1,0:T(1,128)S(1)} %get-tuple-element.81), channel_id=1, source_target_pairs={{1,0},{2,1},{3,2},{4,3},{5,4},{6,5},{7,6},{8,7},{9,8},{10,9},{11,1... | collective-permute-start | bytes 786440 | tf_op jit(solution)/shard_map/ppermute | solution.py:23
  87.0 15.0 %collective-permute-start.13 = (f32[128,1,512]{2,1,0:T(1,128)S(1)}, f32[128,1,512]{2,1,0:T(1,128)S(1)}, u32[]{:S(2)}, u32[]{:S(2)}) collective-permute-start(f32[128,1,512]{2,1,0:T(1,128)S(1)} %get-tuple-element.82), channel_id=1, source_target_pairs={{0,1},{1,2},{2,3},{3,4},{4,5},{5,6},{6,7},{7,8},{8,9},{9,10},{10,1... | collective-permute-start | bytes 786440 | tf_op jit(solution)/shard_map/ppermute | solution.py:20
  90.4 13.4 %collective-permute-start.14 = (f32[4,512]{1,0:T(4,128)S(1)}, f32[4,512]{1,0:T(4,128)S(1)}, u32[]{:S(2)}, u32[]{:S(2)}) collective-permute-start(f32[4,512]{1,0:T(4,128)S(1)} %slice_bitcast_fusion.2), channel_id=1, source_target_pairs={{256,0},{257,1},{258,2},{259,3},{260,4},{261,5},{262,6},{263,7},{2... | collective-permute-start | bytes 24584 | tf_op jit(solution)/shard_map/ppermute | solution.py:12
  106.6 3.1 %collective-permute-start.15 = (f32[4,512]{1,0:T(4,128)S(1)}, f32[4,512]{1,0:T(4,128)S(1)}, u32[]{:S(2)}, u32[]{:S(2)}) collective-permute-start(f32[4,512]{1,0:T(4,128)S(1)} %add.213), channel_id=1, source_target_pairs={{0,256},{1,257},{2,258},{3,259},{4,260},{5,261},{6,262},{7,263},{8... | collective-permute-start | bytes 24584 | tf_op jit(solution)/shard_map/ppermute | solution.py:12
  110.3 9.6 %collective-permute-start.16 = (f32[128,1,512]{2,1,0:T(1,128)S(1)}, f32[128,1,512]{2,1,0:T(1,128)S(1)}, u32[]{:S(2)}, u32[]{:S(2)}) collective-permute-start(f32[128,1,512]{2,1,0:T(1,128)S(1)} %get-tuple-element.79), channel_id=1, source_target_pairs={{1,0},{2,1},{3,2},{4,3},{5,4},{6,5},{7,6},{8,7},{9,8},{10,9},{11,1... | collective-permute-start | bytes 786440 | tf_op jit(solution)/shard_map/ppermute | solution.py:23
  112.3 15.0 %collective-permute-start.17 = (f32[128,1,512]{2,1,0:T(1,128)S(1)}, f32[128,1,512]{2,1,0:T(1,128)S(1)}, u32[]{:S(2)}, u32[]{:S(2)}) collective-permute-start(f32[128,1,512]{2,1,0:T(1,128)S(1)} %get-tuple-element.80), channel_id=1, source_target_pairs={{0,1},{1,2},{2,3},{3,4},{4,5},{5,6},{6,7},{7,8},{8,9},{9,10},{10,1... | collective-permute-start | bytes 786440 | tf_op jit(solution)/shard_map/ppermute | solution.py:20
  115.7 13.4 %collective-permute-start.18 = (f32[4,512]{1,0:T(4,128)S(1)}, f32[4,512]{1,0:T(4,128)S(1)}, u32[]{:S(2)}, u32[]{:S(2)}) collective-permute-start(f32[4,512]{1,0:T(4,128)S(1)} %slice_bitcast_fusion.1), channel_id=1, source_target_pairs={{256,0},{257,1},{258,2},{259,3},{260,4},{261,5},{262,6},{263,7},{2... | collective-permute-start | bytes 24584 | tf_op jit(solution)/shard_map/ppermute | solution.py:12
  131.9 3.1 %collective-permute-start.19 = (f32[4,512]{1,0:T(4,128)S(1)}, f32[4,512]{1,0:T(4,128)S(1)}, u32[]{:S(2)}, u32[]{:S(2)}) collective-permute-start(f32[4,512]{1,0:T(4,128)S(1)} %add.221), channel_id=1, source_target_pairs={{0,256},{1,257},{2,258},{3,259},{4,260},{5,261},{6,262},{7,263},{8... | collective-permute-start | bytes 24584 | tf_op jit(solution)/shard_map/ppermute | solution.py:12
  135.6 9.6 %collective-permute-start.20 = (f32[128,1,512]{2,1,0:T(1,128)S(1)}, f32[128,1,512]{2,1,0:T(1,128)S(1)}, u32[]{:S(2)}, u32[]{:S(2)}) collective-permute-start(f32[128,1,512]{2,1,0:T(1,128)S(1)} %get-tuple-element.77), channel_id=1, source_target_pairs={{1,0},{2,1},{3,2},{4,3},{5,4},{6,5},{7,6},{8,7},{9,8},{10,9},{11,1... | collective-permute-start | bytes 786440 | tf_op jit(solution)/shard_map/ppermute | solution.py:23
  137.5 15.0 %collective-permute-start.21 = (f32[128,1,512]{2,1,0:T(1,128)S(1)}, f32[128,1,512]{2,1,0:T(1,128)S(1)}, u32[]{:S(2)}, u32[]{:S(2)}) collective-permute-start(f32[128,1,512]{2,1,0:T(1,128)S(1)} %get-tuple-element.78), channel_id=1, source_target_pairs={{0,1},{1,2},{2,3},{3,4},{4,5},{5,6},{6,7},{7,8},{8,9},{9,10},{10,1... | collective-permute-start | bytes 786440 | tf_op jit(solution)/shard_map/ppermute | solution.py:20
  140.9 13.4 %collective-permute-start.22 = (f32[4,512]{1,0:T(4,128)S(1)}, f32[4,512]{1,0:T(4,128)S(1)}, u32[]{:S(2)}, u32[]{:S(2)}) collective-permute-start(f32[4,512]{1,0:T(4,128)S(1)} %slice_bitcast_fusion), channel_id=1, source_target_pairs={{256,0},{257,1},{258,2},{259,3},{260,4},{261,5},{262,6},{263,7},{2... | collective-permute-start | bytes 24584 | tf_op jit(solution)/shard_map/ppermute | solution.py:12
  157.1 3.1 %collective-permute-start.23 = (f32[4,512]{1,0:T(4,128)S(1)}, f32[4,512]{1,0:T(4,128)S(1)}, u32[]{:S(2)}, u32[]{:S(2)}) collective-permute-start(f32[4,512]{1,0:T(4,128)S(1)} %add.229), channel_id=1, source_target_pairs={{0,256},{1,257},{2,258},{3,259},{4,260},{5,261},{6,262},{7,263},{8... | collective-permute-start | bytes 24584 | tf_op jit(solution)/shard_map/ppermute | solution.py:12
where the time goes:
time: 162 us; the launch traced here: 161 us
  waiting for transfers between devices  59.2 us (37%)
  starting transfers between devices  58.9 us (36%)
  other arithmetic  19 us (12%)
  local copies, waits for them, and re-layouts  11.6 us (7%)
  matrix products  10.8 us (7%)
  between operations  1.93 us (1%)
    ppermute x6, waiting for transfers between devices, extended(): lax.ppermute(lax.slice_in_dim(block, block.shape[dim] - width, None, axis...  43 us
    ppermute x12, starting transfers between devices, shifted(): lax.ppermute(value, axis, [(source, source + steps) for source in range(f...  24.2 us
    ppermute x6, starting transfers between devices, extended(): lax.ppermute(lax.slice_in_dim(block, block.shape[dim] - width, None, axis...  18.5 us
    ppermute x6, starting transfers between devices, extended(): lax.ppermute(lax.slice_in_dim(block, 0, width, axis=dim), axis, backward)  16.3 us
    add x6, other arithmetic, local(): right_side = source + weights * (across_rows + across_columns(field))  12.5 us
    dot_general x6, matrix products, apply_inverse(): jnp.dot(inverse, flat, precision=lax.Precision.HIGHEST, preferred_element...  10.8 us
    ppermute x12, waiting for transfers between devices, shifted(): lax.ppermute(value, axis, [(source, source + steps) for source in range(f...  8.37 us
    ppermute x6, waiting for transfers between devices, extended(): lax.ppermute(lax.slice_in_dim(block, 0, width, axis=dim), axis, backward)  7.81 us
  transfers between devices with their start and end apart: 24, of which 17 were waited for; matrix products, arithmetic and copies ran while one was open for 11% of the time, Pallas kernels for 0%

commit v1 on v0

v1 whole, which is shorter than its diff:
```python
import functools
import jax
import jax.numpy as jnp
from jax import lax
from jax.experimental import pallas as pl
from jax.experimental.pallas import tpu as pltpu
from jax.sharding import PartitionSpec as P


SWEEPS = 6
LANES = 128
OVERLAP = 16
PAD = 8
GROUP = 4
VMEM = pl.BlockSpec(memory_space=pltpu.VMEM)
SMEM = pl.BlockSpec(memory_space=pltpu.SMEM)


def pack_body(send, core_ref, temp_ref, source_ref, inverse_ref, couple_ref, out_ref):
    rows, half = temp_ref.shape[0], temp_ref.shape[2] // 2
    width = half + OVERLAP
    tiles = half // LANES
    low = [(t, 0, LANES, t * LANES) for t in range(tiles)] + [(tiles, 0, OVERLAP, half)]
    high = [(tiles - 1, LANES - OVERLAP, OVERLAP, 0)] + [
        (tiles + t, 0, LANES, OVERLAP + t * LANES) for t in range(tiles)
    ]
    for slab in range(2):
        turned = (lambda value: pltpu.roll(value, LANES - 1, 1)) if slab == 1 else (lambda value: value)

        @pl.when(core_ref[0] == slab)
        def _():
            for array, ref in enumerate((temp_ref, source_ref)):
                for row in range(rows):
                    base = (array * rows + row) * width
                    for tile, first, count, place in high if (slab == 1) != send else low:
                        block = turned(ref[row, :, tile * LANES : (tile + 1) * LANES].T)
                        out_ref[base + place : base + place + count, :] = block[first : first + count]
            base = 2 * rows * width
            inverse = turned(inverse_ref[...].T)
            if slab == 1:
                inverse = pltpu.roll(inverse, LANES - 1, 0)
            out_ref[base : base + LANES, :] = inverse
            out_ref[base + LANES : base + LANES + 8, :] = turned(jnp.broadcast_to(couple_ref[...], (8, LANES)))


def pack(send, core, temp, source, inverse, couple):
    rows, _, columns = temp.shape
    length = 2 * rows * (columns // 2 + OVERLAP) + LANES + 8
    return pl.pallas_call(
        functools.partial(pack_body, send),
        out_shape=jax.ShapeDtypeStruct((length, LANES), jnp.float32),
        in_specs=[SMEM, VMEM, VMEM, VMEM, VMEM],
        out_specs=VMEM,
        compiler_params=pltpu.CompilerParams(vmem_limit_bytes=8 * 2**20),
        name="pack_send" if send else "pack_own",
    )(core, temp, source, inverse, couple)


def split(value):
    high = value.astype(jnp.bfloat16)
    return high, (value - high.astype(jnp.float32)).astype(jnp.bfloat16)


class Solver:
    def __init__(self, rows, width, place_ref, face_ref, mine_ref, other_ref, weights):
        self.rows, self.width, self.weights = rows, width, weights
        self.core, self.lat, self.lat_count = place_ref[0], place_ref[1], place_ref[2]
        self.odd = lax.rem(self.lat, 2)
        self.payloads = ((self.core, mine_ref), (1 - self.core, other_ref))
        face = face_ref[0]
        base = 2 * rows * width
        first = self.core == 0

        def pick(start, count, slab):
            return jnp.where(first == (slab == 0), mine_ref[start : start + count], other_ref[start : start + count])

        self.couples = [pick(base + LANES, 8, slab)[0:1] for slab in range(2)]
        for slab in range(2):
            high, low = split(pick(base, LANES, slab))
            weights[slab, :LANES, :LANES] = high
            weights[slab, LANES:, :LANES] = high
            weights[slab, :LANES, LANES:] = low
            weights[slab, LANES:, LANES:] = jnp.zeros((LANES, LANES), jnp.bfloat16)
        lane = lax.broadcasted_iota(jnp.int32, (1, LANES), 1)
        self.face_last = jnp.where(lane == LANES - 1, face, 0.0)

    def inside(self, row):
        grid_row = self.lat * self.rows - SWEEPS + row
        return ((grid_row >= 0) & (grid_row < self.lat_count * self.rows)).astype(jnp.float32)

    def apply(self, slab, sides):
        high, low = split(jnp.concatenate(sides, axis=0))
        both = jnp.dot(
            jnp.concatenate([high, low], axis=1), self.weights[slab], preferred_element_type=jnp.float32
        )
        solved = both[:, :LANES] + both[:, LANES:]
        return [solved[k * self.width : (k + 1) * self.width] for k in range(len(sides))]

    def advance(self, rows, sums, unders, extras, store):
        gains = [[couple * self.inside(row) for couple in self.couples] for row in rows]

        def side(k, slab):
            value = sums(k, slab) * gains[k][slab]
            extra = extras(k, slab)
            return value if extra is None else value + extra

        upper = []
        for k in range(len(rows)):
            value, under = side(k, 0), unders(k)
            upper.append(value if under is None else value + under * self.face_last)
        upper = self.apply(0, upper)
        for k, value in enumerate(upper):
            store(k, 0, value)
        lower = self.apply(
            1, [side(k, 1) + upper[k] * self.face_last for k in range(len(rows))]
        )
        for k, value in enumerate(lower):
            store(k, 1, value)


def clear_pads(ref, lead, width):
    zero = jnp.zeros((PAD, LANES), jnp.float32)
    for index in lead:
        ref[(*index, slice(0, PAD))] = zero
        ref[(*index, slice(PAD + width, 2 * PAD + width))] = zero


def strips_body(rows, width, place_ref, face_ref, mine_ref, other_ref, far_first, far_second, strips, weights, last):
    solver = Solver(rows, width, place_ref, face_ref, mine_ref, other_ref, weights)
    middle = slice(PAD, PAD + width)
    clear_pads(strips, [(j, a, s) for j in range(SWEEPS) for a in range(4) for s in range(2)], width)
    for slab, ref in solver.payloads:
        for row in range(rows):
            strips[0, row, slab, middle] = ref[row * width : (row + 1) * width]
    source = lambda row, slab: jnp.where(
        (solver.core == 0) == (slab == 0),
        mine_ref[(rows + row) * width : (rows + row + 1) * width],
        other_ref[(rows + row) * width : (rows + row + 1) * width],
    )
    top = rows - 1
    for reach in range(1, SWEEPS + 1):
        old = functools.partial(lambda at, a, s, cut: strips[at, a, s, cut], reach - 1)

        def sums(k, slab):
            if k in (0, 3):
                return old(0 if k == 0 else top, slab, middle)
            inner, edge = (1, 0) if k == 1 else (top - 1, top)
            return (
                old(inner, slab, middle)
                + old(edge, slab, slice(PAD - 1, PAD - 1 + width))
                + old(edge, slab, slice(PAD + 1, PAD + 1 + width))
            )

        def unders(k):
            return None if k in (0, 3) else old(0 if k == 1 else top, 1, middle)

        def extras(k, slab):
            return source(0 if k == 1 else top, slab) if reach == 1 and k in (1, 2) else None

        def store(k, slab, value):
            if reach < SWEEPS:
                strips[reach, k, slab, middle] = value
            else:
                last[k, slab] = value

        solver.advance(
            [SWEEPS - reach, SWEEPS + 1 - reach, SWEEPS + top - 1 + reach, SWEEPS + top + reach],
            sums, unders, extras, store,
        )
    start = pl.multiple_of(OVERLAP * solver.core, 8)
    half = width - OVERLAP
    odd = solver.odd
    for ref, row in ((far_first, 2 - 2 * odd), (far_second, 2 * odd)):
        for k in range(2):
            for slab in range(2):
                ref[k, slab] = last[row + k, slab, pl.ds(start, half)]


def core_body(rows, width, place_ref, face_ref, mine_ref, other_ref, strips,
              mid_first, mid_second, near_first, near_second, own, field, rhs_source, weights):
    solver = Solver(rows, width, place_ref, face_ref, mine_ref, other_ref, weights)
    middle = slice(PAD, PAD + width)
    half = width - OVERLAP
    clear_pads(field, [(b, s, r) for b in range(2) for s in range(2) for r in range(2, field.shape[2] - 2)], width)
    for slab, ref in solver.payloads:
        for row in range(rows):
            rhs_source[slab, row] = ref[(rows + row) * width : (rows + row + 1) * width]

    def sweep(reach):
        def old(row, slab, cut):
            low, high = SWEEPS + 1 - reach, SWEEPS + rows - 3 + reach
            if row - low in (0, 1):
                return strips[reach - 1, row - low, slab, cut]
            if row - high in (0, 1):
                return strips[reach - 1, 2 + row - high, slab, cut]
            return field[(reach + 1) % 2, slab, row, cut]

        def group(at):
            def sums(k, slab):
                row = at[k]
                return (old(row - 1, slab, middle) + old(row + 1, slab, middle)) + (
                    old(row, slab, slice(PAD - 1, PAD - 1 + width)) + old(row, slab, slice(PAD + 1, PAD + 1 + width))
                )

            def store(k, slab, value):
                field[reach % 2, slab, at[k], middle] = value

            def extras(k, slab):
                return rhs_source[slab, at[k] - SWEEPS] if 0 <= at[k] - SWEEPS < rows else None

            solver.advance(at, sums, lambda k: old(at[k], 1, middle), extras, store)

        todo = list(range(SWEEPS + 2 - reach, SWEEPS + rows - 2 + reach))
        for first in range(0, len(todo), GROUP):
            group(todo[first : first + GROUP])

    for reach in range(1, SWEEPS + 1):
        sweep(reach)
    start = pl.multiple_of(PAD + OVERLAP * solver.core, 8)
    odd, reach = solver.odd, rows + SWEEPS
    for ref, row in (
        (own, SWEEPS),
        (near_first, reach + (4 - reach) * odd),
        (near_second, 4 + (reach - 4) * odd),
        (mid_first, reach + 2 - reach * odd),
        (mid_second, 2 + reach * odd),
    ):
        for k in range(ref.shape[0]):
            for slab in range(2):
                ref[k, slab] = field[SWEEPS % 2, slab, row + k, pl.ds(start, half)]


def sweeps(place, face, mine, other, rows, half):
    width = half + OVERLAP
    shape = lambda count: jax.ShapeDtypeStruct((count, 2, half, LANES), jnp.float32)
    weights = pltpu.VMEM((2, 2 * LANES, 2 * LANES), jnp.bfloat16)
    far_first, far_second, strips = pl.pallas_call(
        functools.partial(strips_body, rows, width),
        out_shape=[
            shape(2),
            shape(2),
            jax.ShapeDtypeStruct((SWEEPS, 4, 2, width + 2 * PAD, LANES), jnp.float32),
        ],
        in_specs=[SMEM, SMEM, VMEM, VMEM],
        out_specs=[VMEM] * 3,
        scratch_shapes=[weights, pltpu.VMEM((4, 2, width, LANES), jnp.float32)],
        compiler_params=pltpu.CompilerParams(vmem_limit_bytes=24 * 2**20),
        name="strips",
    )(place, face, mine, other)
    mid_first, mid_second, near_first, near_second, own = pl.pallas_call(
        functools.partial(core_body, rows, width),
        out_shape=[shape(k) for k in (2, 2, 2, 2, rows)],
        in_specs=[SMEM, SMEM, VMEM, VMEM, VMEM],
        out_specs=[VMEM] * 5,
        scratch_shapes=[
            pltpu.VMEM((2, 2, rows + 2 * SWEEPS, width + 2 * PAD, LANES), jnp.float32),
            pltpu.VMEM((2, rows, width, LANES), jnp.float32),
            weights,
        ],
        compiler_params=pltpu.CompilerParams(vmem_limit_bytes=32 * 2**20),
        name="core",
    )(place, face, mine, other, strips)
    return far_first, far_second, mid_first, mid_second, near_first, near_second, own


def join_body(place_ref, near, far, same, cross):
    core = place_ref[0]
    for k in range(near.shape[0]):
        same[k] = near[k, core] + far[k, core]
        cross[k] = near[k, 1 - core] + far[k, 1 - core]


def hand_body(place_ref, own, mid_first, mid_second, kept, handed):
    core, odd = place_ref[0], lax.rem(place_ref[1], 2)
    for piece, pair in ((mid_first, odd), (mid_second, 1 - odd)):
        for k in range(2):
            row = 2 * pair + k
            kept[row] = own[row, core] + piece[k, core]
            handed[row] = own[row, 1 - core] + piece[k, 1 - core]


def finish_body(place_ref, kept, handed, same_first, cross_first, same_second, cross_second, out_ref):
    odd = lax.rem(place_ref[1], 2)
    half = kept.shape[1]
    for core in range(2):

        @pl.when(place_ref[0] == core)
        def _():
            for same, cross, pair in ((same_second, cross_second, odd), (same_first, cross_first, 1 - odd)):
                for k in range(2):
                    row = 2 * pair + k
                    for side, base, piece in ((core, kept, same), (1 - core, handed, cross)):
                        for tile in range(half // LANES):
                            cut = slice(tile * LANES, (tile + 1) * LANES)
                            value = base[row, cut] + piece[k, cut]
                            if core == 1:
                                value = pltpu.roll(value, 1, 1)
                            at = side * half + tile * LANES
                            out_ref[row, :, at : at + LANES] = value.T


def program(temp_old, source, lat_couple, face_couple, block_inverse):
    _, rows, columns = temp_old.shape
    half = columns // 2
    core, lat = lax.axis_index("depth"), lax.axis_index("lat")
    lat_count = lax.axis_size("lat")
    place = jnp.stack([core, lat, jnp.int32(lat_count)]).astype(jnp.int32)
    params = pltpu.CompilerParams(vmem_limit_bytes=16 * 2**20)
    piece = lambda *shape: jax.ShapeDtypeStruct((*shape, half, LANES), jnp.float32)

    def call(body, outs, *arrays):
        return pl.pallas_call(
            body, out_shape=outs, in_specs=[SMEM] + [VMEM] * len(arrays), out_specs=[VMEM] * len(outs),
            compiler_params=params,
        )(place, *arrays)

    pairs = [
        [(i, i + 1) for i in range(start, lat_count - 1, 2)] + [(i + 1, i) for i in range(start, lat_count - 1, 2)]
        for start in (0, 1)
    ]
    crossed = [
        [(d * lat_count + a, (1 - d) * lat_count + b) for d in range(2) for a, b in group] for group in pairs
    ]

    swap = lambda value: lax.ppermute(value, "depth", [(0, 1), (1, 0)])
    exchange = lambda value, group: lax.ppermute(value, "lat", pairs[group])
    cross = lambda value, group: lax.ppermute(value, ("depth", "lat"), crossed[group])

    temp, src = temp_old.transpose(1, 0, 2), source.transpose(1, 0, 2)
    couple = lat_couple.reshape(1, LANES)
    other = swap(pack(True, place, temp, src, block_inverse, couple))
    mine = pack(False, place, temp, src, block_inverse, couple)
    far_first, far_second, mid_first, mid_second, near_first, near_second, own = sweeps(
        place, face_couple, mine, other, rows, half
    )
    far_first, far_second = exchange(far_first, 0), exchange(far_second, 1)
    mid_first, mid_second = exchange(mid_first, 0), exchange(mid_second, 1)
    joined = [piece(2), piece(2)]
    same_second, cross_second = call(join_body, joined, near_second, far_first)
    same_second, cross_second = exchange(same_second, 1), cross(cross_second, 1)
    same_first, cross_first = call(join_body, joined, near_first, far_second)
    same_first, cross_first = exchange(same_first, 0), cross(cross_first, 0)
    kept, handed = call(hand_body, [piece(rows), piece(rows)], own, mid_first, mid_second)
    (result,) = call(
        finish_body, [jax.ShapeDtypeStruct((rows, LANES, columns), jnp.float32)],
        kept, swap(handed), same_first, cross_first, same_second, cross_second,
    )
    return result.transpose(1, 0, 2)


def solution(mesh):
    return jax.shard_map(
        program,
        mesh=mesh,
        in_specs=(
            P("depth", "lat", None),
            P("depth", "lat", None),
            P("depth"),
            P(),
            P("depth", None),
        ),
        out_specs=P("depth", "lat", None),
        check_vma=False,
    )
```

time: 162 us -> 83.4 us (0.51)
  waiting for transfers between devices: 59.2 us -> 24.5 us
  starting transfers between devices: 58.9 us -> 39.1 us
  other arithmetic: 19 us -> 0.08 us
  Pallas kernels: 0 us -> 14.7 us
  matrix products: 10.8 us -> 0 us
  local copies, waits for them, and re-layouts: 11.6 us -> 3.85 us
    ppermute x24 -> x10, waiting for transfers between devices: 59.2 us -> 24.5 us  [the longest x6 18.5 us: program(): exchange = lambda value, group: lax.ppermute(value, 'lat', pairs[group])]
    ppermute x24 -> x10, starting transfers between devices: 58.9 us -> 39.1 us  [the longest x6 23.4 us: program(): exchange = lambda value, group: lax.ppermute(value, 'lat', pairs[group])]
    add x18 -> x0, other arithmetic: 18.8 us -> none  [the longest x6 12.5 us: local(): right_side = source + weights * (across_rows + across_columns(field))]
    pallas_call x0 -> x8, Pallas kernels: none -> 14.7 us  [the longest x1 5.89 us: sweeps(): pl.pallas_call(functools.partial(core_body, rows, width), out_shape=[shap...]
    dot_general x6 -> x0, matrix products: 10.8 us -> none  [apply_inverse(): jnp.dot(inverse, flat, precision=lax.Precision.HIGHEST, preferred_element...]
    slice x7 -> x0, local copies, waits for them, and re-layouts: 5.34 us -> none  [the longest x6 4.11 us: extended(): lax.slice_in_dim(block, 0, width, axis=dim)]
    transpose x0 -> x2, local copies, waits for them, and re-layouts: none -> 3.84 us  [the longest x1 2.2 us: program(): temp, src = (temp_old.transpose(1, 0, 2), source.transpose(1, 0, 2))]
    reshape x6 -> x0, local copies, waits for them, and re-layouts: 2.95 us -> none  [apply_inverse(): return jnp.dot(inverse, flat, precision=lax.Precision.HIGHEST, preferred_...]
  transfers between devices with their start and end apart: 24 -> 10, of which waited for: 17 -> 5; matrix products, arithmetic and copies ran while one was open for 11% -> 0% of each run, Pallas kernels for 0% -> 4%
where the time goes in v1:
time: 83.4 us; the launch traced here: 83 us
  starting transfers between devices  39.1 us (47%)
  waiting for transfers between devices  24.5 us (29%)
  Pallas kernels  14.7 us (18%)
  local copies, waits for them, and re-layouts  3.85 us (5%)
    ppermute x6, starting transfers between devices, program(): exchange = lambda value, group: lax.ppermute(value, 'lat', pairs[group])  23.4 us
    ppermute x6, waiting for transfers between devices, program(): exchange = lambda value, group: lax.ppermute(value, 'lat', pairs[group])  18.5 us
    ppermute x2, starting transfers between devices, program(): lax.ppermute(value, ('depth', 'lat'), crossed[group])  8.91 us
    ppermute x2, starting transfers between devices, program(): swap = lambda value: lax.ppermute(value, 'depth', [(0, 1), (1, 0)])  6.75 us
    pallas_call x1, Pallas kernels, sweeps(): pl.pallas_call(functools.partial(core_body, rows, width), out_shape=[shap...  5.89 us
    ppermute x2, waiting for transfers between devices, program(): lax.ppermute(value, ('depth', 'lat'), crossed[group])  5.62 us
    pallas_call x4, Pallas kernels, call(): pl.pallas_call(body, out_shape=outs, in_specs=[SMEM] + [VMEM] * len(array...  3.08 us
    pallas_call x1, Pallas kernels, sweeps(): pl.pallas_call(functools.partial(strips_body, rows, width), out_shape=[sh...  2.96 us
  transfers between devices with their start and end apart: 10, of which 5 were waited for; matrix products, arithmetic and copies ran while one was open for 0% of the time, Pallas kernels for 4%

profile of v1, /device:TPU:257, one launch (start us, length us, event | category | flops | bytes accessed | tf_op | source)
XLA Modules:
  0.0 83.0 jit_solution(7942968795975257208)
XLA Ops:
  0.0 0.0 copy-start
  0.0 0.0 copy-start.1
  0.0 2.2 %copy_bitcast_fusion = (f32[4,128,512]{2,1,0:T(8,128)S(1)}, f32[4,128,512]{2,1,0:T(8,128)S(1)}) fusion(f32[128,4,512]{2,1,0:T(4,128)} %param.6, f32[128,4,512]{2,1,0:T(4,128)} %param.5), kind=kLoop, calls=%fused_computation | loop fusion | bytes 4194304 | tf_op jit(solution)/shard_map/transpose | solution.py:329
  2.2 0.1 pad_add_fusion.core_ref.place_ref
  2.3 0.0 copy-done
  2.3 0.0 copy-done.1
  2.3 1.4 %pack_send.1 = f32[2312,128]{1,0:T(8,128)S(1)} custom-call(s32[3]{0:T(128)S(1)} %pad_add_fusion.core_ref.place_ref, f32[4,128,512]{2,1,0:T(8,128)S(1)} %get-tuple-element.34.temp_ref, f32[4,128,512]{2,1,0:T(8,128)S(1)} %get-tuple-element.33.source_ref, f32[128,128]{1,0:T(8,128)S(1)} %copy-done, f32[1,128]{1,0:T(1,128)S(1)} %bitcast.9), custom_call_target="tpu_custom_call" | custom-call | tf_op jit(solution)/shard_map/pack_send/pallas_call | solution.py:49
  3.7 2.3 %collective-permute-start = (f32[2312,128]{1,0:T(8,128)S(1)}, f32[2312,128]{1,0:T(8,128)S(1)}, u32[]{:S(2)}, u32[]{:S(2)}) collective-permute-start(f32[2312,128]{1,0:T(8,128)S(1)} %pack_send.1), channel_id=1, source_target_pairs={{0,256},{256,0},{1,257},{257,1},{2,258},{258,2},{3,259},{259,3},{4... | collective-permute-start | bytes 3551240 | tf_op jit(solution)/shard_map/ppermute | solution.py:325
  5.9 1.4 %pack_own.1.mine_ref = f32[2312,128]{1,0:T(8,128)S(1)} custom-call(s32[3]{0:T(128)S(1)} %pad_add_fusion.core_ref.place_ref, f32[4,128,512]{2,1,0:T(8,128)S(1)} %get-tuple-element.34.temp_ref, f32[4,128,512]{2,1,0:T(8,128)S(1)} %get-tuple-element.33.source_ref, f32[128,128]{1,0:T(8,128)S(1)} %copy-done, f32[1,128]{1,0:T(1,128)S(1)} %bitcast.10), custom_call_target="tpu_custom_call" | custom-call | tf_op jit(solution)/shard_map/pack_own/pallas_call | solution.py:49
  8.0 0.5 collective-permute-done.other_ref
  8.4 3.0 %strips.1 = (f32[2,2,256,128]{3,2,1,0:T(8,128)S(1)}, f32[2,2,256,128]{3,2,1,0:T(8,128)S(1)}, f32[6,4,2,288,128]{4,3,2,1,0:T(8,128)S(1)}) custom-call(s32[3]{0:T(128)S(1)} %pad_add_fusion.core_ref.place_ref, f32[1]{0:T(128)S(6)} %copy.11.face_ref, f32[2312,128]{1,0:T(8,128)S(1)} %pack_own.1.mine_ref, f32[2312,128]{1,0:T(8,128)S(1)} %collective-permute-done.other_ref), custom_call_target="tpu_custom_call" | custom-call | tf_op jit(solution)/shard_map/strips/pallas_call | solution.py:237
  11.4 5.9 %core.1 = (f32[2,2,256,128]{3,2,1,0:T(8,128)S(1)}, f32[2,2,256,128]{3,2,1,0:T(8,128)S(1)}, f32[2,2,256,128]{3,2,1,0:T(8,128)S(1)}, f32[2,2,256,128]{3,2,1,0:T(8,128)S(1)}, f32[4,2,256,128]{3,2,1,0:T(8,128)S(1)}) custom-call(s32[3]{0:T(128)S(1)} %pad_add_fusion.core_ref.place_ref, f32[1]{0:T(128)S(6)} %copy.11.face_ref, f32[2312,128]{1,0:T(8,128)S(1)} %pack_own.1.mine_ref, ...), custom_call_target="tpu_custom_call" | custom-call | tf_op jit(solution)/shard_map/core/pallas_call | solution.py:250
  17.3 3.1 %collective-permute-start.1 = (f32[2,2,256,128]{3,2,1,0:T(8,128)S(1)}, f32[2,2,256,128]{3,2,1,0:T(8,128)S(1)}, u32[]{:S(2)}, u32[]{:S(2)}) collective-permute-start(f32[2,2,256,128]{3,2,1,0:T(8,128)S(1)} %get-tuple-element.21), channel_id=1, source_target_pairs={{0,1},{2,3},{4,5},{6,7},{8,9},{10,11},{12,13},{14,15},{16,17},{18,... | collective-permute-start | bytes 1572872 | tf_op jit(solution)/shard_map/ppermute | solution.py:326
  20.4 5.7 %collective-permute-start.2 = (f32[2,2,256,128]{3,2,1,0:T(8,128)S(1)}, f32[2,2,256,128]{3,2,1,0:T(8,128)S(1)}, u32[]{:S(2)}, u32[]{:S(2)}) collective-permute-start(f32[2,2,256,128]{3,2,1,0:T(8,128)S(1)} %get-tuple-element.22), channel_id=1, source_target_pairs={{1,2},{3,4},{5,6},{7,8},{9,10},{11,12},{13,14},{15,16},{17,18},{19... | collective-permute-start | bytes 1572872 | tf_op jit(solution)/shard_map/ppermute | solution.py:326
  26.1 5.0 %collective-permute-start.4 = (f32[2,2,256,128]{3,2,1,0:T(8,128)S(1)}, f32[2,2,256,128]{3,2,1,0:T(8,128)S(1)}, u32[]{:S(2)}, u32[]{:S(2)}) collective-permute-start(f32[2,2,256,128]{3,2,1,0:T(8,128)S(1)} %get-tuple-element.26), channel_id=1, source_target_pairs={{1,2},{3,4},{5,6},{7,8},{9,10},{11,12},{13,14},{15,16},{17,18},{19... | collective-permute-start | bytes 1572872 | tf_op jit(solution)/shard_map/ppermute | solution.py:326
  31.1 1.9 %collective-permute-start.7 = (f32[2,2,256,128]{3,2,1,0:T(8,128)S(1)}, f32[2,2,256,128]{3,2,1,0:T(8,128)S(1)}, u32[]{:S(2)}, u32[]{:S(2)}) collective-permute-start(f32[2,2,256,128]{3,2,1,0:T(8,128)S(1)} %get-tuple-element.30), channel_id=1, source_target_pairs={{0,1},{2,3},{4,5},{6,7},{8,9},{10,11},{12,13},{14,15},{16,17},{18,... | collective-permute-start | bytes 1572872 | tf_op jit(solution)/shard_map/ppermute | solution.py:326
  33.1 0.0 collective-permute-done.1.mid_first
  33.1 7.5 %collective-permute-done.2.mid_second = f32[2,2,256,128]{3,2,1,0:T(8,128)S(1)} collective-permute-done((f32[2,2,256,128]{3,2,1,0:T(8,128)S(1)}, f32[2,2,256,128]{3,2,1,0:T(8,128)S(1)}, u32[]{:S(2)}, u32[]{:S(2)}) %collective-permute-start.2) | collective-permute-done | bytes 524320 | tf_op jit(solution)/shard_map/ppermute | solution.py:326
  40.6 0.7 shard_map.55
  41.3 4.5 %collective-permute-start.3 = (f32[4,256,128]{2,1,0:T(8,128)S(1)}, f32[4,256,128]{2,1,0:T(8,128)S(1)}, u32[]{:S(2)}, u32[]{:S(2)}) collective-permute-start(f32[4,256,128]{2,1,0:T(8,128)S(1)} %get-tuple-element.24), channel_id=1, source_target_pairs={{0,256},{256,0},{1,257},{257,1},{2,258},{258,2},{3,259},{259,3},{4... | collective-permute-start | bytes 1572872 | tf_op jit(solution)/shard_map/ppermute | solution.py:325
  45.8 6.1 %collective-permute-done.4.far = f32[2,2,256,128]{3,2,1,0:T(8,128)S(1)} collective-permute-done((f32[2,2,256,128]{3,2,1,0:T(8,128)S(1)}, f32[2,2,256,128]{3,2,1,0:T(8,128)S(1)}, u32[]{:S(2)}, u32[]{:S(2)}) %collective-permute-start.4) | collective-permute-done | bytes 524320 | tf_op jit(solution)/shard_map/ppermute | solution.py:326
  51.8 0.6 shard_map.56
  52.4 1.9 %collective-permute-start.5 = (f32[2,256,128]{2,1,0:T(8,128)S(1)}, f32[2,256,128]{2,1,0:T(8,128)S(1)}, u32[]{:S(2)}, u32[]{:S(2)}) collective-permute-start(f32[2,256,128]{2,1,0:T(8,128)S(1)} %get-tuple-element.27), channel_id=1, source_target_pairs={{0,1},{2,3},{4,5},{6,7},{8,9},{10,11},{12,13},{14,15},{16,17},{18,... | collective-permute-start | bytes 786440 | tf_op jit(solution)/shard_map/ppermute | solution.py:326
  54.4 5.0 %collective-permute-start.6 = (f32[2,256,128]{2,1,0:T(8,128)S(1)}, f32[2,256,128]{2,1,0:T(8,128)S(1)}, u32[]{:S(2)}, u32[]{:S(2)}) collective-permute-start(f32[2,256,128]{2,1,0:T(8,128)S(1)} %get-tuple-element.28), channel_id=1, source_target_pairs={{0,257},{2,259},{4,261},{6,263},{8,265},{10,267},{12,269},{14,271}... | collective-permute-start | bytes 786440 | tf_op jit(solution)/shard_map/ppermute | solution.py:327
  59.4 0.0 collective-permute-done.7.far
  59.4 0.6 shard_map.57
  60.0 5.7 %collective-permute-start.8 = (f32[2,256,128]{2,1,0:T(8,128)S(1)}, f32[2,256,128]{2,1,0:T(8,128)S(1)}, u32[]{:S(2)}, u32[]{:S(2)}) collective-permute-start(f32[2,256,128]{2,1,0:T(8,128)S(1)} %get-tuple-element.31), channel_id=1, source_target_pairs={{1,2},{3,4},{5,6},{7,8},{9,10},{11,12},{13,14},{15,16},{17,18},{19... | collective-permute-start | bytes 786440 | tf_op jit(solution)/shard_map/ppermute | solution.py:326
  65.7 3.9 %collective-permute-start.9 = (f32[2,256,128]{2,1,0:T(8,128)S(1)}, f32[2,256,128]{2,1,0:T(8,128)S(1)}, u32[]{:S(2)}, u32[]{:S(2)}) collective-permute-start(f32[2,256,128]{2,1,0:T(8,128)S(1)} %get-tuple-element.32), channel_id=1, source_target_pairs={{1,258},{3,260},{5,262},{7,264},{9,266},{11,268},{13,270},{15,272}... | collective-permute-start | bytes 786440 | tf_op jit(solution)/shard_map/ppermute | solution.py:327
  69.6 0.0 collective-permute-done.5.same_first
  69.6 0.0 collective-permute-done.6.cross_first
  69.7 4.9 %collective-permute-done.8.same_second = f32[2,256,128]{2,1,0:T(8,128)S(1)} collective-permute-done((f32[2,256,128]{2,1,0:T(8,128)S(1)}, f32[2,256,128]{2,1,0:T(8,128)S(1)}, u32[]{:S(2)}, u32[]{:S(2)}) %collective-permute-start.8) | collective-permute-done | bytes 262176 | tf_op jit(solution)/shard_map/ppermute | solution.py:326
  74.6 5.6 %collective-permute-done.9.cross_second = f32[2,256,128]{2,1,0:T(8,128)S(1)} collective-permute-done((f32[2,256,128]{2,1,0:T(8,128)S(1)}, f32[2,256,128]{2,1,0:T(8,128)S(1)}, u32[]{:S(2)}, u32[]{:S(2)}) %collective-permute-start.9) | collective-permute-done | bytes 262176 | tf_op jit(solution)/shard_map/ppermute | solution.py:327
  80.2 0.0 collective-permute-done.3.handed
  80.2 1.2 %shard_map.58 = f32[4,128,512]{2,1,0:T(8,128)S(1)} custom-call(s32[3]{0:T(128)S(1)} %pad_add_fusion.core_ref.place_ref, f32[4,256,128]{2,1,0:T(8,128)S(1)} %get-tuple-element.23.kept, f32[4,256,128]{2,1,0:T(8,128)S(1)} %collective-permute-done.3.handed, f32[2,256,128]{2,1,0:T(8,128)S(1)} %collective-permute-done.5.same_first, ...), custom_call_target="tpu_custom_call" | custom-call | tf_op jit(solution)/shard_map/pallas_call | solution.py:312
  81.4 1.6 %copy.8 = f32[128,4,512]{2,1,0:T(4,128)} copy(f32[128,4,512]{2,0,1:T(8,128)S(1)} %bitcast.8) | data formatting | bytes 2097152 | tf_op jit(solution)/shard_map/transpose | solution.py:348
Async XLA Ops:
  0.0 2.3 %copy-start = (f32[128,128]{1,0:T(8,128)S(1)}, f32[128,128]{1,0:T(8,128)}, u32[]{:S(2)}) copy-start(f32[128,128]{1,0:T(8,128)} %inverse_ref.3) | copy-start | bytes 196612
  0.0 2.3 %copy-start.1 = (f32[128]{0:T(128)S(1)}, f32[128]{0:T(128)}, u32[]{:S(2)}) copy-start(f32[128]{0:T(128)} %param.7) | copy-start | bytes 1540
  3.7 4.7 %collective-permute-start = (f32[2312,128]{1,0:T(8,128)S(1)}, f32[2312,128]{1,0:T(8,128)S(1)}, u32[]{:S(2)}, u32[]{:S(2)}) collective-permute-start(f32[2312,128]{1,0:T(8,128)S(1)} %pack_send.1), channel_id=1, source_target_pairs={{0,256},{256,0},{1,257},{257,1},{2,258},{258,2},{3,259},{259,3},{4... | collective-permute-start | bytes 3551240 | tf_op jit(solution)/shard_map/ppermute | solution.py:325
  17.3 15.8 %collective-permute-start.1 = (f32[2,2,256,128]{3,2,1,0:T(8,128)S(1)}, f32[2,2,256,128]{3,2,1,0:T(8,128)S(1)}, u32[]{:S(2)}, u32[]{:S(2)}) collective-permute-start(f32[2,2,256,128]{3,2,1,0:T(8,128)S(1)} %get-tuple-element.21), channel_id=1, source_target_pairs={{0,1},{2,3},{4,5},{6,7},{8,9},{10,11},{12,13},{14,15},{16,17},{18,... | collective-permute-start | bytes 1572872 | tf_op jit(solution)/shard_map/ppermute | solution.py:326
  20.4 20.2 %collective-permute-start.2 = (f32[2,2,256,128]{3,2,1,0:T(8,128)S(1)}, f32[2,2,256,128]{3,2,1,0:T(8,128)S(1)}, u32[]{:S(2)}, u32[]{:S(2)}) collective-permute-start(f32[2,2,256,128]{3,2,1,0:T(8,128)S(1)} %get-tuple-element.22), channel_id=1, source_target_pairs={{1,2},{3,4},{5,6},{7,8},{9,10},{11,12},{13,14},{15,16},{17,18},{19... | collective-permute-start | bytes 1572872 | tf_op jit(solution)/shard_map/ppermute | solution.py:326
  26.1 25.7 %collective-permute-start.4 = (f32[2,2,256,128]{3,2,1,0:T(8,128)S(1)}, f32[2,2,256,128]{3,2,1,0:T(8,128)S(1)}, u32[]{:S(2)}, u32[]{:S(2)}) collective-permute-start(f32[2,2,256,128]{3,2,1,0:T(8,128)S(1)} %get-tuple-element.26), channel_id=1, source_target_pairs={{1,2},{3,4},{5,6},{7,8},{9,10},{11,12},{13,14},{15,16},{17,18},{19... | collective-permute-start | bytes 1572872 | tf_op jit(solution)/shard_map/ppermute | solution.py:326
  31.1 28.3 %collective-permute-start.7 = (f32[2,2,256,128]{3,2,1,0:T(8,128)S(1)}, f32[2,2,256,128]{3,2,1,0:T(8,128)S(1)}, u32[]{:S(2)}, u32[]{:S(2)}) collective-permute-start(f32[2,2,256,128]{3,2,1,0:T(8,128)S(1)} %get-tuple-element.30), channel_id=1, source_target_pairs={{0,1},{2,3},{4,5},{6,7},{8,9},{10,11},{12,13},{14,15},{16,17},{18,... | collective-permute-start | bytes 1572872 | tf_op jit(solution)/shard_map/ppermute | solution.py:326
  41.3 38.9 %collective-permute-start.3 = (f32[4,256,128]{2,1,0:T(8,128)S(1)}, f32[4,256,128]{2,1,0:T(8,128)S(1)}, u32[]{:S(2)}, u32[]{:S(2)}) collective-permute-start(f32[4,256,128]{2,1,0:T(8,128)S(1)} %get-tuple-element.24), channel_id=1, source_target_pairs={{0,256},{256,0},{1,257},{257,1},{2,258},{258,2},{3,259},{259,3},{4... | collective-permute-start | bytes 1572872 | tf_op jit(solution)/shard_map/ppermute | solution.py:325
  52.4 17.2 %collective-permute-start.5 = (f32[2,256,128]{2,1,0:T(8,128)S(1)}, f32[2,256,128]{2,1,0:T(8,128)S(1)}, u32[]{:S(2)}, u32[]{:S(2)}) collective-permute-start(f32[2,256,128]{2,1,0:T(8,128)S(1)} %get-tuple-element.27), channel_id=1, source_target_pairs={{0,1},{2,3},{4,5},{6,7},{8,9},{10,11},{12,13},{14,15},{16,17},{18,... | collective-permute-start | bytes 786440 | tf_op jit(solution)/shard_map/ppermute | solution.py:326
  54.4 15.3 %collective-permute-start.6 = (f32[2,256,128]{2,1,0:T(8,128)S(1)}, f32[2,256,128]{2,1,0:T(8,128)S(1)}, u32[]{:S(2)}, u32[]{:S(2)}) collective-permute-start(f32[2,256,128]{2,1,0:T(8,128)S(1)} %get-tuple-element.28), channel_id=1, source_target_pairs={{0,257},{2,259},{4,261},{6,263},{8,265},{10,267},{12,269},{14,271}... | collective-permute-start | bytes 786440 | tf_op jit(solution)/shard_map/ppermute | solution.py:327
  60.0 14.6 %collective-permute-start.8 = (f32[2,256,128]{2,1,0:T(8,128)S(1)}, f32[2,256,128]{2,1,0:T(8,128)S(1)}, u32[]{:S(2)}, u32[]{:S(2)}) collective-permute-start(f32[2,256,128]{2,1,0:T(8,128)S(1)} %get-tuple-element.31), channel_id=1, source_target_pairs={{1,2},{3,4},{5,6},{7,8},{9,10},{11,12},{13,14},{15,16},{17,18},{19... | collective-permute-start | bytes 786440 | tf_op jit(solution)/shard_map/ppermute | solution.py:326
  65.7 14.4 %collective-permute-start.9 = (f32[2,256,128]{2,1,0:T(8,128)S(1)}, f32[2,256,128]{2,1,0:T(8,128)S(1)}, u32[]{:S(2)}, u32[]{:S(2)}) collective-permute-start(f32[2,256,128]{2,1,0:T(8,128)S(1)} %get-tuple-element.32), channel_id=1, source_target_pairs={{1,258},{3,260},{5,262},{7,264},{9,266},{11,268},{13,270},{15,272}... | collective-permute-start | bytes 786440 | tf_op jit(solution)/shard_map/ppermute | solution.py:327

commit v2 on v1

--- a/solution.py
+++ b/solution.py
@@ -16,26 +16,72 @@
 SMEM = pl.BlockSpec(memory_space=pltpu.SMEM)
 
 
-def pack_body(send, core_ref, temp_ref, source_ref, inverse_ref, couple_ref, out_ref):
-    rows, half = temp_ref.shape[0], temp_ref.shape[2] // 2
+def position():
+    return lax.axis_index("depth"), lax.axis_index("lat")
+
+
+def lines_of(array):
+    layers, rows, columns = array.shape
+    return array.reshape(layers, rows, columns // LANES, LANES).transpose(0, 2, 1, 3).reshape(-1, LANES)
+
+
+def array_of(lines, shape):
+    layers, rows, columns = shape
+    return lines.reshape(layers, columns // LANES, rows, LANES).transpose(0, 2, 1, 3).reshape(shape)
+
+
+def pack_lines(send, rows, core, ref, array, out_ref):
+    step = ref.shape[0] // (LANES + 1)
+    tiles = step // rows // 2
+    half = tiles * LANES
     width = half + OVERLAP
-    tiles = half // LANES
     low = [(t, 0, LANES, t * LANES) for t in range(tiles)] + [(tiles, 0, OVERLAP, half)]
     high = [(tiles - 1, LANES - OVERLAP, OVERLAP, 0)] + [
         (tiles + t, 0, LANES, OVERLAP + t * LANES) for t in range(tiles)
     ]
     for slab in range(2):
+
+        @pl.when(core == slab)
+        def _():
+            for row in range(rows):
+                base = (array * rows + row) * width
+                for tile, first, count, place in high if (slab == 1) != send else low:
+                    line = (slab * 2 * tiles + tile) * rows + row
+                    block = ref[pl.ds(line, LANES, stride=step), :].T
+                    out_ref[base + place : base + place + count, :] = block[first : first + count]
+
+
+def pack_send_body(rows, temp_hbm, source_hbm, inverse_hbm, couple_hbm,
+                   out_ref, temp_ref, source_ref, inverse_ref, couple_ref, sems):
+    core, _ = position()
+    lines = temp_hbm.shape[0]
+    step = lines // LANES
+    copies = []
+
+    def copy(origin, target):
+        copies.append(pltpu.make_async_copy(origin, target, sems.at[len(copies)]))
+        copies[-1].start()
+        return copies[-1]
+
+    waits = []
+    for hbm, ref in ((temp_hbm, temp_ref), (source_hbm, source_ref)):
+        waits.append((
+            copy(hbm, ref.at[pl.ds(0, lines)]),
+            copy(hbm.at[pl.ds(0, step)], ref.at[pl.ds(lines, step)]),
+        ))
+    rest = [copy(inverse_hbm, inverse_ref), copy(couple_hbm, couple_ref)]
+    for array, ref in enumerate((temp_ref, source_ref)):
+        for wait in waits[array]:
+            wait.wait()
+        pack_lines(True, rows, core, ref, array, out_ref)
+    for wait in rest:
+        wait.wait()
+    base = out_ref.shape[0] - LANES - 8
+    for slab in range(2):
         turned = (lambda value: pltpu.roll(value, LANES - 1, 1)) if slab == 1 else (lambda value: value)
 
-        @pl.when(core_ref[0] == slab)
+        @pl.when(core == slab)
         def _():
-            for array, ref in enumerate((temp_ref, source_ref)):
-                for row in range(rows):
-                    base = (array * rows + row) * width
-                    for tile, first, count, place in high if (slab == 1) != send else low:
-                        block = turned(ref[row, :, tile * LANES : (tile + 1) * LANES].T)
-                        out_ref[base + place : base + place + count, :] = block[first : first + count]
-            base = 2 * rows * width
             inverse = turned(inverse_ref[...].T)
             if slab == 1:
                 inverse = pltpu.roll(inverse, LANES - 1, 0)
@@ -43,17 +89,32 @@
             out_ref[base + LANES : base + LANES + 8, :] = turned(jnp.broadcast_to(couple_ref[...], (8, LANES)))
 
 
-def pack(send, core, temp, source, inverse, couple):
-    rows, _, columns = temp.shape
+def pack_own_body(rows, temp_ref, source_ref, sent_ref, out_ref):
+    core, _ = position()
+    for array, ref in enumerate((temp_ref, source_ref)):
+        pack_lines(False, rows, core, ref, array, out_ref)
+    base = out_ref.shape[0] - LANES - 8
+    out_ref[base:, :] = sent_ref[base:, :]
+
+
+def pack_send(rows, temp, source, inverse, couple):
+    columns = temp.shape[0] // rows
     length = 2 * rows * (columns // 2 + OVERLAP) + LANES + 8
+    shape = lambda count: jax.ShapeDtypeStruct((count, LANES), jnp.float32)
+    lines = shape(temp.shape[0] // LANES * (LANES + 1))
     return pl.pallas_call(
-        functools.partial(pack_body, send),
-        out_shape=jax.ShapeDtypeStruct((length, LANES), jnp.float32),
-        in_specs=[SMEM, VMEM, VMEM, VMEM, VMEM],
-        out_specs=VMEM,
-        compiler_params=pltpu.CompilerParams(vmem_limit_bytes=8 * 2**20),
-        name="pack_send" if send else "pack_own",
-    )(core, temp, source, inverse, couple)
+        functools.partial(pack_send_body, rows),
+        out_shape=[shape(length), lines, lines],
+        in_specs=[pl.BlockSpec(memory_space=pltpu.HBM)] * 4,
+        out_specs=[VMEM] * 3,
+        scratch_shapes=[
+            pltpu.VMEM(inverse.shape, jnp.float32),
+            pltpu.VMEM(couple.shape, jnp.float32),
+            pltpu.SemaphoreType.DMA((6,)),
+        ],
+        compiler_params=pltpu.CompilerParams(vmem_limit_bytes=12 * 2**20),
+        name="pack_send",
+    )(*(pltpu.with_memory_space_constraint(array, pltpu.HBM) for array in (temp, source, inverse, couple)))
 
 
 def split(value):
@@ -62,14 +123,14 @@
 
 
 class Solver:
-    def __init__(self, rows, width, place_ref, face_ref, mine_ref, other_ref, weights):
-        self.rows, self.width, self.weights = rows, width, weights
-        self.core, self.lat, self.lat_count = place_ref[0], place_ref[1], place_ref[2]
+    def __init__(self, rows, width, lat_count, face_ref, mine_ref, other_ref, weights):
+        self.rows, self.width, self.weights, self.lat_count = rows, width, weights, lat_count
+        self.core, self.lat = position()
         self.odd = lax.rem(self.lat, 2)
         self.payloads = ((self.core, mine_ref), (1 - self.core, other_ref))
-        face = face_ref[0]
         base = 2 * rows * width
         first = self.core == 0
+        face = face_ref[0]
 
         def pick(start, count, slab):
             return jnp.where(first == (slab == 0), mine_ref[start : start + count], other_ref[start : start + count])
@@ -125,8 +186,8 @@
         ref[(*index, slice(PAD + width, 2 * PAD + width))] = zero
 
 
-def strips_body(rows, width, place_ref, face_ref, mine_ref, other_ref, far_first, far_second, strips, weights, last):
-    solver = Solver(rows, width, place_ref, face_ref, mine_ref, other_ref, weights)
+def strips_body(rows, width, lat_count, face_ref, mine_ref, other_ref, far_first, far_second, strips, weights, last):
+    solver = Solver(rows, width, lat_count, face_ref, mine_ref, other_ref, weights)
     middle = slice(PAD, PAD + width)
     clear_pads(strips, [(j, a, s) for j in range(SWEEPS) for a in range(4) for s in range(2)], width)
     for slab, ref in solver.payloads:
@@ -176,9 +237,9 @@
                 ref[k, slab] = last[row + k, slab, pl.ds(start, half)]
 
 
-def core_body(rows, width, place_ref, face_ref, mine_ref, other_ref, strips,
+def core_body(rows, width, lat_count, face_ref, mine_ref, other_ref, strips,
               mid_first, mid_second, near_first, near_second, own, field, rhs_source, weights):
-    solver = Solver(rows, width, place_ref, face_ref, mine_ref, other_ref, weights)
+    solver = Solver(rows, width, lat_count, face_ref, mine_ref, other_ref, weights)
     middle = slice(PAD, PAD + width)
     half = width - OVERLAP
     clear_pads(field, [(b, s, r) for b in range(2) for s in range(2) for r in range(2, field.shape[2] - 2)], width)
@@ -230,27 +291,27 @@
                 ref[k, slab] = field[SWEEPS % 2, slab, row + k, pl.ds(start, half)]
 
 
-def sweeps(place, face, mine, other, rows, half):
+def sweeps(face, mine, other, rows, half, lat_count):
     width = half + OVERLAP
     shape = lambda count: jax.ShapeDtypeStruct((count, 2, half, LANES), jnp.float32)
     weights = pltpu.VMEM((2, 2 * LANES, 2 * LANES), jnp.bfloat16)
     far_first, far_second, strips = pl.pallas_call(
-        functools.partial(strips_body, rows, width),
+        functools.partial(strips_body, rows, width, lat_count),
         out_shape=[
             shape(2),
             shape(2),
             jax.ShapeDtypeStruct((SWEEPS, 4, 2, width + 2 * PAD, LANES), jnp.float32),
         ],
-        in_specs=[SMEM, SMEM, VMEM, VMEM],
+        in_specs=[SMEM] + [VMEM] * 2,
         out_specs=[VMEM] * 3,
         scratch_shapes=[weights, pltpu.VMEM((4, 2, width, LANES), jnp.float32)],
         compiler_params=pltpu.CompilerParams(vmem_limit_bytes=24 * 2**20),
         name="strips",
-    )(place, face, mine, other)
+    )(face, mine, other)
     mid_first, mid_second, near_first, near_second, own = pl.pallas_call(
-        functools.partial(core_body, rows, width),
+        functools.partial(core_body, rows, width, lat_count),
         out_shape=[shape(k) for k in (2, 2, 2, 2, rows)],
-        in_specs=[SMEM, SMEM, VMEM, VMEM, VMEM],
+        in_specs=[SMEM] + [VMEM] * 3,
         out_specs=[VMEM] * 5,
         scratch_shapes=[
             pltpu.VMEM((2, 2, rows + 2 * SWEEPS, width + 2 * PAD, LANES), jnp.float32),
@@ -259,19 +320,20 @@
         ],
         compiler_params=pltpu.CompilerParams(vmem_limit_bytes=32 * 2**20),
         name="core",
-    )(place, face, mine, other, strips)
+    )(face, mine, other, strips)
     return far_first, far_second, mid_first, mid_second, near_first, near_second, own
 
 
-def join_body(place_ref, near, far, same, cross):
-    core = place_ref[0]
+def join_body(near, far, same, cross):
+    core, _ = position()
     for k in range(near.shape[0]):
         same[k] = near[k, core] + far[k, core]
         cross[k] = near[k, 1 - core] + far[k, 1 - core]
 
 
-def hand_body(place_ref, own, mid_first, mid_second, kept, handed):
-    core, odd = place_ref[0], lax.rem(place_ref[1], 2)
+def hand_body(own, mid_first, mid_second, kept, handed):
+    core, lat = position()
+    odd = lax.rem(lat, 2)
     for piece, pair in ((mid_first, odd), (mid_second, 1 - odd)):
         for k in range(2):
             row = 2 * pair + k
@@ -279,40 +341,54 @@
             handed[row] = own[row, 1 - core] + piece[k, 1 - core]
 
 
-def finish_body(place_ref, kept, handed, same_first, cross_first, same_second, cross_second, out_ref):
-    odd = lax.rem(place_ref[1], 2)
-    half = kept.shape[1]
+def finish_body(kept, handed, same_first, cross_first, same_second, cross_second, out_hbm, lines, sems):
+    at_core, lat = position()
+    rows, half, _ = kept.shape
+    tiles = half // LANES
+    step = 2 * tiles * rows
     for core in range(2):
-
-        @pl.when(place_ref[0] == core)
-        def _():
-            for same, cross, pair in ((same_second, cross_second, odd), (same_first, cross_first, 1 - odd)):
-                for k in range(2):
-                    row = 2 * pair + k
-                    for side, base, piece in ((core, kept, same), (1 - core, handed, cross)):
-                        for tile in range(half // LANES):
-                            cut = slice(tile * LANES, (tile + 1) * LANES)
-                            value = base[row, cut] + piece[k, cut]
-                            if core == 1:
-                                value = pltpu.roll(value, 1, 1)
-                            at = side * half + tile * LANES
-                            out_ref[row, :, at : at + LANES] = value.T
+        for odd in range(2):
+
+            @pl.when((at_core == core) & (lax.rem(lat, 2) == odd))
+            def _():
+                copies = []
+                for side, base, pieces in (
+                    (core, kept, (same_first, same_second)),
+                    (1 - core, handed, (cross_first, cross_second)),
+                ):
+                    for tile in range(tiles):
+                        cut = slice(tile * LANES, (tile + 1) * LANES)
+                        place = (side * tiles + tile) * rows
+                        for row in range(rows):
+                            piece = pieces[1] if row // 2 == odd else pieces[0]
+                            value = base[row, cut] + piece[row % 2, cut]
+                            lines[pl.ds(core * step + place + row, LANES, stride=step), :] = value.T
+                        if core == 1:
+                            lines[place : place + rows] = lines[LANES * step + place : LANES * step + place + rows]
+                        copies.append(
+                            pltpu.make_async_copy(
+                                lines.reshape(LANES + 1, step, LANES).at[pl.ds(0, LANES), pl.ds(place, rows)],
+                                out_hbm.reshape(LANES, step, LANES).at[:, pl.ds(place, rows)],
+                                sems.at[side * tiles + tile],
+                            )
+                        )
+                        copies[-1].start()
+                for copy in copies:
+                    copy.wait()
 
 
 def program(temp_old, source, lat_couple, face_couple, block_inverse):
     _, rows, columns = temp_old.shape
     half = columns // 2
-    core, lat = lax.axis_index("depth"), lax.axis_index("lat")
     lat_count = lax.axis_size("lat")
-    place = jnp.stack([core, lat, jnp.int32(lat_count)]).astype(jnp.int32)
     params = pltpu.CompilerParams(vmem_limit_bytes=16 * 2**20)
     piece = lambda *shape: jax.ShapeDtypeStruct((*shape, half, LANES), jnp.float32)
 
     def call(body, outs, *arrays):
         return pl.pallas_call(
-            body, out_shape=outs, in_specs=[SMEM] + [VMEM] * len(arrays), out_specs=[VMEM] * len(outs),
+            body, out_shape=outs, in_specs=[VMEM] * len(arrays), out_specs=[VMEM] * len(outs),
             compiler_params=params,
-        )(place, *arrays)
+        )(*arrays)
 
     pairs = [
         [(i, i + 1) for i in range(start, lat_count - 1, 2)] + [(i + 1, i) for i in range(start, lat_count - 1, 2)]
@@ -326,12 +402,14 @@
     exchange = lambda value, group: lax.ppermute(value, "lat", pairs[group])
     cross = lambda value, group: lax.ppermute(value, ("depth", "lat"), crossed[group])
 
-    temp, src = temp_old.transpose(1, 0, 2), source.transpose(1, 0, 2)
-    couple = lat_couple.reshape(1, LANES)
-    other = swap(pack(True, place, temp, src, block_inverse, couple))
-    mine = pack(False, place, temp, src, block_inverse, couple)
+    temp, src = lines_of(temp_old), lines_of(source)
+    sent, temp, src = pack_send(rows, temp, src, block_inverse, lat_couple.reshape(1, LANES))
+    other = swap(sent)
+    (mine,) = call(
+        functools.partial(pack_own_body, rows), [jax.ShapeDtypeStruct(sent.shape, jnp.float32)], temp, src, sent
+    )
     far_first, far_second, mid_first, mid_second, near_first, near_second, own = sweeps(
-        place, face_couple, mine, other, rows, half
+        face_couple, mine, other, rows, half, lat_count
     )
     far_first, far_second = exchange(far_first, 0), exchange(far_second, 1)
     mid_first, mid_second = exchange(mid_first, 0), exchange(mid_second, 1)
@@ -341,11 +419,20 @@
     same_first, cross_first = call(join_body, joined, near_first, far_second)
     same_first, cross_first = exchange(same_first, 0), cross(cross_first, 0)
     kept, handed = call(hand_body, [piece(rows), piece(rows)], own, mid_first, mid_second)
-    (result,) = call(
-        finish_body, [jax.ShapeDtypeStruct((rows, LANES, columns), jnp.float32)],
-        kept, swap(handed), same_first, cross_first, same_second, cross_second,
-    )
-    return result.transpose(1, 0, 2)
+    lines = temp_old.size // LANES
+    result = pl.pallas_call(
+        finish_body,
+        out_shape=jax.ShapeDtypeStruct((lines, LANES), jnp.float32),
+        in_specs=[VMEM] * 6,
+        out_specs=pl.BlockSpec(memory_space=pltpu.HBM),
+        scratch_shapes=[
+            pltpu.VMEM((lines // LANES * (LANES + 1), LANES), jnp.float32),
+            pltpu.SemaphoreType.DMA((columns // LANES,)),
+        ],
+        compiler_params=params,
+        name="finish",
+    )(kept, swap(handed), same_first, cross_first, same_second, cross_second)
+    return array_of(result, temp_old.shape)
 
 
 def solution(mesh):

time: 83.4 us -> 78.9 us (0.946)
  local copies, waits for them, and re-layouts: 3.85 us -> 0 us
  Pallas kernels: 14.7 us -> 12.4 us
  waiting for transfers between devices: 24.5 us -> 26.2 us
    transpose x2 -> x0, local copies, waits for them, and re-layouts: 3.84 us -> none  [the longest x1 2.2 us: program(): temp, src = (temp_old.transpose(1, 0, 2), source.transpose(1, 0, 2))]
    pallas_call x8, Pallas kernels: 14.7 us -> 12.4 us  [the longest x1 5.65 us: sweeps(): pl.pallas_call(functools.partial(core_body, rows, width, lat_count), out_...]
    ppermute x6, waiting for transfers between devices: 18.5 us -> 19.3 us  [program(): exchange = lambda value, group: lax.ppermute(value, 'lat', pairs[group])]
  transfers between devices with their start and end apart: 10 -> 10, of which waited for: 5 -> 5; matrix products, arithmetic and copies ran while one was open for 0% -> 0% of each run, Pallas kernels for 4% -> 1%
where the time goes in v2:
time: 78.9 us; the launch traced here: 78.5 us
  starting transfers between devices  39.1 us (50%)
  waiting for transfers between devices  26.2 us (33%)
  Pallas kernels  12.4 us (16%)
  between operations  0.8 us (1%)
    ppermute x6, starting transfers between devices, program(): exchange = lambda value, group: lax.ppermute(value, 'lat', pairs[group])  23.4 us
    ppermute x6, waiting for transfers between devices, program(): exchange = lambda value, group: lax.ppermute(value, 'lat', pairs[group])  19.3 us
    ppermute x2, starting transfers between devices, program(): lax.ppermute(value, ('depth', 'lat'), crossed[group])  8.91 us
    ppermute x2, starting transfers between devices, program(): swap = lambda value: lax.ppermute(value, 'depth', [(0, 1), (1, 0)])  6.81 us
    pallas_call x1, Pallas kernels, sweeps(): pl.pallas_call(functools.partial(core_body, rows, width, lat_count), out_...  5.65 us
    ppermute x2, waiting for transfers between devices, program(): lax.ppermute(value, ('depth', 'lat'), crossed[group])  5.62 us
    pallas_call x1, Pallas kernels, sweeps(): pl.pallas_call(functools.partial(strips_body, rows, width, lat_count), ou...  2.56 us
    pallas_call x1, Pallas kernels, pack_send(): pl.pallas_call(functools.partial(pack_send_body, rows), out_shape=[shape(...  2.17 us
  transfers between devices with their start and end apart: 10, of which 5 were waited for; matrix products, arithmetic and copies ran while one was open for 0% of the time, Pallas kernels for 1%

profile of v2, /device:TPU:257, one launch (start us, length us, event | category | flops | bytes accessed | tf_op | source)
XLA Modules:
  0.0 78.5 jit_solution(6392987419476051165)
XLA Ops:
  0.0 2.2 %pack_send.1 = (f32[2312,128]{1,0:T(8,128)S(1)}, f32[2064,128]{1,0:T(8,128)S(1)}, f32[2064,128]{1,0:T(8,128)S(1)}) custom-call(f32[2048,128]{1,0:T(8,128)} %bitcast.16, f32[2048,128]{1,0:T(8,128)} %bitcast.17, f32[128,128]{1,0:T(8,128)} %inverse_hbm.1, f32[1,128]{1,0:T(1,128)} %bitcast.18), custom_call_target="tpu_custom_call" | custom-call | tf_op jit(solution)/shard_map/pack_send/pallas_call | solution.py:105
  2.2 2.5 %collective-permute-start = (f32[2312,128]{1,0:T(8,128)S(1)}, f32[2312,128]{1,0:T(8,128)S(1)}, u32[]{:S(2)}, u32[]{:S(2)}) collective-permute-start(f32[2312,128]{1,0:T(8,128)S(1)} %get-tuple-element.24.sent_ref), channel_id=1, source_target_pairs={{0,256},{256,0},{1,257},{257,1},{2,258},{258,2},{3,259},{259,3},{4... | collective-permute-start | bytes 3551240 | tf_op jit(solution)/shard_map/ppermute | solution.py:401
  5.4 0.6 shard_map.55.mine_ref
  6.0 1.2 %collective-permute-done.other_ref = f32[2312,128]{1,0:T(8,128)S(1)} collective-permute-done((f32[2312,128]{1,0:T(8,128)S(1)}, f32[2312,128]{1,0:T(8,128)S(1)}, u32[]{:S(2)}, u32[]{:S(2)}) %collective-permute-start) | collective-permute-done | bytes 1183776 | tf_op jit(solution)/shard_map/ppermute | solution.py:401
  7.2 2.6 %strips.1 = (f32[2,2,256,128]{3,2,1,0:T(8,128)S(1)}, f32[2,2,256,128]{3,2,1,0:T(8,128)S(1)}, f32[6,4,2,288,128]{4,3,2,1,0:T(8,128)S(1)}) custom-call(f32[1]{0:T(128)S(6)} %copy.9.face_ref, f32[2312,128]{1,0:T(8,128)S(1)} %shard_map.55.mine_ref, f32[2312,128]{1,0:T(8,128)S(1)} %collective-permute-done.other_ref), custom_call_target="tpu_custom_call" | custom-call | tf_op jit(solution)/shard_map/strips/pallas_call | solution.py:298
  9.7 5.7 %core.1 = (f32[2,2,256,128]{3,2,1,0:T(8,128)S(1)}, f32[2,2,256,128]{3,2,1,0:T(8,128)S(1)}, f32[2,2,256,128]{3,2,1,0:T(8,128)S(1)}, f32[2,2,256,128]{3,2,1,0:T(8,128)S(1)}, f32[4,2,256,128]{3,2,1,0:T(8,128)S(1)}) custom-call(f32[1]{0:T(128)S(6)} %copy.9.face_ref, f32[2312,128]{1,0:T(8,128)S(1)} %shard_map.55.mine_ref, ...), custom_call_target="tpu_custom_call" | custom-call | tf_op jit(solution)/shard_map/core/pallas_call | solution.py:311
  15.4 3.1 %collective-permute-start.1 = (f32[2,2,256,128]{3,2,1,0:T(8,128)S(1)}, f32[2,2,256,128]{3,2,1,0:T(8,128)S(1)}, u32[]{:S(2)}, u32[]{:S(2)}) collective-permute-start(f32[2,2,256,128]{3,2,1,0:T(8,128)S(1)} %get-tuple-element.27), channel_id=1, source_target_pairs={{0,1},{2,3},{4,5},{6,7},{8,9},{10,11},{12,13},{14,15},{16,17},{18,... | collective-permute-start | bytes 1572872 | tf_op jit(solution)/shard_map/ppermute | solution.py:402
  18.5 5.7 %collective-permute-start.2 = (f32[2,2,256,128]{3,2,1,0:T(8,128)S(1)}, f32[2,2,256,128]{3,2,1,0:T(8,128)S(1)}, u32[]{:S(2)}, u32[]{:S(2)}) collective-permute-start(f32[2,2,256,128]{3,2,1,0:T(8,128)S(1)} %get-tuple-element.28), channel_id=1, source_target_pairs={{1,2},{3,4},{5,6},{7,8},{9,10},{11,12},{13,14},{15,16},{17,18},{19... | collective-permute-start | bytes 1572872 | tf_op jit(solution)/shard_map/ppermute | solution.py:402
  24.3 5.0 %collective-permute-start.4 = (f32[2,2,256,128]{3,2,1,0:T(8,128)S(1)}, f32[2,2,256,128]{3,2,1,0:T(8,128)S(1)}, u32[]{:S(2)}, u32[]{:S(2)}) collective-permute-start(f32[2,2,256,128]{3,2,1,0:T(8,128)S(1)} %get-tuple-element.32), channel_id=1, source_target_pairs={{1,2},{3,4},{5,6},{7,8},{9,10},{11,12},{13,14},{15,16},{17,18},{19... | collective-permute-start | bytes 1572872 | tf_op jit(solution)/shard_map/ppermute | solution.py:402
  29.3 1.9 %collective-permute-start.7 = (f32[2,2,256,128]{3,2,1,0:T(8,128)S(1)}, f32[2,2,256,128]{3,2,1,0:T(8,128)S(1)}, u32[]{:S(2)}, u32[]{:S(2)}) collective-permute-start(f32[2,2,256,128]{3,2,1,0:T(8,128)S(1)} %get-tuple-element.36), channel_id=1, source_target_pairs={{0,1},{2,3},{4,5},{6,7},{8,9},{10,11},{12,13},{14,15},{16,17},{18,... | collective-permute-start | bytes 1572872 | tf_op jit(solution)/shard_map/ppermute | solution.py:402
  31.2 0.0 collective-permute-done.1.mid_first
  31.2 7.6 %collective-permute-done.2.mid_second = f32[2,2,256,128]{3,2,1,0:T(8,128)S(1)} collective-permute-done((f32[2,2,256,128]{3,2,1,0:T(8,128)S(1)}, f32[2,2,256,128]{3,2,1,0:T(8,128)S(1)}, u32[]{:S(2)}, u32[]{:S(2)}) %collective-permute-start.2) | collective-permute-done | bytes 524320 | tf_op jit(solution)/shard_map/ppermute | solution.py:402
  38.8 0.1 shard_map.56
  38.9 4.3 %collective-permute-start.3 = (f32[4,256,128]{2,1,0:T(8,128)S(1)}, f32[4,256,128]{2,1,0:T(8,128)S(1)}, u32[]{:S(2)}, u32[]{:S(2)}) collective-permute-start(f32[4,256,128]{2,1,0:T(8,128)S(1)} %get-tuple-element.30), channel_id=1, source_target_pairs={{0,256},{256,0},{1,257},{257,1},{2,258},{258,2},{3,259},{259,3},{4... | collective-permute-start | bytes 1572872 | tf_op jit(solution)/shard_map/ppermute | solution.py:401
  43.2 6.8 %collective-permute-done.4.far = f32[2,2,256,128]{3,2,1,0:T(8,128)S(1)} collective-permute-done((f32[2,2,256,128]{3,2,1,0:T(8,128)S(1)}, f32[2,2,256,128]{3,2,1,0:T(8,128)S(1)}, u32[]{:S(2)}, u32[]{:S(2)}) %collective-permute-start.4) | collective-permute-done | bytes 524320 | tf_op jit(solution)/shard_map/ppermute | solution.py:402
  50.0 0.1 shard_map.57
  50.1 1.9 %collective-permute-start.5 = (f32[2,256,128]{2,1,0:T(8,128)S(1)}, f32[2,256,128]{2,1,0:T(8,128)S(1)}, u32[]{:S(2)}, u32[]{:S(2)}) collective-permute-start(f32[2,256,128]{2,1,0:T(8,128)S(1)} %get-tuple-element.33), channel_id=1, source_target_pairs={{0,1},{2,3},{4,5},{6,7},{8,9},{10,11},{12,13},{14,15},{16,17},{18,... | collective-permute-start | bytes 786440 | tf_op jit(solution)/shard_map/ppermute | solution.py:402
  52.0 4.9 %collective-permute-start.6 = (f32[2,256,128]{2,1,0:T(8,128)S(1)}, f32[2,256,128]{2,1,0:T(8,128)S(1)}, u32[]{:S(2)}, u32[]{:S(2)}) collective-permute-start(f32[2,256,128]{2,1,0:T(8,128)S(1)} %get-tuple-element.34), channel_id=1, source_target_pairs={{0,257},{2,259},{4,261},{6,263},{8,265},{10,267},{12,269},{14,271}... | collective-permute-start | bytes 786440 | tf_op jit(solution)/shard_map/ppermute | solution.py:403
  57.0 0.0 collective-permute-done.7.far
  57.0 0.1 shard_map.58
  57.1 5.7 %collective-permute-start.8 = (f32[2,256,128]{2,1,0:T(8,128)S(1)}, f32[2,256,128]{2,1,0:T(8,128)S(1)}, u32[]{:S(2)}, u32[]{:S(2)}) collective-permute-start(f32[2,256,128]{2,1,0:T(8,128)S(1)} %get-tuple-element.37), channel_id=1, source_target_pairs={{1,2},{3,4},{5,6},{7,8},{9,10},{11,12},{13,14},{15,16},{17,18},{19... | collective-permute-start | bytes 786440 | tf_op jit(solution)/shard_map/ppermute | solution.py:402
  62.8 4.0 %collective-permute-start.9 = (f32[2,256,128]{2,1,0:T(8,128)S(1)}, f32[2,256,128]{2,1,0:T(8,128)S(1)}, u32[]{:S(2)}, u32[]{:S(2)}) collective-permute-start(f32[2,256,128]{2,1,0:T(8,128)S(1)} %get-tuple-element.38), channel_id=1, source_target_pairs={{1,258},{3,260},{5,262},{7,264},{9,266},{11,268},{13,270},{15,272}... | collective-permute-start | bytes 786440 | tf_op jit(solution)/shard_map/ppermute | solution.py:403
  66.8 0.0 collective-permute-done.5.same_first
  66.8 0.0 collective-permute-done.6.cross_first
  66.8 4.9 %collective-permute-done.8.same_second = f32[2,256,128]{2,1,0:T(8,128)S(1)} collective-permute-done((f32[2,256,128]{2,1,0:T(8,128)S(1)}, f32[2,256,128]{2,1,0:T(8,128)S(1)}, u32[]{:S(2)}, u32[]{:S(2)}) %collective-permute-start.8) | collective-permute-done | bytes 262176 | tf_op jit(solution)/shard_map/ppermute | solution.py:402
  71.7 5.6 %collective-permute-done.9.cross_second = f32[2,256,128]{2,1,0:T(8,128)S(1)} collective-permute-done((f32[2,256,128]{2,1,0:T(8,128)S(1)}, f32[2,256,128]{2,1,0:T(8,128)S(1)}, u32[]{:S(2)}, u32[]{:S(2)}) %collective-permute-start.9) | collective-permute-done | bytes 262176 | tf_op jit(solution)/shard_map/ppermute | solution.py:403
  77.3 0.0 collective-permute-done.3.handed
  77.3 1.2 %finish.1 = f32[2048,128]{1,0:T(8,128)} custom-call(f32[4,256,128]{2,1,0:T(8,128)S(1)} %get-tuple-element.29.kept, f32[4,256,128]{2,1,0:T(8,128)S(1)} %collective-permute-done.3.handed, f32[2,256,128]{2,1,0:T(8,128)S(1)} %collective-permute-done.5.same_first, f32[2,256,128]{2,1,0:T(8,128)S(1)} %collective-permute-done.6.cross_first, ...), custom_call_target="tpu_custom_call" | custom-call | tf_op jit(solution)/shard_map/finish/pallas_call | solution.py:423
Async XLA Ops:
  2.2 5.0 %collective-permute-start = (f32[2312,128]{1,0:T(8,128)S(1)}, f32[2312,128]{1,0:T(8,128)S(1)}, u32[]{:S(2)}, u32[]{:S(2)}) collective-permute-start(f32[2312,128]{1,0:T(8,128)S(1)} %get-tuple-element.24.sent_ref), channel_id=1, source_target_pairs={{0,256},{256,0},{1,257},{257,1},{2,258},{258,2},{3,259},{259,3},{4... | collective-permute-start | bytes 3551240 | tf_op jit(solution)/shard_map/ppermute | solution.py:401
  15.4 15.8 %collective-permute-start.1 = (f32[2,2,256,128]{3,2,1,0:T(8,128)S(1)}, f32[2,2,256,128]{3,2,1,0:T(8,128)S(1)}, u32[]{:S(2)}, u32[]{:S(2)}) collective-permute-start(f32[2,2,256,128]{3,2,1,0:T(8,128)S(1)} %get-tuple-element.27), channel_id=1, source_target_pairs={{0,1},{2,3},{4,5},{6,7},{8,9},{10,11},{12,13},{14,15},{16,17},{18,... | collective-permute-start | bytes 1572872 | tf_op jit(solution)/shard_map/ppermute | solution.py:402
  18.5 20.3 %collective-permute-start.2 = (f32[2,2,256,128]{3,2,1,0:T(8,128)S(1)}, f32[2,2,256,128]{3,2,1,0:T(8,128)S(1)}, u32[]{:S(2)}, u32[]{:S(2)}) collective-permute-start(f32[2,2,256,128]{3,2,1,0:T(8,128)S(1)} %get-tuple-element.28), channel_id=1, source_target_pairs={{1,2},{3,4},{5,6},{7,8},{9,10},{11,12},{13,14},{15,16},{17,18},{19... | collective-permute-start | bytes 1572872 | tf_op jit(solution)/shard_map/ppermute | solution.py:402
  24.3 25.8 %collective-permute-start.4 = (f32[2,2,256,128]{3,2,1,0:T(8,128)S(1)}, f32[2,2,256,128]{3,2,1,0:T(8,128)S(1)}, u32[]{:S(2)}, u32[]{:S(2)}) collective-permute-start(f32[2,2,256,128]{3,2,1,0:T(8,128)S(1)} %get-tuple-element.32), channel_id=1, source_target_pairs={{1,2},{3,4},{5,6},{7,8},{9,10},{11,12},{13,14},{15,16},{17,18},{19... | collective-permute-start | bytes 1572872 | tf_op jit(solution)/shard_map/ppermute | solution.py:402
  29.3 27.7 %collective-permute-start.7 = (f32[2,2,256,128]{3,2,1,0:T(8,128)S(1)}, f32[2,2,256,128]{3,2,1,0:T(8,128)S(1)}, u32[]{:S(2)}, u32[]{:S(2)}) collective-permute-start(f32[2,2,256,128]{3,2,1,0:T(8,128)S(1)} %get-tuple-element.36), channel_id=1, source_target_pairs={{0,1},{2,3},{4,5},{6,7},{8,9},{10,11},{12,13},{14,15},{16,17},{18,... | collective-permute-start | bytes 1572872 | tf_op jit(solution)/shard_map/ppermute | solution.py:402
  38.9 38.4 %collective-permute-start.3 = (f32[4,256,128]{2,1,0:T(8,128)S(1)}, f32[4,256,128]{2,1,0:T(8,128)S(1)}, u32[]{:S(2)}, u32[]{:S(2)}) collective-permute-start(f32[4,256,128]{2,1,0:T(8,128)S(1)} %get-tuple-element.30), channel_id=1, source_target_pairs={{0,256},{256,0},{1,257},{257,1},{2,258},{258,2},{3,259},{259,3},{4... | collective-permute-start | bytes 1572872 | tf_op jit(solution)/shard_map/ppermute | solution.py:401
  50.1 16.7 %collective-permute-start.5 = (f32[2,256,128]{2,1,0:T(8,128)S(1)}, f32[2,256,128]{2,1,0:T(8,128)S(1)}, u32[]{:S(2)}, u32[]{:S(2)}) collective-permute-start(f32[2,256,128]{2,1,0:T(8,128)S(1)} %get-tuple-element.33), channel_id=1, source_target_pairs={{0,1},{2,3},{4,5},{6,7},{8,9},{10,11},{12,13},{14,15},{16,17},{18,... | collective-permute-start | bytes 786440 | tf_op jit(solution)/shard_map/ppermute | solution.py:402
  52.0 14.8 %collective-permute-start.6 = (f32[2,256,128]{2,1,0:T(8,128)S(1)}, f32[2,256,128]{2,1,0:T(8,128)S(1)}, u32[]{:S(2)}, u32[]{:S(2)}) collective-permute-start(f32[2,256,128]{2,1,0:T(8,128)S(1)} %get-tuple-element.34), channel_id=1, source_target_pairs={{0,257},{2,259},{4,261},{6,263},{8,265},{10,267},{12,269},{14,271}... | collective-permute-start | bytes 786440 | tf_op jit(solution)/shard_map/ppermute | solution.py:403
  57.1 14.7 %collective-permute-start.8 = (f32[2,256,128]{2,1,0:T(8,128)S(1)}, f32[2,256,128]{2,1,0:T(8,128)S(1)}, u32[]{:S(2)}, u32[]{:S(2)}) collective-permute-start(f32[2,256,128]{2,1,0:T(8,128)S(1)} %get-tuple-element.37), channel_id=1, source_target_pairs={{1,2},{3,4},{5,6},{7,8},{9,10},{11,12},{13,14},{15,16},{17,18},{19... | collective-permute-start | bytes 786440 | tf_op jit(solution)/shard_map/ppermute | solution.py:402
  62.8 14.5 %collective-permute-start.9 = (f32[2,256,128]{2,1,0:T(8,128)S(1)}, f32[2,256,128]{2,1,0:T(8,128)S(1)}, u32[]{:S(2)}, u32[]{:S(2)}) collective-permute-start(f32[2,256,128]{2,1,0:T(8,128)S(1)} %get-tuple-element.38), channel_id=1, source_target_pairs={{1,258},{3,260},{5,262},{7,264},{9,266},{11,268},{13,270},{15,272}... | collective-permute-start | bytes 786440 | tf_op jit(solution)/shard_map/ppermute | solution.py:403

commit v3 on v2

--- a/solution.py
+++ b/solution.py
@@ -30,70 +30,102 @@
     return lines.reshape(layers, columns // LANES, rows, LANES).transpose(0, 2, 1, 3).reshape(shape)
 
 
-def pack_lines(send, rows, core, ref, array, out_ref):
-    step = ref.shape[0] // (LANES + 1)
+def window_pieces(rows, step, upper):
     tiles = step // rows // 2
     half = tiles * LANES
-    width = half + OVERLAP
-    low = [(t, 0, LANES, t * LANES) for t in range(tiles)] + [(tiles, 0, OVERLAP, half)]
-    high = [(tiles - 1, LANES - OVERLAP, OVERLAP, 0)] + [
-        (tiles + t, 0, LANES, OVERLAP + t * LANES) for t in range(tiles)
+    if not upper:
+        return [(t, 0, LANES, t * LANES) for t in range(tiles)] + [(tiles, 0, OVERLAP, half)]
+    return [(tiles + t, 0, LANES, OVERLAP + t * LANES) for t in range(tiles)] + [
+        (tiles - 1, LANES - OVERLAP, OVERLAP, 0)
     ]
-    for slab in range(2):
-
-        @pl.when(core == slab)
-        def _():
-            for row in range(rows):
-                base = (array * rows + row) * width
-                for tile, first, count, place in high if (slab == 1) != send else low:
-                    line = (slab * 2 * tiles + tile) * rows + row
-                    block = ref[pl.ds(line, LANES, stride=step), :].T
-                    out_ref[base + place : base + place + count, :] = block[first : first + count]
+
+
+def pack_piece(rows, slab, ref, array, piece, out_ref, scale=None):
+    step = ref.shape[0] // (LANES + 1)
+    width = step // rows // 2 * LANES + OVERLAP
+    tile, first, count, place = piece
+    for row in range(rows):
+        base = (array * rows + row) * width + place
+        block = ref[pl.ds((slab * step) + tile * rows + row, LANES, stride=step), :].T
+        block = block[first : first + count]
+        out_ref[base : base + count, :] = block if scale is None else block * scale
 
 
 def pack_send_body(rows, temp_hbm, source_hbm, inverse_hbm, couple_hbm,
                    out_ref, temp_ref, source_ref, inverse_ref, couple_ref, sems):
-    core, _ = position()
-    lines = temp_hbm.shape[0]
-    step = lines // LANES
-    copies = []
-
-    def copy(origin, target):
-        copies.append(pltpu.make_async_copy(origin, target, sems.at[len(copies)]))
-        copies[-1].start()
-        return copies[-1]
-
-    waits = []
-    for hbm, ref in ((temp_hbm, temp_ref), (source_hbm, source_ref)):
-        waits.append((
-            copy(hbm, ref.at[pl.ds(0, lines)]),
-            copy(hbm.at[pl.ds(0, step)], ref.at[pl.ds(lines, step)]),
-        ))
-    rest = [copy(inverse_hbm, inverse_ref), copy(couple_hbm, couple_ref)]
-    for array, ref in enumerate((temp_ref, source_ref)):
-        for wait in waits[array]:
-            wait.wait()
-        pack_lines(True, rows, core, ref, array, out_ref)
-    for wait in rest:
-        wait.wait()
-    base = out_ref.shape[0] - LANES - 8
+    at_core, _ = position()
+    step = temp_hbm.shape[0] // LANES
+    tiles = step // rows
+    arrays = ((temp_hbm, temp_ref), (source_hbm, source_ref))
+
+    def tile_copy(array, tile):
+        hbm, ref = arrays[array]
+        cut = pl.ds(tile * rows, rows)
+        return pltpu.make_async_copy(
+            hbm.reshape(LANES, step, LANES).at[:, cut],
+            ref.reshape(LANES + 1, step, LANES).at[pl.ds(0, LANES), cut],
+            sems.at[array * tiles + tile],
+        )
+
+    inverse_copy = pltpu.make_async_copy(inverse_hbm, inverse_ref, sems.at[2 * tiles])
+    couple_copy = pltpu.make_async_copy(couple_hbm, couple_ref, sems.at[2 * tiles + 1])
     for slab in range(2):
+        pieces = window_pieces(rows, step, slab == 0)
+        unused = [tile for tile in range(tiles) if tile not in [piece[0] for piece in pieces]]
         turned = (lambda value: pltpu.roll(value, LANES - 1, 1)) if slab == 1 else (lambda value: value)
 
-        @pl.when(core == slab)
+        @pl.when(at_core == slab)
         def _():
-            inverse = turned(inverse_ref[...].T)
+            inverse_copy.start()
+            couple_copy.start()
+            for array in range(2):
+                for piece in pieces:
+                    tile_copy(array, piece[0]).start()
+            for array in range(2):
+                for tile in unused:
+                    tile_copy(array, tile).start()
+
+            def arrive(array, tile):
+                tile_copy(array, tile).wait()
+                if slab == 1:
+                    ref = arrays[array][1]
+                    ref[LANES * step + tile * rows : LANES * step + (tile + 1) * rows] = ref[
+                        tile * rows : (tile + 1) * rows
+                    ]
+
+            inverse_copy.wait()
+            couple_copy.wait()
+            base = out_ref.shape[0] - LANES - 8
+            inverse = turned((inverse_ref[...] * couple_ref[...]).T)
             if slab == 1:
                 inverse = pltpu.roll(inverse, LANES - 1, 0)
             out_ref[base : base + LANES, :] = inverse
-            out_ref[base + LANES : base + LANES + 8, :] = turned(jnp.broadcast_to(couple_ref[...], (8, LANES)))
+            scale = 1.0 / turned(jnp.broadcast_to(couple_ref[...], (8, LANES)))
+            out_ref[base + LANES :, :] = scale
+            for array in range(2):
+                for piece in pieces:
+                    arrive(array, piece[0])
+                    pack_piece(
+                        rows, slab, arrays[array][1], array, piece, out_ref, scale[0:1] if array == 1 else None
+                    )
+            for array in range(2):
+                for tile in unused:
+                    arrive(array, tile)
 
 
 def pack_own_body(rows, temp_ref, source_ref, sent_ref, out_ref):
     core, _ = position()
-    for array, ref in enumerate((temp_ref, source_ref)):
-        pack_lines(False, rows, core, ref, array, out_ref)
+    step = temp_ref.shape[0] // (LANES + 1)
     base = out_ref.shape[0] - LANES - 8
+    scale = sent_ref[base + LANES : base + LANES + 1, :]
+    for slab in range(2):
+
+        @pl.when(core == slab)
+        def _():
+            for array, ref in enumerate((temp_ref, source_ref)):
+                for piece in window_pieces(rows, step, slab == 1):
+                    pack_piece(rows, slab, ref, array, piece, out_ref, scale if array == 1 else None)
+
     out_ref[base:, :] = sent_ref[base:, :]
 
 
@@ -110,7 +142,7 @@
         scratch_shapes=[
             pltpu.VMEM(inverse.shape, jnp.float32),
             pltpu.VMEM(couple.shape, jnp.float32),
-            pltpu.SemaphoreType.DMA((6,)),
+            pltpu.SemaphoreType.DMA((2 * columns // LANES + 2,)),
         ],
         compiler_params=pltpu.CompilerParams(vmem_limit_bytes=12 * 2**20),
         name="pack_send",
@@ -135,7 +167,6 @@
         def pick(start, count, slab):
             return jnp.where(first == (slab == 0), mine_ref[start : start + count], other_ref[start : start + count])
 
-        self.couples = [pick(base + LANES, 8, slab)[0:1] for slab in range(2)]
         for slab in range(2):
             high, low = split(pick(base, LANES, slab))
             weights[slab, :LANES, :LANES] = high
@@ -143,7 +174,9 @@
             weights[slab, :LANES, LANES:] = low
             weights[slab, LANES:, LANES:] = jnp.zeros((LANES, LANES), jnp.bfloat16)
         lane = lax.broadcasted_iota(jnp.int32, (1, LANES), 1)
-        self.face_last = jnp.where(lane == LANES - 1, face, 0.0)
+        self.face_last = [
+            jnp.where(lane == LANES - 1, face * pick(base + LANES, 8, slab)[0:1], 0.0) for slab in range(2)
+        ]
 
     def inside(self, row):
         grid_row = self.lat * self.rows - SWEEPS + row
@@ -158,22 +191,20 @@
         return [solved[k * self.width : (k + 1) * self.width] for k in range(len(sides))]
 
     def advance(self, rows, sums, unders, extras, store):
-        gains = [[couple * self.inside(row) for couple in self.couples] for row in rows]
-
         def side(k, slab):
-            value = sums(k, slab) * gains[k][slab]
+            value = sums(k, slab)
             extra = extras(k, slab)
             return value if extra is None else value + extra
 
         upper = []
         for k in range(len(rows)):
             value, under = side(k, 0), unders(k)
-            upper.append(value if under is None else value + under * self.face_last)
+            upper.append(value if under is None else value + under * self.face_last[0])
         upper = self.apply(0, upper)
         for k, value in enumerate(upper):
             store(k, 0, value)
         lower = self.apply(
-            1, [side(k, 1) + upper[k] * self.face_last for k in range(len(rows))]
+            1, [side(k, 1) + upper[k] * self.face_last[1] for k in range(len(rows))]
         )
         for k, value in enumerate(lower):
             store(k, 1, value)
@@ -237,55 +268,104 @@
                 ref[k, slab] = last[row + k, slab, pl.ds(start, half)]
 
 
-def core_body(rows, width, lat_count, face_ref, mine_ref, other_ref, strips,
-              mid_first, mid_second, near_first, near_second, own, field, rhs_source, weights):
+def sums_of(solver, old, at):
+    rows, width = solver.rows, solver.width
+    middle = slice(PAD, PAD + width)
+
+    def beside(row, step, slab):
+        value = old(row + step, slab, middle)
+        edges = {-1: (SWEEPS - rows, SWEEPS), 1: (SWEEPS + rows - 1, SWEEPS + 2 * rows - 1)}[step]
+        return value * solver.inside(row + step) if row in edges else value
+
+    def sums(k, slab):
+        row = at[k]
+        return (beside(row, -1, slab) + beside(row, 1, slab)) + (
+            old(row, slab, slice(PAD - 1, PAD - 1 + width)) + old(row, slab, slice(PAD + 1, PAD + 1 + width))
+        )
+
+    return sums
+
+
+def middle_body(rows, width, lat_count, face_ref, mine_ref, other_ref, strips,
+                mid_first, mid_second, inner, source_ref, weights, last):
+    solver = Solver(rows, width, lat_count, face_ref, mine_ref, other_ref, weights)
+    middle = slice(PAD, PAD + width)
+    clear_pads(inner, [(j, a, s) for j in range(SWEEPS - 1) for a in range(4) for s in range(2)], width)
+    for slab, ref in solver.payloads:
+        for row in range(rows):
+            source_ref[slab, row] = ref[(rows + row) * width : (rows + row + 1) * width]
+
+    def sweep(reach):
+        low, high = SWEEPS + 2 - reach, SWEEPS + rows - 4 + reach
+        at = [low, low + 1] if reach == 1 else [low, low + 1, high, high + 1]
+
+        def old(row, slab, cut):
+            for index, first in ((0, low - 1), (2, high + 1)):
+                if row - first in (0, 1):
+                    return strips[reach - 1, index + row - first, slab, cut]
+            for index, first in ((0, low + 1), (2, high - 1)):
+                if row - first in (0, 1):
+                    return inner[reach - 2, index + row - first, slab, cut]
+            raise ValueError(row)
+
+        def store(k, slab, value):
+            if reach == SWEEPS:
+                last[k, slab] = value
+                return
+            inner[reach - 1, k, slab, middle] = value
+            if reach == 1:
+                inner[reach - 1, 2 + k, slab, middle] = value
+
+        def extras(k, slab):
+            return source_ref[slab, at[k] - SWEEPS] if 0 <= at[k] - SWEEPS < rows else None
+
+        solver.advance(at, sums_of(solver, old, at), lambda k: old(at[k], 1, middle), extras, store)
+
+    for reach in range(1, SWEEPS + 1):
+        sweep(reach)
+    start = pl.multiple_of(OVERLAP * solver.core, 8)
+    half = width - OVERLAP
+    odd = solver.odd
+    for ref, row in ((mid_first, 2 - 2 * odd), (mid_second, 2 * odd)):
+        for k in range(2):
+            for slab in range(2):
+                ref[k, slab] = last[row + k, slab, pl.ds(start, half)]
+
+
+def core_body(rows, width, lat_count, face_ref, mine_ref, other_ref, inner, source_ref,
+              near_first, near_second, own, field, weights):
     solver = Solver(rows, width, lat_count, face_ref, mine_ref, other_ref, weights)
     middle = slice(PAD, PAD + width)
     half = width - OVERLAP
-    clear_pads(field, [(b, s, r) for b in range(2) for s in range(2) for r in range(2, field.shape[2] - 2)], width)
-    for slab, ref in solver.payloads:
-        for row in range(rows):
-            rhs_source[slab, row] = ref[(rows + row) * width : (rows + row + 1) * width]
+    clear_pads(field, [(b, s, r) for b in range(2) for s in range(2) for r in range(field.shape[2])], width)
 
     def sweep(reach):
+        low, high = SWEEPS + 3 - reach, SWEEPS + rows - 5 + reach
+
         def old(row, slab, cut):
-            low, high = SWEEPS + 1 - reach, SWEEPS + rows - 3 + reach
-            if row - low in (0, 1):
-                return strips[reach - 1, row - low, slab, cut]
-            if row - high in (0, 1):
-                return strips[reach - 1, 2 + row - high, slab, cut]
-            return field[(reach + 1) % 2, slab, row, cut]
+            for index, first in ((0, low), (2, high)):
+                if row - first in (0, 1):
+                    return inner[reach - 2, index + row - first, slab, cut]
+            return field[(reach + 1) % 2, slab, row - 4, cut]
 
         def group(at):
-            def sums(k, slab):
-                row = at[k]
-                return (old(row - 1, slab, middle) + old(row + 1, slab, middle)) + (
-                    old(row, slab, slice(PAD - 1, PAD - 1 + width)) + old(row, slab, slice(PAD + 1, PAD + 1 + width))
-                )
-
             def store(k, slab, value):
-                field[reach % 2, slab, at[k], middle] = value
+                field[reach % 2, slab, at[k] - 4, middle] = value
 
             def extras(k, slab):
-                return rhs_source[slab, at[k] - SWEEPS] if 0 <= at[k] - SWEEPS < rows else None
-
-            solver.advance(at, sums, lambda k: old(at[k], 1, middle), extras, store)
-
-        todo = list(range(SWEEPS + 2 - reach, SWEEPS + rows - 2 + reach))
+                return source_ref[slab, at[k] - SWEEPS] if 0 <= at[k] - SWEEPS < rows else None
+
+            solver.advance(at, sums_of(solver, old, at), lambda k: old(at[k], 1, middle), extras, store)
+
+        todo = list(range(low + 1, high + 1))
         for first in range(0, len(todo), GROUP):
             group(todo[first : first + GROUP])
 
-    for reach in range(1, SWEEPS + 1):
+    for reach in range(3, SWEEPS + 1):
         sweep(reach)
     start = pl.multiple_of(PAD + OVERLAP * solver.core, 8)
-    odd, reach = solver.odd, rows + SWEEPS
-    for ref, row in (
-        (own, SWEEPS),
-        (near_first, reach + (4 - reach) * odd),
-        (near_second, 4 + (reach - 4) * odd),
-        (mid_first, reach + 2 - reach * odd),
-        (mid_second, 2 + reach * odd),
-    ):
+    odd = solver.odd
+    for ref, row in ((own, 2), (near_first, 6 - 6 * odd), (near_second, 6 * odd)):
         for k in range(ref.shape[0]):
             for slab in range(2):
                 ref[k, slab] = field[SWEEPS % 2, slab, row + k, pl.ds(start, half)]
@@ -308,19 +388,29 @@
         compiler_params=pltpu.CompilerParams(vmem_limit_bytes=24 * 2**20),
         name="strips",
     )(face, mine, other)
-    mid_first, mid_second, near_first, near_second, own = pl.pallas_call(
+    mid_first, mid_second, inner, terms = pl.pallas_call(
+        functools.partial(middle_body, rows, width, lat_count),
+        out_shape=[
+            shape(2),
+            shape(2),
+            jax.ShapeDtypeStruct((SWEEPS - 1, 4, 2, width + 2 * PAD, LANES), jnp.float32),
+            jax.ShapeDtypeStruct((2, rows, width, LANES), jnp.float32),
+        ],
+        in_specs=[SMEM] + [VMEM] * 3,
+        out_specs=[VMEM] * 4,
+        scratch_shapes=[weights, pltpu.VMEM((4, 2, width, LANES), jnp.float32)],
+        compiler_params=pltpu.CompilerParams(vmem_limit_bytes=32 * 2**20),
+        name="middle",
+    )(face, mine, other, strips)
+    near_first, near_second, own = pl.pallas_call(
         functools.partial(core_body, rows, width, lat_count),
-        out_shape=[shape(k) for k in (2, 2, 2, 2, rows)],
-        in_specs=[SMEM] + [VMEM] * 3,
-        out_specs=[VMEM] * 5,
-        scratch_shapes=[
-            pltpu.VMEM((2, 2, rows + 2 * SWEEPS, width + 2 * PAD, LANES), jnp.float32),
-            pltpu.VMEM((2, rows, width, LANES), jnp.float32),
-            weights,
-        ],
+        out_shape=[shape(k) for k in (2, 2, rows)],
+        in_specs=[SMEM] + [VMEM] * 4,
+        out_specs=[VMEM] * 3,
+        scratch_shapes=[pltpu.VMEM((2, 2, rows + 4, width + 2 * PAD, LANES), jnp.float32), weights],
         compiler_params=pltpu.CompilerParams(vmem_limit_bytes=32 * 2**20),
         name="core",
-    )(face, mine, other, strips)
+    )(face, mine, other, inner, terms)
     return far_first, far_second, mid_first, mid_second, near_first, near_second, own
 
 
@@ -341,9 +431,10 @@
             handed[row] = own[row, 1 - core] + piece[k, 1 - core]
 
 
-def finish_body(kept, handed, same_first, cross_first, same_second, cross_second, out_hbm, lines, sems):
+def finish_body(crossed, base, first, second, *refs):
+    out_hbm, lines, sems = refs[-3:]
     at_core, lat = position()
-    rows, half, _ = kept.shape
+    rows, half, _ = base.shape
     tiles = half // LANES
     step = 2 * tiles * rows
     for core in range(2):
@@ -351,30 +442,47 @@
 
             @pl.when((at_core == core) & (lax.rem(lat, 2) == odd))
             def _():
+                side = 1 - core if crossed else core
                 copies = []
-                for side, base, pieces in (
-                    (core, kept, (same_first, same_second)),
-                    (1 - core, handed, (cross_first, cross_second)),
-                ):
-                    for tile in range(tiles):
-                        cut = slice(tile * LANES, (tile + 1) * LANES)
-                        place = (side * tiles + tile) * rows
-                        for row in range(rows):
-                            piece = pieces[1] if row // 2 == odd else pieces[0]
-                            value = base[row, cut] + piece[row % 2, cut]
-                            lines[pl.ds(core * step + place + row, LANES, stride=step), :] = value.T
-                        if core == 1:
-                            lines[place : place + rows] = lines[LANES * step + place : LANES * step + place + rows]
-                        copies.append(
-                            pltpu.make_async_copy(
-                                lines.reshape(LANES + 1, step, LANES).at[pl.ds(0, LANES), pl.ds(place, rows)],
-                                out_hbm.reshape(LANES, step, LANES).at[:, pl.ds(place, rows)],
-                                sems.at[side * tiles + tile],
-                            )
+                for tile in range(tiles):
+                    cut = slice(tile * LANES, (tile + 1) * LANES)
+                    for row in range(rows):
+                        piece = second if row // 2 == odd else first
+                        value = base[row, cut] + piece[row % 2, cut]
+                        line = core * tiles * rows + tile * rows + row
+                        lines[pl.ds(line, LANES, stride=tiles * rows), :] = value.T
+                    if core == 1:
+                        last = (LANES * tiles + tile) * rows
+                        lines[tile * rows : (tile + 1) * rows] = lines[last : last + rows]
+                    copies.append(
+                        pltpu.make_async_copy(
+                            lines.reshape(LANES + 1, tiles * rows, LANES).at[pl.ds(0, LANES), pl.ds(tile * rows, rows)],
+                            out_hbm.reshape(LANES, step, LANES).at[:, pl.ds((side * tiles + tile) * rows, rows)],
+                            sems.at[tile],
                         )
-                        copies[-1].start()
+                    )
+                    copies[-1].start()
                 for copy in copies:
                     copy.wait()
+
+
+def finish(base, first, second, lines, before=None):
+    _, half, _ = base.shape
+    hbm = pl.BlockSpec(memory_space=pltpu.HBM)
+    crossed = before is not None
+    return pl.pallas_call(
+        functools.partial(finish_body, crossed),
+        out_shape=jax.ShapeDtypeStruct((lines, LANES), jnp.float32),
+        in_specs=[VMEM] * 3 + [hbm] * crossed,
+        out_specs=hbm,
+        scratch_shapes=[
+            pltpu.VMEM((lines // LANES * (LANES + 1) // 2, LANES), jnp.float32),
+            pltpu.SemaphoreType.DMA((half // LANES,)),
+        ],
+        input_output_aliases={3: 0} if crossed else {},
+        compiler_params=pltpu.CompilerParams(vmem_limit_bytes=8 * 2**20),
+        name="finish_crossed" if crossed else "finish_own",
+    )(base, first, second, *([before] if crossed else []))
 
 
 def program(temp_old, source, lat_couple, face_couple, block_inverse):
@@ -420,18 +528,8 @@
     same_first, cross_first = exchange(same_first, 0), cross(cross_first, 0)
     kept, handed = call(hand_body, [piece(rows), piece(rows)], own, mid_first, mid_second)
     lines = temp_old.size // LANES
-    result = pl.pallas_call(
-        finish_body,
-        out_shape=jax.ShapeDtypeStruct((lines, LANES), jnp.float32),
-        in_specs=[VMEM] * 6,
-        out_specs=pl.BlockSpec(memory_space=pltpu.HBM),
-        scratch_shapes=[
-            pltpu.VMEM((lines // LANES * (LANES + 1), LANES), jnp.float32),
-            pltpu.SemaphoreType.DMA((columns // LANES,)),
-        ],
-        compiler_params=params,
-        name="finish",
-    )(kept, swap(handed), same_first, cross_first, same_second, cross_second)
+    result = finish(kept, same_first, same_second, lines)
+    result = finish(swap(handed), cross_first, cross_second, lines, result)
     return array_of(result, temp_old.shape)
 
 

time: 78.9 us -> 66 us (0.84)
  waiting for transfers between devices: 26.2 us -> 13.1 us
    ppermute x6, waiting for transfers between devices: 19.3 us -> 5.67 us  [program(): exchange = lambda value, group: lax.ppermute(value, 'lat', pairs[group])]
    pallas_call x1 -> x3, Pallas kernels: 1.19 us -> 4.43 us  [the longest x1 2.51 us: sweeps(): pl.pallas_call(functools.partial(middle_body, rows, width, lat_count), ou...]
    pallas_call x1, Pallas kernels: 5.65 us -> 2.6 us  [sweeps(): pl.pallas_call(functools.partial(core_body, rows, width, lat_count), out_...]
  transfers between devices with their start and end apart: 10 -> 10, of which waited for: 5 -> 5; matrix products, arithmetic and copies ran while one was open for 0% -> 0% of each run, Pallas kernels for 1% -> 7%
where the time goes in v3:
time: 66 us; the launch traced here: 65.7 us
  starting transfers between devices  39.5 us (60%)
  waiting for transfers between devices  13.1 us (20%)
  Pallas kernels  12.2 us (18%)
  between operations  0.82 us (1%)
    ppermute x6, starting transfers between devices, program(): exchange = lambda value, group: lax.ppermute(value, 'lat', pairs[group])  23.4 us
    ppermute x2, starting transfers between devices, program(): lax.ppermute(value, ('depth', 'lat'), crossed[group])  9.03 us
    ppermute x2, starting transfers between devices, program(): swap = lambda value: lax.ppermute(value, 'depth', [(0, 1), (1, 0)])  7.11 us
    ppermute x2, waiting for transfers between devices, program(): lax.ppermute(value, ('depth', 'lat'), crossed[group])  6.17 us
    ppermute x6, waiting for transfers between devices, program(): exchange = lambda value, group: lax.ppermute(value, 'lat', pairs[group])  5.67 us
    pallas_call x1, Pallas kernels, sweeps(): pl.pallas_call(functools.partial(core_body, rows, width, lat_count), out_...  2.6 us
    pallas_call x1, Pallas kernels, sweeps(): pl.pallas_call(functools.partial(middle_body, rows, width, lat_count), ou...  2.51 us
    pallas_call x1, Pallas kernels, sweeps(): pl.pallas_call(functools.partial(strips_body, rows, width, lat_count), ou...  2.48 us
  transfers between devices with their start and end apart: 10, of which 5 were waited for; matrix products, arithmetic and copies ran while one was open for 0% of the time, Pallas kernels for 7%

profile of v3, /device:TPU:257, one launch (start us, length us, event | category | flops | bytes accessed | tf_op | source)
XLA Modules:
  0.0 65.7 jit_solution(13843433611575128893)
XLA Ops:
  0.0 1.9 %pack_send.1 = (f32[2312,128]{1,0:T(8,128)S(1)}, f32[2064,128]{1,0:T(8,128)S(1)}, f32[2064,128]{1,0:T(8,128)S(1)}) custom-call(f32[2048,128]{1,0:T(8,128)} %bitcast.16, f32[2048,128]{1,0:T(8,128)} %bitcast.17, f32[128,128]{1,0:T(8,128)} %inverse_hbm.1, f32[1,128]{1,0:T(1,128)} %bitcast.18), custom_call_target="tpu_custom_call" | custom-call | tf_op jit(solution)/shard_map/pack_send/pallas_call | solution.py:137
  1.9 2.6 %collective-permute-start = (f32[2312,128]{1,0:T(8,128)S(1)}, f32[2312,128]{1,0:T(8,128)S(1)}, u32[]{:S(2)}, u32[]{:S(2)}) collective-permute-start(f32[2312,128]{1,0:T(8,128)S(1)} %get-tuple-element.26.sent_ref), channel_id=1, source_target_pairs={{0,256},{256,0},{1,257},{257,1},{2,258},{258,2},{3,259},{259,3},{4... | collective-permute-start | bytes 3551240 | tf_op jit(solution)/shard_map/ppermute | solution.py:509
  5.2 0.5 shard_map.55.mine_ref
  5.7 1.3 %collective-permute-done.other_ref = f32[2312,128]{1,0:T(8,128)S(1)} collective-permute-done((f32[2312,128]{1,0:T(8,128)S(1)}, f32[2312,128]{1,0:T(8,128)S(1)}, u32[]{:S(2)}, u32[]{:S(2)}) %collective-permute-start) | collective-permute-done | bytes 1183776 | tf_op jit(solution)/shard_map/ppermute | solution.py:509
  7.0 2.5 %strips.1 = (f32[2,2,256,128]{3,2,1,0:T(8,128)S(1)}, f32[2,2,256,128]{3,2,1,0:T(8,128)S(1)}, f32[6,4,2,288,128]{4,3,2,1,0:T(8,128)S(1)}) custom-call(f32[1]{0:T(128)S(6)} %copy.11.face_ref, f32[2312,128]{1,0:T(8,128)S(1)} %shard_map.55.mine_ref, f32[2312,128]{1,0:T(8,128)S(1)} %collective-permute-done.other_ref), custom_call_target="tpu_custom_call" | custom-call | tf_op jit(solution)/shard_map/strips/pallas_call | solution.py:378
  9.5 2.5 %middle.1 = (f32[2,2,256,128]{3,2,1,0:T(8,128)S(1)}, f32[2,2,256,128]{3,2,1,0:T(8,128)S(1)}, f32[5,4,2,288,128]{4,3,2,1,0:T(8,128)S(1)}, f32[2,4,272,128]{3,2,1,0:T(8,128)S(1)}) custom-call(f32[1]{0:T(128)S(6)} %copy.11.face_ref, f32[2312,128]{1,0:T(8,128)S(1)} %shard_map.55.mine_ref, f32[2312,128]{1,0:T(8,128)S(1)} %collective-permute-done.other_ref, ...), custom_call_target="tpu_custom_call" | custom-call | tf_op jit(solution)/shard_map/middle/pallas_call | solution.py:391
  12.0 3.1 %collective-permute-start.1 = (f32[2,2,256,128]{3,2,1,0:T(8,128)S(1)}, f32[2,2,256,128]{3,2,1,0:T(8,128)S(1)}, u32[]{:S(2)}, u32[]{:S(2)}) collective-permute-start(f32[2,2,256,128]{3,2,1,0:T(8,128)S(1)} %get-tuple-element.31), channel_id=1, source_target_pairs={{0,1},{2,3},{4,5},{6,7},{8,9},{10,11},{12,13},{14,15},{16,17},{18,... | collective-permute-start | bytes 1572872 | tf_op jit(solution)/shard_map/ppermute | solution.py:510
  15.1 5.7 %collective-permute-start.2 = (f32[2,2,256,128]{3,2,1,0:T(8,128)S(1)}, f32[2,2,256,128]{3,2,1,0:T(8,128)S(1)}, u32[]{:S(2)}, u32[]{:S(2)}) collective-permute-start(f32[2,2,256,128]{3,2,1,0:T(8,128)S(1)} %get-tuple-element.32), channel_id=1, source_target_pairs={{1,2},{3,4},{5,6},{7,8},{9,10},{11,12},{13,14},{15,16},{17,18},{19... | collective-permute-start | bytes 1572872 | tf_op jit(solution)/shard_map/ppermute | solution.py:510
  20.8 1.9 %collective-permute-start.6 = (f32[2,2,256,128]{3,2,1,0:T(8,128)S(1)}, f32[2,2,256,128]{3,2,1,0:T(8,128)S(1)}, u32[]{:S(2)}, u32[]{:S(2)}) collective-permute-start(f32[2,2,256,128]{3,2,1,0:T(8,128)S(1)} %get-tuple-element.38), channel_id=1, source_target_pairs={{0,1},{2,3},{4,5},{6,7},{8,9},{10,11},{12,13},{14,15},{16,17},{18,... | collective-permute-start | bytes 1572872 | tf_op jit(solution)/shard_map/ppermute | solution.py:510
  22.8 5.0 %collective-permute-start.4 = (f32[2,2,256,128]{3,2,1,0:T(8,128)S(1)}, f32[2,2,256,128]{3,2,1,0:T(8,128)S(1)}, u32[]{:S(2)}, u32[]{:S(2)}) collective-permute-start(f32[2,2,256,128]{3,2,1,0:T(8,128)S(1)} %get-tuple-element.35), channel_id=1, source_target_pairs={{1,2},{3,4},{5,6},{7,8},{9,10},{11,12},{13,14},{15,16},{17,18},{19... | collective-permute-start | bytes 1572872 | tf_op jit(solution)/shard_map/ppermute | solution.py:510
  27.8 2.6 %core.1 = (f32[2,2,256,128]{3,2,1,0:T(8,128)S(1)}, f32[2,2,256,128]{3,2,1,0:T(8,128)S(1)}, f32[4,2,256,128]{3,2,1,0:T(8,128)S(1)}) custom-call(f32[1]{0:T(128)S(6)} %copy.11.face_ref, f32[2312,128]{1,0:T(8,128)S(1)} %shard_map.55.mine_ref, f32[2312,128]{1,0:T(8,128)S(1)} %collective-permute-done.other_ref, ...), custom_call_target="tpu_custom_call" | custom-call | tf_op jit(solution)/shard_map/core/pallas_call | solution.py:405
  30.4 0.0 collective-permute-done.1.mid_first
  30.4 4.9 %collective-permute-done.2.mid_second = f32[2,2,256,128]{3,2,1,0:T(8,128)S(1)} collective-permute-done((f32[2,2,256,128]{3,2,1,0:T(8,128)S(1)}, f32[2,2,256,128]{3,2,1,0:T(8,128)S(1)}, u32[]{:S(2)}, u32[]{:S(2)}) %collective-permute-start.2) | collective-permute-done | bytes 524320 | tf_op jit(solution)/shard_map/ppermute | solution.py:510
  35.3 0.1 shard_map.56
  35.4 4.5 %collective-permute-start.3 = (f32[4,256,128]{2,1,0:T(8,128)S(1)}, f32[4,256,128]{2,1,0:T(8,128)S(1)}, u32[]{:S(2)}, u32[]{:S(2)}) collective-permute-start(f32[4,256,128]{2,1,0:T(8,128)S(1)} %get-tuple-element.33), channel_id=1, source_target_pairs={{0,256},{256,0},{1,257},{257,1},{2,258},{258,2},{3,259},{259,3},{4... | collective-permute-start | bytes 1572872 | tf_op jit(solution)/shard_map/ppermute | solution.py:509
  39.9 0.0 collective-permute-done.6.far
  39.9 0.1 shard_map.58
  40.0 5.7 %collective-permute-start.9 = (f32[2,256,128]{2,1,0:T(8,128)S(1)}, f32[2,256,128]{2,1,0:T(8,128)S(1)}, u32[]{:S(2)}, u32[]{:S(2)}) collective-permute-start(f32[2,256,128]{2,1,0:T(8,128)S(1)} %get-tuple-element.42), channel_id=1, source_target_pairs={{1,2},{3,4},{5,6},{7,8},{9,10},{11,12},{13,14},{15,16},{17,18},{19... | collective-permute-start | bytes 786440 | tf_op jit(solution)/shard_map/ppermute | solution.py:510
  45.7 0.8 %collective-permute-done.4.far = f32[2,2,256,128]{3,2,1,0:T(8,128)S(1)} collective-permute-done((f32[2,2,256,128]{3,2,1,0:T(8,128)S(1)}, f32[2,2,256,128]{3,2,1,0:T(8,128)S(1)}, u32[]{:S(2)}, u32[]{:S(2)}) %collective-permute-start.4) | collective-permute-done | bytes 524320 | tf_op jit(solution)/shard_map/ppermute | solution.py:510
  46.5 0.1 shard_map.57
  46.6 1.9 %collective-permute-start.8 = (f32[2,256,128]{2,1,0:T(8,128)S(1)}, f32[2,256,128]{2,1,0:T(8,128)S(1)}, u32[]{:S(2)}, u32[]{:S(2)}) collective-permute-start(f32[2,256,128]{2,1,0:T(8,128)S(1)} %get-tuple-element.41), channel_id=1, source_target_pairs={{0,1},{2,3},{4,5},{6,7},{8,9},{10,11},{12,13},{14,15},{16,17},{18,... | collective-permute-start | bytes 786440 | tf_op jit(solution)/shard_map/ppermute | solution.py:510
  48.5 7.1 %collective-permute-start.7 = (f32[2,256,128]{2,1,0:T(8,128)S(1)}, f32[2,256,128]{2,1,0:T(8,128)S(1)}, u32[]{:S(2)}, u32[]{:S(2)}) collective-permute-start(f32[2,256,128]{2,1,0:T(8,128)S(1)} %get-tuple-element.39), channel_id=1, source_target_pairs={{1,258},{3,260},{5,262},{7,264},{9,266},{11,268},{13,270},{15,272}... | collective-permute-start | bytes 786440 | tf_op jit(solution)/shard_map/ppermute | solution.py:511
  55.6 1.9 %collective-permute-start.5 = (f32[2,256,128]{2,1,0:T(8,128)S(1)}, f32[2,256,128]{2,1,0:T(8,128)S(1)}, u32[]{:S(2)}, u32[]{:S(2)}) collective-permute-start(f32[2,256,128]{2,1,0:T(8,128)S(1)} %get-tuple-element.36), channel_id=1, source_target_pairs={{0,257},{2,259},{4,261},{6,263},{8,265},{10,267},{12,269},{14,271}... | collective-permute-start | bytes 786440 | tf_op jit(solution)/shard_map/ppermute | solution.py:511
  57.5 0.0 collective-permute-done.9.second
  57.6 0.0 collective-permute-done.8.first
  57.6 1.0 %finish_own.1.refs_0_ = f32[2048,128]{1,0:T(8,128)} custom-call(f32[4,256,128]{2,1,0:T(8,128)S(1)} %get-tuple-element.40.base, f32[2,256,128]{2,1,0:T(8,128)S(1)} %collective-permute-done.8.first, f32[2,256,128]{2,1,0:T(8,128)S(1)} %collective-permute-done.9.second), custom_call_target="tpu_custom_call" | custom-call | tf_op jit(solution)/shard_map/finish_own/pallas_call | solution.py:473
  58.5 5.4 %collective-permute-done.7.second = f32[2,256,128]{2,1,0:T(8,128)S(1)} collective-permute-done((f32[2,256,128]{2,1,0:T(8,128)S(1)}, f32[2,256,128]{2,1,0:T(8,128)S(1)}, u32[]{:S(2)}, u32[]{:S(2)}) %collective-permute-start.7) | collective-permute-done | bytes 262176 | tf_op jit(solution)/shard_map/ppermute | solution.py:511
  63.9 0.8 %collective-permute-done.5.first = f32[2,256,128]{2,1,0:T(8,128)S(1)} collective-permute-done((f32[2,256,128]{2,1,0:T(8,128)S(1)}, f32[2,256,128]{2,1,0:T(8,128)S(1)}, u32[]{:S(2)}, u32[]{:S(2)}) %collective-permute-start.5) | collective-permute-done | bytes 262176 | tf_op jit(solution)/shard_map/ppermute | solution.py:511
  64.7 0.0 collective-permute-done.3.base
  64.7 0.9 %finish_crossed.1 = f32[2048,128]{1,0:T(8,128)} custom-call(f32[4,256,128]{2,1,0:T(8,128)S(1)} %collective-permute-done.3.base, f32[2,256,128]{2,1,0:T(8,128)S(1)} %collective-permute-done.5.first, f32[2,256,128]{2,1,0:T(8,128)S(1)} %collective-permute-done.7.second, f32[2048,128]{1,0:T(8,128)} %finish_own.1.refs_0_), custom_call_target="tpu_custom_call", output_to_operand_aliasing={{}: (3, {})} | custom-call | tf_op jit(solution)/shard_map/finish_crossed/pallas_call | solution.py:473
Async XLA Ops:
  1.9 5.0 %collective-permute-start = (f32[2312,128]{1,0:T(8,128)S(1)}, f32[2312,128]{1,0:T(8,128)S(1)}, u32[]{:S(2)}, u32[]{:S(2)}) collective-permute-start(f32[2312,128]{1,0:T(8,128)S(1)} %get-tuple-element.26.sent_ref), channel_id=1, source_target_pairs={{0,256},{256,0},{1,257},{257,1},{2,258},{258,2},{3,259},{259,3},{4... | collective-permute-start | bytes 3551240 | tf_op jit(solution)/shard_map/ppermute | solution.py:509
  12.0 18.4 %collective-permute-start.1 = (f32[2,2,256,128]{3,2,1,0:T(8,128)S(1)}, f32[2,2,256,128]{3,2,1,0:T(8,128)S(1)}, u32[]{:S(2)}, u32[]{:S(2)}) collective-permute-start(f32[2,2,256,128]{3,2,1,0:T(8,128)S(1)} %get-tuple-element.31), channel_id=1, source_target_pairs={{0,1},{2,3},{4,5},{6,7},{8,9},{10,11},{12,13},{14,15},{16,17},{18,... | collective-permute-start | bytes 1572872 | tf_op jit(solution)/shard_map/ppermute | solution.py:510
  15.1 20.2 %collective-permute-start.2 = (f32[2,2,256,128]{3,2,1,0:T(8,128)S(1)}, f32[2,2,256,128]{3,2,1,0:T(8,128)S(1)}, u32[]{:S(2)}, u32[]{:S(2)}) collective-permute-start(f32[2,2,256,128]{3,2,1,0:T(8,128)S(1)} %get-tuple-element.32), channel_id=1, source_target_pairs={{1,2},{3,4},{5,6},{7,8},{9,10},{11,12},{13,14},{15,16},{17,18},{19... | collective-permute-start | bytes 1572872 | tf_op jit(solution)/shard_map/ppermute | solution.py:510
  20.8 19.1 %collective-permute-start.6 = (f32[2,2,256,128]{3,2,1,0:T(8,128)S(1)}, f32[2,2,256,128]{3,2,1,0:T(8,128)S(1)}, u32[]{:S(2)}, u32[]{:S(2)}) collective-permute-start(f32[2,2,256,128]{3,2,1,0:T(8,128)S(1)} %get-tuple-element.38), channel_id=1, source_target_pairs={{0,1},{2,3},{4,5},{6,7},{8,9},{10,11},{12,13},{14,15},{16,17},{18,... | collective-permute-start | bytes 1572872 | tf_op jit(solution)/shard_map/ppermute | solution.py:510
  22.8 23.7 %collective-permute-start.4 = (f32[2,2,256,128]{3,2,1,0:T(8,128)S(1)}, f32[2,2,256,128]{3,2,1,0:T(8,128)S(1)}, u32[]{:S(2)}, u32[]{:S(2)}) collective-permute-start(f32[2,2,256,128]{3,2,1,0:T(8,128)S(1)} %get-tuple-element.35), channel_id=1, source_target_pairs={{1,2},{3,4},{5,6},{7,8},{9,10},{11,12},{13,14},{15,16},{17,18},{19... | collective-permute-start | bytes 1572872 | tf_op jit(solution)/shard_map/ppermute | solution.py:510
  35.4 29.3 %collective-permute-start.3 = (f32[4,256,128]{2,1,0:T(8,128)S(1)}, f32[4,256,128]{2,1,0:T(8,128)S(1)}, u32[]{:S(2)}, u32[]{:S(2)}) collective-permute-start(f32[4,256,128]{2,1,0:T(8,128)S(1)} %get-tuple-element.33), channel_id=1, source_target_pairs={{0,256},{256,0},{1,257},{257,1},{2,258},{258,2},{3,259},{259,3},{4... | collective-permute-start | bytes 1572872 | tf_op jit(solution)/shard_map/ppermute | solution.py:509
  40.0 17.5 %collective-permute-start.9 = (f32[2,256,128]{2,1,0:T(8,128)S(1)}, f32[2,256,128]{2,1,0:T(8,128)S(1)}, u32[]{:S(2)}, u32[]{:S(2)}) collective-permute-start(f32[2,256,128]{2,1,0:T(8,128)S(1)} %get-tuple-element.42), channel_id=1, source_target_pairs={{1,2},{3,4},{5,6},{7,8},{9,10},{11,12},{13,14},{15,16},{17,18},{19... | collective-permute-start | bytes 786440 | tf_op jit(solution)/shard_map/ppermute | solution.py:510
  46.6 11.0 %collective-permute-start.8 = (f32[2,256,128]{2,1,0:T(8,128)S(1)}, f32[2,256,128]{2,1,0:T(8,128)S(1)}, u32[]{:S(2)}, u32[]{:S(2)}) collective-permute-start(f32[2,256,128]{2,1,0:T(8,128)S(1)} %get-tuple-element.41), channel_id=1, source_target_pairs={{0,1},{2,3},{4,5},{6,7},{8,9},{10,11},{12,13},{14,15},{16,17},{18,... | collective-permute-start | bytes 786440 | tf_op jit(solution)/shard_map/ppermute | solution.py:510
  48.5 15.4 %collective-permute-start.7 = (f32[2,256,128]{2,1,0:T(8,128)S(1)}, f32[2,256,128]{2,1,0:T(8,128)S(1)}, u32[]{:S(2)}, u32[]{:S(2)}) collective-permute-start(f32[2,256,128]{2,1,0:T(8,128)S(1)} %get-tuple-element.39), channel_id=1, source_target_pairs={{1,258},{3,260},{5,262},{7,264},{9,266},{11,268},{13,270},{15,272}... | collective-permute-start | bytes 786440 | tf_op jit(solution)/shard_map/ppermute | solution.py:511
  55.6 9.1 %collective-permute-start.5 = (f32[2,256,128]{2,1,0:T(8,128)S(1)}, f32[2,256,128]{2,1,0:T(8,128)S(1)}, u32[]{:S(2)}, u32[]{:S(2)}) collective-permute-start(f32[2,256,128]{2,1,0:T(8,128)S(1)} %get-tuple-element.36), channel_id=1, source_target_pairs={{0,257},{2,259},{4,261},{6,263},{8,265},{10,267},{12,269},{14,271}... | collective-permute-start | bytes 786440 | tf_op jit(solution)/shard_map/ppermute | solution.py:511

commit v4 on v3

--- a/solution.py
+++ b/solution.py
@@ -12,6 +12,7 @@
 OVERLAP = 16
 PAD = 8
 GROUP = 4
+FINISH = ((True,), (False,))
 VMEM = pl.BlockSpec(memory_space=pltpu.VMEM)
 SMEM = pl.BlockSpec(memory_space=pltpu.SMEM)
 
@@ -255,10 +256,15 @@
             else:
                 last[k, slab] = value
 
-        solver.advance(
-            [SWEEPS - reach, SWEEPS + 1 - reach, SWEEPS + top - 1 + reach, SWEEPS + top + reach],
-            sums, unders, extras, store,
-        )
+        at = [SWEEPS - reach, SWEEPS + 1 - reach, SWEEPS + top - 1 + reach, SWEEPS + top + reach]
+        for group in [(0,), (3,), (1,), (2,)]:
+            solver.advance(
+                [at[k] for k in group],
+                lambda k, slab, group=group: sums(group[k], slab),
+                lambda k, group=group: unders(group[k]),
+                lambda k, slab, group=group: extras(group[k], slab),
+                lambda k, slab, value, group=group: store(group[k], slab, value),
+            )
     start = pl.multiple_of(OVERLAP * solver.core, 8)
     half = width - OVERLAP
     odd = solver.odd
@@ -431,7 +437,8 @@
             handed[row] = own[row, 1 - core] + piece[k, 1 - core]
 
 
-def finish_body(crossed, base, first, second, *refs):
+def finish_body(crossed, parts, base, *refs):
+    pieces = dict(zip(parts, refs))
     out_hbm, lines, sems = refs[-3:]
     at_core, lat = position()
     rows, half, _ = base.shape
@@ -446,18 +453,19 @@
                 copies = []
                 for tile in range(tiles):
                     cut = slice(tile * LANES, (tile + 1) * LANES)
-                    for row in range(rows):
-                        piece = second if row // 2 == odd else first
-                        value = base[row, cut] + piece[row % 2, cut]
+                    todo = [row for row in range(rows) if (row // 2 == odd) in parts]
+                    for row in todo:
+                        value = base[row, cut] + pieces[row // 2 == odd][row % 2, cut]
                         line = core * tiles * rows + tile * rows + row
                         lines[pl.ds(line, LANES, stride=tiles * rows), :] = value.T
+                    at, count = tile * rows + todo[0], len(todo)
                     if core == 1:
-                        last = (LANES * tiles + tile) * rows
-                        lines[tile * rows : (tile + 1) * rows] = lines[last : last + rows]
+                        last = LANES * tiles * rows + at
+                        lines[at : at + count] = lines[last : last + count]
                     copies.append(
                         pltpu.make_async_copy(
-                            lines.reshape(LANES + 1, tiles * rows, LANES).at[pl.ds(0, LANES), pl.ds(tile * rows, rows)],
-                            out_hbm.reshape(LANES, step, LANES).at[:, pl.ds((side * tiles + tile) * rows, rows)],
+                            lines.reshape(LANES + 1, tiles * rows, LANES).at[pl.ds(0, LANES), pl.ds(at, count)],
+                            out_hbm.reshape(LANES, step, LANES).at[:, pl.ds(side * tiles * rows + at, count)],
                             sems.at[tile],
                         )
                     )
@@ -466,23 +474,22 @@
                     copy.wait()
 
 
-def finish(base, first, second, lines, before=None):
+def finish(base, pieces, lines, before=None):
     _, half, _ = base.shape
     hbm = pl.BlockSpec(memory_space=pltpu.HBM)
     crossed = before is not None
     return pl.pallas_call(
-        functools.partial(finish_body, crossed),
+        functools.partial(finish_body, crossed, tuple(pieces)),
         out_shape=jax.ShapeDtypeStruct((lines, LANES), jnp.float32),
-        in_specs=[VMEM] * 3 + [hbm] * crossed,
+        in_specs=[VMEM] * (1 + len(pieces)) + [hbm] * crossed,
         out_specs=hbm,
         scratch_shapes=[
             pltpu.VMEM((lines // LANES * (LANES + 1) // 2, LANES), jnp.float32),
             pltpu.SemaphoreType.DMA((half // LANES,)),
         ],
-        input_output_aliases={3: 0} if crossed else {},
+        input_output_aliases={1 + len(pieces): 0} if crossed else {},
         compiler_params=pltpu.CompilerParams(vmem_limit_bytes=8 * 2**20),
-        name="finish_crossed" if crossed else "finish_own",
-    )(base, first, second, *([before] if crossed else []))
+    )(base, *pieces.values(), *([before] if crossed else []))
 
 
 def program(temp_old, source, lat_couple, face_couple, block_inverse):
@@ -528,8 +535,11 @@
     same_first, cross_first = exchange(same_first, 0), cross(cross_first, 0)
     kept, handed = call(hand_body, [piece(rows), piece(rows)], own, mid_first, mid_second)
     lines = temp_old.size // LANES
-    result = finish(kept, same_first, same_second, lines)
-    result = finish(swap(handed), cross_first, cross_second, lines, result)
+    result = finish(kept, {False: same_first, True: same_second}, lines)
+    handed = swap(handed)
+    for pieces in FINISH:
+        crossed = {False: cross_first, True: cross_second}
+        result = finish(handed, {part: crossed[part] for part in pieces}, lines, result)
     return array_of(result, temp_old.shape)
 
 

time: 66 us -> 66.3 us (level)
  waiting for transfers between devices: 13.1 us -> 12.3 us
    ppermute x2, waiting for transfers between devices: 6.17 us -> 5.34 us  [program(): lax.ppermute(value, ('depth', 'lat'), crossed[group])]
    pallas_call x2 -> x3, Pallas kernels: 1.92 us -> 2.65 us  [finish(): pl.pallas_call(functools.partial(finish_body, crossed, tuple(pieces)), ou...]
  transfers between devices with their start and end apart: 10 -> 10, of which waited for: 5 -> 4; matrix products, arithmetic and copies ran while one was open for 0% -> 0% of each run, Pallas kernels for 7% -> 8%
where the time goes in v4:
time: 66.3 us; the launch traced here: 65.4 us
  starting transfers between devices  39.6 us (60%)
  Pallas kernels  12.7 us (19%)
  waiting for transfers between devices  12.3 us (19%)
  between operations  0.84 us (1%)
    ppermute x6, starting transfers between devices, program(): exchange = lambda value, group: lax.ppermute(value, 'lat', pairs[group])  23.4 us
    ppermute x2, starting transfers between devices, program(): lax.ppermute(value, ('depth', 'lat'), crossed[group])  9.04 us
    ppermute x2, starting transfers between devices, program(): swap = lambda value: lax.ppermute(value, 'depth', [(0, 1), (1, 0)])  7.12 us
    ppermute x6, waiting for transfers between devices, program(): exchange = lambda value, group: lax.ppermute(value, 'lat', pairs[group])  5.65 us
    ppermute x2, waiting for transfers between devices, program(): lax.ppermute(value, ('depth', 'lat'), crossed[group])  5.34 us
    pallas_call x3, Pallas kernels, finish(): pl.pallas_call(functools.partial(finish_body, crossed, tuple(pieces)), ou...  2.65 us
    pallas_call x1, Pallas kernels, sweeps(): pl.pallas_call(functools.partial(core_body, rows, width, lat_count), out_...  2.6 us
    pallas_call x1, Pallas kernels, sweeps(): pl.pallas_call(functools.partial(middle_body, rows, width, lat_count), ou...  2.51 us
  transfers between devices with their start and end apart: 10, of which 4 were waited for; matrix products, arithmetic and copies ran while one was open for 0% of the time, Pallas kernels for 8%

profile of v4, /device:TPU:257, one launch (start us, length us, event | category | flops | bytes accessed | tf_op | source)
XLA Modules:
  0.0 65.4 jit_solution(10880655700214370451)
XLA Ops:
  0.0 1.9 %pack_send.1 = (f32[2312,128]{1,0:T(8,128)S(1)}, f32[2064,128]{1,0:T(8,128)S(1)}, f32[2064,128]{1,0:T(8,128)S(1)}) custom-call(f32[2048,128]{1,0:T(8,128)} %bitcast.16, f32[2048,128]{1,0:T(8,128)} %bitcast.17, f32[128,128]{1,0:T(8,128)} %inverse_hbm.1, f32[1,128]{1,0:T(1,128)} %bitcast.18), custom_call_target="tpu_custom_call" | custom-call | tf_op jit(solution)/shard_map/pack_send/pallas_call | solution.py:138
  1.9 2.6 %collective-permute-start = (f32[2312,128]{1,0:T(8,128)S(1)}, f32[2312,128]{1,0:T(8,128)S(1)}, u32[]{:S(2)}, u32[]{:S(2)}) collective-permute-start(f32[2312,128]{1,0:T(8,128)S(1)} %get-tuple-element.26.sent_ref), channel_id=1, source_target_pairs={{0,256},{256,0},{1,257},{257,1},{2,258},{258,2},{3,259},{259,3},{4... | collective-permute-start | bytes 3551240 | tf_op jit(solution)/shard_map/ppermute | solution.py:516
  5.2 0.5 shard_map.55.mine_ref
  5.7 1.3 %collective-permute-done.other_ref = f32[2312,128]{1,0:T(8,128)S(1)} collective-permute-done((f32[2312,128]{1,0:T(8,128)S(1)}, f32[2312,128]{1,0:T(8,128)S(1)}, u32[]{:S(2)}, u32[]{:S(2)}) %collective-permute-start) | collective-permute-done | bytes 1183776 | tf_op jit(solution)/shard_map/ppermute | solution.py:516
  7.0 2.3 %strips.1 = (f32[2,2,256,128]{3,2,1,0:T(8,128)S(1)}, f32[2,2,256,128]{3,2,1,0:T(8,128)S(1)}, f32[6,4,2,288,128]{4,3,2,1,0:T(8,128)S(1)}) custom-call(f32[1]{0:T(128)S(6)} %copy.13.face_ref, f32[2312,128]{1,0:T(8,128)S(1)} %shard_map.55.mine_ref, f32[2312,128]{1,0:T(8,128)S(1)} %collective-permute-done.other_ref), custom_call_target="tpu_custom_call" | custom-call | tf_op jit(solution)/shard_map/strips/pallas_call | solution.py:384
  9.3 2.5 %middle.1 = (f32[2,2,256,128]{3,2,1,0:T(8,128)S(1)}, f32[2,2,256,128]{3,2,1,0:T(8,128)S(1)}, f32[5,4,2,288,128]{4,3,2,1,0:T(8,128)S(1)}, f32[2,4,272,128]{3,2,1,0:T(8,128)S(1)}) custom-call(f32[1]{0:T(128)S(6)} %copy.13.face_ref, f32[2312,128]{1,0:T(8,128)S(1)} %shard_map.55.mine_ref, f32[2312,128]{1,0:T(8,128)S(1)} %collective-permute-done.other_ref, ...), custom_call_target="tpu_custom_call" | custom-call | tf_op jit(solution)/shard_map/middle/pallas_call | solution.py:397
  11.8 3.1 %collective-permute-start.1 = (f32[2,2,256,128]{3,2,1,0:T(8,128)S(1)}, f32[2,2,256,128]{3,2,1,0:T(8,128)S(1)}, u32[]{:S(2)}, u32[]{:S(2)}) collective-permute-start(f32[2,2,256,128]{3,2,1,0:T(8,128)S(1)} %get-tuple-element.31), channel_id=1, source_target_pairs={{0,1},{2,3},{4,5},{6,7},{8,9},{10,11},{12,13},{14,15},{16,17},{18,... | collective-permute-start | bytes 1572872 | tf_op jit(solution)/shard_map/ppermute | solution.py:517
  14.9 5.7 %collective-permute-start.2 = (f32[2,2,256,128]{3,2,1,0:T(8,128)S(1)}, f32[2,2,256,128]{3,2,1,0:T(8,128)S(1)}, u32[]{:S(2)}, u32[]{:S(2)}) collective-permute-start(f32[2,2,256,128]{3,2,1,0:T(8,128)S(1)} %get-tuple-element.32), channel_id=1, source_target_pairs={{1,2},{3,4},{5,6},{7,8},{9,10},{11,12},{13,14},{15,16},{17,18},{19... | collective-permute-start | bytes 1572872 | tf_op jit(solution)/shard_map/ppermute | solution.py:517
  20.7 1.9 %collective-permute-start.6 = (f32[2,2,256,128]{3,2,1,0:T(8,128)S(1)}, f32[2,2,256,128]{3,2,1,0:T(8,128)S(1)}, u32[]{:S(2)}, u32[]{:S(2)}) collective-permute-start(f32[2,2,256,128]{3,2,1,0:T(8,128)S(1)} %get-tuple-element.38), channel_id=1, source_target_pairs={{0,1},{2,3},{4,5},{6,7},{8,9},{10,11},{12,13},{14,15},{16,17},{18,... | collective-permute-start | bytes 1572872 | tf_op jit(solution)/shard_map/ppermute | solution.py:517
  22.6 5.0 %collective-permute-start.4 = (f32[2,2,256,128]{3,2,1,0:T(8,128)S(1)}, f32[2,2,256,128]{3,2,1,0:T(8,128)S(1)}, u32[]{:S(2)}, u32[]{:S(2)}) collective-permute-start(f32[2,2,256,128]{3,2,1,0:T(8,128)S(1)} %get-tuple-element.35), channel_id=1, source_target_pairs={{1,2},{3,4},{5,6},{7,8},{9,10},{11,12},{13,14},{15,16},{17,18},{19... | collective-permute-start | bytes 1572872 | tf_op jit(solution)/shard_map/ppermute | solution.py:517
  27.6 2.6 %core.1 = (f32[2,2,256,128]{3,2,1,0:T(8,128)S(1)}, f32[2,2,256,128]{3,2,1,0:T(8,128)S(1)}, f32[4,2,256,128]{3,2,1,0:T(8,128)S(1)}) custom-call(f32[1]{0:T(128)S(6)} %copy.13.face_ref, f32[2312,128]{1,0:T(8,128)S(1)} %shard_map.55.mine_ref, f32[2312,128]{1,0:T(8,128)S(1)} %collective-permute-done.other_ref, ...), custom_call_target="tpu_custom_call" | custom-call | tf_op jit(solution)/shard_map/core/pallas_call | solution.py:411
  30.2 0.0 collective-permute-done.1.mid_first
  30.2 4.9 %collective-permute-done.2.mid_second = f32[2,2,256,128]{3,2,1,0:T(8,128)S(1)} collective-permute-done((f32[2,2,256,128]{3,2,1,0:T(8,128)S(1)}, f32[2,2,256,128]{3,2,1,0:T(8,128)S(1)}, u32[]{:S(2)}, u32[]{:S(2)}) %collective-permute-start.2) | collective-permute-done | bytes 524320 | tf_op jit(solution)/shard_map/ppermute | solution.py:517
  35.1 0.1 shard_map.56
  35.2 4.5 %collective-permute-start.3 = (f32[4,256,128]{2,1,0:T(8,128)S(1)}, f32[4,256,128]{2,1,0:T(8,128)S(1)}, u32[]{:S(2)}, u32[]{:S(2)}) collective-permute-start(f32[4,256,128]{2,1,0:T(8,128)S(1)} %get-tuple-element.33), channel_id=1, source_target_pairs={{0,256},{256,0},{1,257},{257,1},{2,258},{258,2},{3,259},{259,3},{4... | collective-permute-start | bytes 1572872 | tf_op jit(solution)/shard_map/ppermute | solution.py:516
  39.7 0.0 collective-permute-done.6.far
  39.7 0.1 shard_map.58
  39.8 5.7 %collective-permute-start.9 = (f32[2,256,128]{2,1,0:T(8,128)S(1)}, f32[2,256,128]{2,1,0:T(8,128)S(1)}, u32[]{:S(2)}, u32[]{:S(2)}) collective-permute-start(f32[2,256,128]{2,1,0:T(8,128)S(1)} %get-tuple-element.42), channel_id=1, source_target_pairs={{1,2},{3,4},{5,6},{7,8},{9,10},{11,12},{13,14},{15,16},{17,18},{19... | collective-permute-start | bytes 786440 | tf_op jit(solution)/shard_map/ppermute | solution.py:517
  45.5 0.8 %collective-permute-done.4.far = f32[2,2,256,128]{3,2,1,0:T(8,128)S(1)} collective-permute-done((f32[2,2,256,128]{3,2,1,0:T(8,128)S(1)}, f32[2,2,256,128]{3,2,1,0:T(8,128)S(1)}, u32[]{:S(2)}, u32[]{:S(2)}) %collective-permute-start.4) | collective-permute-done | bytes 524320 | tf_op jit(solution)/shard_map/ppermute | solution.py:517
  46.3 0.1 shard_map.57
  46.4 1.9 %collective-permute-start.8 = (f32[2,256,128]{2,1,0:T(8,128)S(1)}, f32[2,256,128]{2,1,0:T(8,128)S(1)}, u32[]{:S(2)}, u32[]{:S(2)}) collective-permute-start(f32[2,256,128]{2,1,0:T(8,128)S(1)} %get-tuple-element.41), channel_id=1, source_target_pairs={{0,1},{2,3},{4,5},{6,7},{8,9},{10,11},{12,13},{14,15},{16,17},{18,... | collective-permute-start | bytes 786440 | tf_op jit(solution)/shard_map/ppermute | solution.py:517
  48.3 7.1 %collective-permute-start.7 = (f32[2,256,128]{2,1,0:T(8,128)S(1)}, f32[2,256,128]{2,1,0:T(8,128)S(1)}, u32[]{:S(2)}, u32[]{:S(2)}) collective-permute-start(f32[2,256,128]{2,1,0:T(8,128)S(1)} %get-tuple-element.39), channel_id=1, source_target_pairs={{1,258},{3,260},{5,262},{7,264},{9,266},{11,268},{13,270},{15,272}... | collective-permute-start | bytes 786440 | tf_op jit(solution)/shard_map/ppermute | solution.py:518
  55.4 1.9 %collective-permute-start.5 = (f32[2,256,128]{2,1,0:T(8,128)S(1)}, f32[2,256,128]{2,1,0:T(8,128)S(1)}, u32[]{:S(2)}, u32[]{:S(2)}) collective-permute-start(f32[2,256,128]{2,1,0:T(8,128)S(1)} %get-tuple-element.36), channel_id=1, source_target_pairs={{0,257},{2,259},{4,261},{6,263},{8,265},{10,267},{12,269},{14,271}... | collective-permute-start | bytes 786440 | tf_op jit(solution)/shard_map/ppermute | solution.py:518
  57.4 0.0 collective-permute-done.9.refs_1_
  57.4 0.0 collective-permute-done.8.refs_0_
  57.4 1.0 %shard_map.59.refs_1_ = f32[2048,128]{1,0:T(8,128)} custom-call(f32[4,256,128]{2,1,0:T(8,128)S(1)} %get-tuple-element.40.base, f32[2,256,128]{2,1,0:T(8,128)S(1)} %collective-permute-done.8.refs_0_, f32[2,256,128]{2,1,0:T(8,128)S(1)} %collective-permute-done.9.refs_1_), custom_call_target="tpu_custom_call" | custom-call | tf_op jit(solution)/shard_map/pallas_call | solution.py:481
  58.4 5.3 %collective-permute-done.7.refs_0_ = f32[2,256,128]{2,1,0:T(8,128)S(1)} collective-permute-done((f32[2,256,128]{2,1,0:T(8,128)S(1)}, f32[2,256,128]{2,1,0:T(8,128)S(1)}, u32[]{:S(2)}, u32[]{:S(2)}) %collective-permute-start.7) | collective-permute-done | bytes 262176 | tf_op jit(solution)/shard_map/ppermute | solution.py:518
  63.7 0.0 collective-permute-done.3.base
  63.7 0.8 %shard_map.60.refs_1_ = f32[2048,128]{1,0:T(8,128)} custom-call(f32[4,256,128]{2,1,0:T(8,128)S(1)} %collective-permute-done.3.base, f32[2,256,128]{2,1,0:T(8,128)S(1)} %collective-permute-done.7.refs_0_, f32[2048,128]{1,0:T(8,128)} %shard_map.59.refs_1_), custom_call_target="tpu_custom_call", output_to_operand_aliasing={{}: (2, {})} | custom-call | tf_op jit(solution)/shard_map/pallas_call | solution.py:481
  64.5 0.0 collective-permute-done.5.refs_0_
  64.5 0.9 %shard_map.61 = f32[2048,128]{1,0:T(8,128)} custom-call(f32[4,256,128]{2,1,0:T(8,128)S(1)} %collective-permute-done.3.base, f32[2,256,128]{2,1,0:T(8,128)S(1)} %collective-permute-done.5.refs_0_, f32[2048,128]{1,0:T(8,128)} %shard_map.60.refs_1_), custom_call_target="tpu_custom_call", output_to_operand_aliasing={{}: (2, {})} | custom-call | tf_op jit(solution)/shard_map/pallas_call | solution.py:481
Async XLA Ops:
  1.9 5.0 %collective-permute-start = (f32[2312,128]{1,0:T(8,128)S(1)}, f32[2312,128]{1,0:T(8,128)S(1)}, u32[]{:S(2)}, u32[]{:S(2)}) collective-permute-start(f32[2312,128]{1,0:T(8,128)S(1)} %get-tuple-element.26.sent_ref), channel_id=1, source_target_pairs={{0,256},{256,0},{1,257},{257,1},{2,258},{258,2},{3,259},{259,3},{4... | collective-permute-start | bytes 3551240 | tf_op jit(solution)/shard_map/ppermute | solution.py:516
  11.8 18.4 %collective-permute-start.1 = (f32[2,2,256,128]{3,2,1,0:T(8,128)S(1)}, f32[2,2,256,128]{3,2,1,0:T(8,128)S(1)}, u32[]{:S(2)}, u32[]{:S(2)}) collective-permute-start(f32[2,2,256,128]{3,2,1,0:T(8,128)S(1)} %get-tuple-element.31), channel_id=1, source_target_pairs={{0,1},{2,3},{4,5},{6,7},{8,9},{10,11},{12,13},{14,15},{16,17},{18,... | collective-permute-start | bytes 1572872 | tf_op jit(solution)/shard_map/ppermute | solution.py:517
  14.9 20.1 %collective-permute-start.2 = (f32[2,2,256,128]{3,2,1,0:T(8,128)S(1)}, f32[2,2,256,128]{3,2,1,0:T(8,128)S(1)}, u32[]{:S(2)}, u32[]{:S(2)}) collective-permute-start(f32[2,2,256,128]{3,2,1,0:T(8,128)S(1)} %get-tuple-element.32), channel_id=1, source_target_pairs={{1,2},{3,4},{5,6},{7,8},{9,10},{11,12},{13,14},{15,16},{17,18},{19... | collective-permute-start | bytes 1572872 | tf_op jit(solution)/shard_map/ppermute | solution.py:517
  20.7 19.1 %collective-permute-start.6 = (f32[2,2,256,128]{3,2,1,0:T(8,128)S(1)}, f32[2,2,256,128]{3,2,1,0:T(8,128)S(1)}, u32[]{:S(2)}, u32[]{:S(2)}) collective-permute-start(f32[2,2,256,128]{3,2,1,0:T(8,128)S(1)} %get-tuple-element.38), channel_id=1, source_target_pairs={{0,1},{2,3},{4,5},{6,7},{8,9},{10,11},{12,13},{14,15},{16,17},{18,... | collective-permute-start | bytes 1572872 | tf_op jit(solution)/shard_map/ppermute | solution.py:517
  22.6 23.7 %collective-permute-start.4 = (f32[2,2,256,128]{3,2,1,0:T(8,128)S(1)}, f32[2,2,256,128]{3,2,1,0:T(8,128)S(1)}, u32[]{:S(2)}, u32[]{:S(2)}) collective-permute-start(f32[2,2,256,128]{3,2,1,0:T(8,128)S(1)} %get-tuple-element.35), channel_id=1, source_target_pairs={{1,2},{3,4},{5,6},{7,8},{9,10},{11,12},{13,14},{15,16},{17,18},{19... | collective-permute-start | bytes 1572872 | tf_op jit(solution)/shard_map/ppermute | solution.py:517
  35.2 28.5 %collective-permute-start.3 = (f32[4,256,128]{2,1,0:T(8,128)S(1)}, f32[4,256,128]{2,1,0:T(8,128)S(1)}, u32[]{:S(2)}, u32[]{:S(2)}) collective-permute-start(f32[4,256,128]{2,1,0:T(8,128)S(1)} %get-tuple-element.33), channel_id=1, source_target_pairs={{0,256},{256,0},{1,257},{257,1},{2,258},{258,2},{3,259},{259,3},{4... | collective-permute-start | bytes 1572872 | tf_op jit(solution)/shard_map/ppermute | solution.py:516
  39.8 17.5 %collective-permute-start.9 = (f32[2,256,128]{2,1,0:T(8,128)S(1)}, f32[2,256,128]{2,1,0:T(8,128)S(1)}, u32[]{:S(2)}, u32[]{:S(2)}) collective-permute-start(f32[2,256,128]{2,1,0:T(8,128)S(1)} %get-tuple-element.42), channel_id=1, source_target_pairs={{1,2},{3,4},{5,6},{7,8},{9,10},{11,12},{13,14},{15,16},{17,18},{19... | collective-permute-start | bytes 786440 | tf_op jit(solution)/shard_map/ppermute | solution.py:517
  46.4 11.0 %collective-permute-start.8 = (f32[2,256,128]{2,1,0:T(8,128)S(1)}, f32[2,256,128]{2,1,0:T(8,128)S(1)}, u32[]{:S(2)}, u32[]{:S(2)}) collective-permute-start(f32[2,256,128]{2,1,0:T(8,128)S(1)} %get-tuple-element.41), channel_id=1, source_target_pairs={{0,1},{2,3},{4,5},{6,7},{8,9},{10,11},{12,13},{14,15},{16,17},{18,... | collective-permute-start | bytes 786440 | tf_op jit(solution)/shard_map/ppermute | solution.py:517
  48.3 15.4 %collective-permute-start.7 = (f32[2,256,128]{2,1,0:T(8,128)S(1)}, f32[2,256,128]{2,1,0:T(8,128)S(1)}, u32[]{:S(2)}, u32[]{:S(2)}) collective-permute-start(f32[2,256,128]{2,1,0:T(8,128)S(1)} %get-tuple-element.39), channel_id=1, source_target_pairs={{1,258},{3,260},{5,262},{7,264},{9,266},{11,268},{13,270},{15,272}... | collective-permute-start | bytes 786440 | tf_op jit(solution)/shard_map/ppermute | solution.py:518
  55.4 9.1 %collective-permute-start.5 = (f32[2,256,128]{2,1,0:T(8,128)S(1)}, f32[2,256,128]{2,1,0:T(8,128)S(1)}, u32[]{:S(2)}, u32[]{:S(2)}) collective-permute-start(f32[2,256,128]{2,1,0:T(8,128)S(1)} %get-tuple-element.36), channel_id=1, source_target_pairs={{0,257},{2,259},{4,261},{6,263},{8,265},{10,267},{12,269},{14,271}... | collective-permute-start | bytes 786440 | tf_op jit(solution)/shard_map/ppermute | solution.py:518

commit v5 on v4

--- a/solution.py
+++ b/solution.py
@@ -52,6 +52,19 @@
         out_ref[base : base + count, :] = block if scale is None else block * scale
 
 
+def tile_copy(rows, hbm, ref, tile, sem):
+    target = ref.reshape(LANES + 1, ref.shape[0] // (LANES + 1), LANES)
+    cut = pl.ds(tile * rows, rows)
+    return pltpu.make_async_copy(
+        hbm.reshape(LANES, hbm.shape[0] // LANES, LANES).at[:, cut], target.at[pl.ds(0, LANES), cut], sem
+    )
+
+
+def repeat_first(rows, ref, tile):
+    last = ref.shape[0] - ref.shape[0] // (LANES + 1) + tile * rows
+    ref[last : last + rows] = ref[tile * rows : (tile + 1) * rows]
+
+
 def pack_send_body(rows, temp_hbm, source_hbm, inverse_hbm, couple_hbm,
                    out_ref, temp_ref, source_ref, inverse_ref, couple_ref, sems):
     at_core, _ = position()
@@ -59,20 +72,13 @@
     tiles = step // rows
     arrays = ((temp_hbm, temp_ref), (source_hbm, source_ref))
 
-    def tile_copy(array, tile):
-        hbm, ref = arrays[array]
-        cut = pl.ds(tile * rows, rows)
-        return pltpu.make_async_copy(
-            hbm.reshape(LANES, step, LANES).at[:, cut],
-            ref.reshape(LANES + 1, step, LANES).at[pl.ds(0, LANES), cut],
-            sems.at[array * tiles + tile],
-        )
+    def array_copy(array, tile):
+        return tile_copy(rows, *arrays[array], tile, sems.at[array * tiles + tile])
 
     inverse_copy = pltpu.make_async_copy(inverse_hbm, inverse_ref, sems.at[2 * tiles])
     couple_copy = pltpu.make_async_copy(couple_hbm, couple_ref, sems.at[2 * tiles + 1])
     for slab in range(2):
         pieces = window_pieces(rows, step, slab == 0)
-        unused = [tile for tile in range(tiles) if tile not in [piece[0] for piece in pieces]]
         turned = (lambda value: pltpu.roll(value, LANES - 1, 1)) if slab == 1 else (lambda value: value)
 
         @pl.when(at_core == slab)
@@ -81,18 +87,12 @@
             couple_copy.start()
             for array in range(2):
                 for piece in pieces:
-                    tile_copy(array, piece[0]).start()
-            for array in range(2):
-                for tile in unused:
-                    tile_copy(array, tile).start()
+                    array_copy(array, piece[0]).start()
 
             def arrive(array, tile):
-                tile_copy(array, tile).wait()
+                array_copy(array, tile).wait()
                 if slab == 1:
-                    ref = arrays[array][1]
-                    ref[LANES * step + tile * rows : LANES * step + (tile + 1) * rows] = ref[
-                        tile * rows : (tile + 1) * rows
-                    ]
+                    repeat_first(rows, arrays[array][1], tile)
 
             inverse_copy.wait()
             couple_copy.wait()
@@ -109,25 +109,51 @@
                     pack_piece(
                         rows, slab, arrays[array][1], array, piece, out_ref, scale[0:1] if array == 1 else None
                     )
-            for array in range(2):
-                for tile in unused:
-                    arrive(array, tile)
-
-
-def pack_own_body(rows, temp_ref, source_ref, sent_ref, out_ref):
+
+
+def pack_own_body(rows, temp_hbm, source_hbm, temp_ref, source_ref, sent_ref, out_ref, more_temp, more_source, sems):
     core, _ = position()
-    step = temp_ref.shape[0] // (LANES + 1)
+    step = temp_hbm.shape[0] // LANES
+    arrays = ((temp_hbm, temp_ref, more_temp), (source_hbm, source_ref, more_source))
     base = out_ref.shape[0] - LANES - 8
-    scale = sent_ref[base + LANES : base + LANES + 1, :]
+    scale = (None, sent_ref[base + LANES : base + LANES + 1, :])
     for slab in range(2):
 
         @pl.when(core == slab)
         def _():
-            for array, ref in enumerate((temp_ref, source_ref)):
-                for piece in window_pieces(rows, step, slab == 1):
-                    pack_piece(rows, slab, ref, array, piece, out_ref, scale if array == 1 else None)
+            held = [piece[0] for piece in window_pieces(rows, step, slab == 0)]
+            pieces = window_pieces(rows, step, slab == 1)
+            (tile,) = [at for at in range(step // rows) if at not in held]
+            copies = [tile_copy(rows, hbm, more, tile, sems.at[at]) for at, (hbm, _, more) in enumerate(arrays)]
+            for copy in copies:
+                copy.start()
+            for array, (_, ref, _) in enumerate(arrays):
+                for piece in pieces:
+                    if piece[0] != tile:
+                        pack_piece(rows, slab, ref, array, piece, out_ref, scale[array])
+            for array, (_, _, more) in enumerate(arrays):
+                copies[array].wait()
+                if slab == 1:
+                    repeat_first(rows, more, tile)
+                for piece in pieces:
+                    if piece[0] == tile:
+                        pack_piece(rows, slab, more, array, piece, out_ref, scale[array])
 
     out_ref[base:, :] = sent_ref[base:, :]
+
+
+def pack_own(rows, temp, source, temp_held, source_held, sent):
+    hbm = pl.BlockSpec(memory_space=pltpu.HBM)
+    lines = pltpu.VMEM(temp_held.shape, jnp.float32)
+    return pl.pallas_call(
+        functools.partial(pack_own_body, rows),
+        out_shape=jax.ShapeDtypeStruct(sent.shape, jnp.float32),
+        in_specs=[hbm] * 2 + [VMEM] * 3,
+        out_specs=VMEM,
+        scratch_shapes=[lines, lines, pltpu.SemaphoreType.DMA((2,))],
+        compiler_params=pltpu.CompilerParams(vmem_limit_bytes=12 * 2**20),
+        name="pack_own",
+    )(*(pltpu.with_memory_space_constraint(array, pltpu.HBM) for array in (temp, source)), temp_held, source_held, sent)
 
 
 def pack_send(rows, temp, source, inverse, couple):
@@ -509,6 +535,8 @@
         [(i, i + 1) for i in range(start, lat_count - 1, 2)] + [(i + 1, i) for i in range(start, lat_count - 1, 2)]
         for start in (0, 1)
     ]
+    last = lat_count - 1
+    far_pairs = [[pair for pair in group if pair not in ((1, 0), (last - 1, last))] for group in pairs]
     crossed = [
         [(d * lat_count + a, (1 - d) * lat_count + b) for d in range(2) for a, b in group] for group in pairs
     ]
@@ -518,15 +546,15 @@
     cross = lambda value, group: lax.ppermute(value, ("depth", "lat"), crossed[group])
 
     temp, src = lines_of(temp_old), lines_of(source)
-    sent, temp, src = pack_send(rows, temp, src, block_inverse, lat_couple.reshape(1, LANES))
+    sent, *held = pack_send(rows, temp, src, block_inverse, lat_couple.reshape(1, LANES))
     other = swap(sent)
-    (mine,) = call(
-        functools.partial(pack_own_body, rows), [jax.ShapeDtypeStruct(sent.shape, jnp.float32)], temp, src, sent
-    )
+    mine = pack_own(rows, temp, src, *held, sent)
     far_first, far_second, mid_first, mid_second, near_first, near_second, own = sweeps(
         face_couple, mine, other, rows, half, lat_count
     )
-    far_first, far_second = exchange(far_first, 0), exchange(far_second, 1)
+    far_first, far_second = (
+        lax.ppermute(value, "lat", far_pairs[group]) for group, value in enumerate((far_first, far_second))
+    )
     mid_first, mid_second = exchange(mid_first, 0), exchange(mid_second, 1)
     joined = [piece(2), piece(2)]
     same_second, cross_second = call(join_body, joined, near_second, far_first)

time: 66.3 us -> 66.3 us (level)
  Pallas kernels: 12.7 us -> 13.8 us
  waiting for transfers between devices: 12.3 us -> 11.3 us
    ppermute x0 -> x2, starting transfers between devices: none -> 6.91 us  [program(): lax.ppermute(value, 'lat', far_pairs[group])]
    ppermute x6 -> x4, starting transfers between devices: 23.4 us -> 16.5 us  [program(): exchange = lambda value, group: lax.ppermute(value, 'lat', pairs[group])]
    pallas_call x0 -> x1, Pallas kernels: none -> 1.56 us  [pack_own(): pl.pallas_call(functools.partial(pack_own_body, rows), out_shape=jax.Shap...]
    ppermute x2, waiting for transfers between devices: 1.28 us -> 0.24 us  [program(): swap = lambda value: lax.ppermute(value, 'depth', [(0, 1), (1, 0)])]
    ppermute x0 -> x2, waiting for transfers between devices: none -> 0.78 us  [program(): lax.ppermute(value, 'lat', far_pairs[group])]
    ppermute x6 -> x4, waiting for transfers between devices: 5.65 us -> 4.89 us  [program(): exchange = lambda value, group: lax.ppermute(value, 'lat', pairs[group])]
  transfers between devices with their start and end apart: 10 -> 10, of which waited for: 4 -> 4; matrix products, arithmetic and copies ran while one was open for 0% -> 0% of each run, Pallas kernels for 8% -> 9%
where the time goes in v5:
time: 66.3 us; the launch traced here: 65.4 us
  starting transfers between devices  39.5 us (60%)
  Pallas kernels  13.8 us (21%)
  waiting for transfers between devices  11.3 us (17%)
  between operations  0.84 us (1%)
    ppermute x4, starting transfers between devices, program(): exchange = lambda value, group: lax.ppermute(value, 'lat', pairs[group])  16.5 us
    ppermute x2, starting transfers between devices, program(): lax.ppermute(value, ('depth', 'lat'), crossed[group])  9.03 us
    ppermute x2, starting transfers between devices, program(): swap = lambda value: lax.ppermute(value, 'depth', [(0, 1), (1, 0)])  7.11 us
    ppermute x2, starting transfers between devices, program(): lax.ppermute(value, 'lat', far_pairs[group])  6.91 us
    ppermute x2, waiting for transfers between devices, program(): lax.ppermute(value, ('depth', 'lat'), crossed[group])  5.35 us
    ppermute x4, waiting for transfers between devices, program(): exchange = lambda value, group: lax.ppermute(value, 'lat', pairs[group])  4.89 us
    pallas_call x3, Pallas kernels, finish(): pl.pallas_call(functools.partial(finish_body, crossed, tuple(pieces)), ou...  2.65 us
    pallas_call x1, Pallas kernels, sweeps(): pl.pallas_call(functools.partial(core_body, rows, width, lat_count), out_...  2.6 us
  transfers between devices with their start and end apart: 10, of which 4 were waited for; matrix products, arithmetic and copies ran while one was open for 0% of the time, Pallas kernels for 9%

profile of v5, /device:TPU:257, one launch (start us, length us, event | category | flops | bytes accessed | tf_op | source)
XLA Modules:
  0.0 65.4 jit_solution(6480333420607461252)
XLA Ops:
  0.0 1.9 %pack_send.1 = (f32[2312,128]{1,0:T(8,128)S(1)}, f32[2064,128]{1,0:T(8,128)S(1)}, f32[2064,128]{1,0:T(8,128)S(1)}) custom-call(f32[2048,128]{1,0:T(8,128)} %bitcast.16, f32[2048,128]{1,0:T(8,128)} %bitcast.18, f32[128,128]{1,0:T(8,128)} %inverse_hbm.1, f32[1,128]{1,0:T(1,128)} %bitcast.20), custom_call_target="tpu_custom_call" | custom-call | tf_op jit(solution)/shard_map/pack_send/pallas_call | solution.py:164
  1.9 2.6 %collective-permute-start = (f32[2312,128]{1,0:T(8,128)S(1)}, f32[2312,128]{1,0:T(8,128)S(1)}, u32[]{:S(2)}, u32[]{:S(2)}) collective-permute-start(f32[2312,128]{1,0:T(8,128)S(1)} %get-tuple-element.26.sent_ref), channel_id=1, source_target_pairs={{0,256},{256,0},{1,257},{257,1},{2,258},{258,2},{3,259},{259,3},{4... | collective-permute-start | bytes 3551240 | tf_op jit(solution)/shard_map/ppermute | solution.py:544
  5.2 1.6 %pack_own.1.mine_ref = f32[2312,128]{1,0:T(8,128)S(1)} custom-call(f32[2048,128]{1,0:T(8,128)} %bitcast.17, f32[2048,128]{1,0:T(8,128)} %bitcast.19, f32[2064,128]{1,0:T(8,128)S(1)} %get-tuple-element.24.temp_ref, f32[2064,128]{1,0:T(8,128)S(1)} %get-tuple-element.25.source_ref, f32[2312,128]{1,0:T(8,128)S(1)} %get-tuple-element.26.sent_ref), custom_call_target="tpu_custom_call" | custom-call | tf_op jit(solution)/shard_map/pack_own/pallas_call | solution.py:148
  6.7 0.2 collective-permute-done.other_ref
  7.0 2.3 %strips.1 = (f32[2,2,256,128]{3,2,1,0:T(8,128)S(1)}, f32[2,2,256,128]{3,2,1,0:T(8,128)S(1)}, f32[6,4,2,288,128]{4,3,2,1,0:T(8,128)S(1)}) custom-call(f32[1]{0:T(128)S(6)} %copy.13.face_ref, f32[2312,128]{1,0:T(8,128)S(1)} %pack_own.1.mine_ref, f32[2312,128]{1,0:T(8,128)S(1)} %collective-permute-done.other_ref), custom_call_target="tpu_custom_call" | custom-call | tf_op jit(solution)/shard_map/strips/pallas_call | solution.py:410
  9.3 2.5 %middle.1 = (f32[2,2,256,128]{3,2,1,0:T(8,128)S(1)}, f32[2,2,256,128]{3,2,1,0:T(8,128)S(1)}, f32[5,4,2,288,128]{4,3,2,1,0:T(8,128)S(1)}, f32[2,4,272,128]{3,2,1,0:T(8,128)S(1)}) custom-call(f32[1]{0:T(128)S(6)} %copy.13.face_ref, f32[2312,128]{1,0:T(8,128)S(1)} %pack_own.1.mine_ref, f32[2312,128]{1,0:T(8,128)S(1)} %collective-permute-done.other_ref, ...), custom_call_target="tpu_custom_call" | custom-call | tf_op jit(solution)/shard_map/middle/pallas_call | solution.py:423
  11.8 3.1 %collective-permute-start.1 = (f32[2,2,256,128]{3,2,1,0:T(8,128)S(1)}, f32[2,2,256,128]{3,2,1,0:T(8,128)S(1)}, u32[]{:S(2)}, u32[]{:S(2)}) collective-permute-start(f32[2,2,256,128]{3,2,1,0:T(8,128)S(1)} %get-tuple-element.31), channel_id=1, source_target_pairs={{0,1},{2,3},{4,5},{6,7},{8,9},{10,11},{12,13},{14,15},{16,17},{18,... | collective-permute-start | bytes 1572872 | tf_op jit(solution)/shard_map/ppermute | solution.py:545
  14.9 5.7 %collective-permute-start.2 = (f32[2,2,256,128]{3,2,1,0:T(8,128)S(1)}, f32[2,2,256,128]{3,2,1,0:T(8,128)S(1)}, u32[]{:S(2)}, u32[]{:S(2)}) collective-permute-start(f32[2,2,256,128]{3,2,1,0:T(8,128)S(1)} %get-tuple-element.32), channel_id=1, source_target_pairs={{1,2},{3,4},{5,6},{7,8},{9,10},{11,12},{13,14},{15,16},{17,18},{19... | collective-permute-start | bytes 1572872 | tf_op jit(solution)/shard_map/ppermute | solution.py:545
  20.7 1.9 %collective-permute-start.6 = (f32[2,2,256,128]{3,2,1,0:T(8,128)S(1)}, f32[2,2,256,128]{3,2,1,0:T(8,128)S(1)}, u32[]{:S(2)}, u32[]{:S(2)}) collective-permute-start(f32[2,2,256,128]{3,2,1,0:T(8,128)S(1)} %get-tuple-element.38), channel_id=1, source_target_pairs={{0,1},{2,3},{4,5},{6,7},{8,9},{10,11},{12,13},{14,15},{16,17},{18,... | collective-permute-start | bytes 1572872 | tf_op jit(solution)/shard_map/ppermute | solution.py:556
  22.6 5.0 %collective-permute-start.4 = (f32[2,2,256,128]{3,2,1,0:T(8,128)S(1)}, f32[2,2,256,128]{3,2,1,0:T(8,128)S(1)}, u32[]{:S(2)}, u32[]{:S(2)}) collective-permute-start(f32[2,2,256,128]{3,2,1,0:T(8,128)S(1)} %get-tuple-element.35), channel_id=1, source_target_pairs={{1,2},{3,4},{5,6},{7,8},{9,10},{11,12},{13,14},{15,16},{17,18},{19... | collective-permute-start | bytes 1572872 | tf_op jit(solution)/shard_map/ppermute | solution.py:556
  27.6 2.6 %core.1 = (f32[2,2,256,128]{3,2,1,0:T(8,128)S(1)}, f32[2,2,256,128]{3,2,1,0:T(8,128)S(1)}, f32[4,2,256,128]{3,2,1,0:T(8,128)S(1)}) custom-call(f32[1]{0:T(128)S(6)} %copy.13.face_ref, f32[2312,128]{1,0:T(8,128)S(1)} %pack_own.1.mine_ref, f32[2312,128]{1,0:T(8,128)S(1)} %collective-permute-done.other_ref, f32[5,4,2,288,128]{4,3,2,1,0:T(8,128)S(1)} %get-tuple-element.28.inner, ...), custom_call_target="tpu_custom_call" | custom-call | tf_op jit(solution)/shard_map/core/pallas_call | solution.py:437
  30.2 0.0 collective-permute-done.1.mid_first
  30.2 4.9 %collective-permute-done.2.mid_second = f32[2,2,256,128]{3,2,1,0:T(8,128)S(1)} collective-permute-done((f32[2,2,256,128]{3,2,1,0:T(8,128)S(1)}, f32[2,2,256,128]{3,2,1,0:T(8,128)S(1)}, u32[]{:S(2)}, u32[]{:S(2)}) %collective-permute-start.2) | collective-permute-done | bytes 524320 | tf_op jit(solution)/shard_map/ppermute | solution.py:545
  35.1 0.1 shard_map.55
  35.2 4.5 %collective-permute-start.3 = (f32[4,256,128]{2,1,0:T(8,128)S(1)}, f32[4,256,128]{2,1,0:T(8,128)S(1)}, u32[]{:S(2)}, u32[]{:S(2)}) collective-permute-start(f32[4,256,128]{2,1,0:T(8,128)S(1)} %get-tuple-element.33), channel_id=1, source_target_pairs={{0,256},{256,0},{1,257},{257,1},{2,258},{258,2},{3,259},{259,3},{4... | collective-permute-start | bytes 1572872 | tf_op jit(solution)/shard_map/ppermute | solution.py:544
  39.7 0.0 collective-permute-done.6.far
  39.7 0.1 shard_map.57
  39.8 5.7 %collective-permute-start.9 = (f32[2,256,128]{2,1,0:T(8,128)S(1)}, f32[2,256,128]{2,1,0:T(8,128)S(1)}, u32[]{:S(2)}, u32[]{:S(2)}) collective-permute-start(f32[2,256,128]{2,1,0:T(8,128)S(1)} %get-tuple-element.42), channel_id=1, source_target_pairs={{1,2},{3,4},{5,6},{7,8},{9,10},{11,12},{13,14},{15,16},{17,18},{19... | collective-permute-start | bytes 786440 | tf_op jit(solution)/shard_map/ppermute | solution.py:545
  45.5 0.8 %collective-permute-done.4.far = f32[2,2,256,128]{3,2,1,0:T(8,128)S(1)} collective-permute-done((f32[2,2,256,128]{3,2,1,0:T(8,128)S(1)}, f32[2,2,256,128]{3,2,1,0:T(8,128)S(1)}, u32[]{:S(2)}, u32[]{:S(2)}) %collective-permute-start.4) | collective-permute-done | bytes 524320 | tf_op jit(solution)/shard_map/ppermute | solution.py:556
  46.3 0.1 shard_map.56
  46.4 1.9 %collective-permute-start.8 = (f32[2,256,128]{2,1,0:T(8,128)S(1)}, f32[2,256,128]{2,1,0:T(8,128)S(1)}, u32[]{:S(2)}, u32[]{:S(2)}) collective-permute-start(f32[2,256,128]{2,1,0:T(8,128)S(1)} %get-tuple-element.41), channel_id=1, source_target_pairs={{0,1},{2,3},{4,5},{6,7},{8,9},{10,11},{12,13},{14,15},{16,17},{18,... | collective-permute-start | bytes 786440 | tf_op jit(solution)/shard_map/ppermute | solution.py:545
  48.3 7.1 %collective-permute-start.7 = (f32[2,256,128]{2,1,0:T(8,128)S(1)}, f32[2,256,128]{2,1,0:T(8,128)S(1)}, u32[]{:S(2)}, u32[]{:S(2)}) collective-permute-start(f32[2,256,128]{2,1,0:T(8,128)S(1)} %get-tuple-element.39), channel_id=1, source_target_pairs={{1,258},{3,260},{5,262},{7,264},{9,266},{11,268},{13,270},{15,272}... | collective-permute-start | bytes 786440 | tf_op jit(solution)/shard_map/ppermute | solution.py:546
  55.4 1.9 %collective-permute-start.5 = (f32[2,256,128]{2,1,0:T(8,128)S(1)}, f32[2,256,128]{2,1,0:T(8,128)S(1)}, u32[]{:S(2)}, u32[]{:S(2)}) collective-permute-start(f32[2,256,128]{2,1,0:T(8,128)S(1)} %get-tuple-element.36), channel_id=1, source_target_pairs={{0,257},{2,259},{4,261},{6,263},{8,265},{10,267},{12,269},{14,271}... | collective-permute-start | bytes 786440 | tf_op jit(solution)/shard_map/ppermute | solution.py:546
  57.4 0.0 collective-permute-done.9.refs_1_
  57.4 0.0 collective-permute-done.8.refs_0_
  57.4 1.0 %shard_map.58.refs_1_ = f32[2048,128]{1,0:T(8,128)} custom-call(f32[4,256,128]{2,1,0:T(8,128)S(1)} %get-tuple-element.40.base, f32[2,256,128]{2,1,0:T(8,128)S(1)} %collective-permute-done.8.refs_0_, f32[2,256,128]{2,1,0:T(8,128)S(1)} %collective-permute-done.9.refs_1_), custom_call_target="tpu_custom_call" | custom-call | tf_op jit(solution)/shard_map/pallas_call | solution.py:507
  58.4 5.4 %collective-permute-done.7.refs_0_ = f32[2,256,128]{2,1,0:T(8,128)S(1)} collective-permute-done((f32[2,256,128]{2,1,0:T(8,128)S(1)}, f32[2,256,128]{2,1,0:T(8,128)S(1)}, u32[]{:S(2)}, u32[]{:S(2)}) %collective-permute-start.7) | collective-permute-done | bytes 262176 | tf_op jit(solution)/shard_map/ppermute | solution.py:546
  63.7 0.0 collective-permute-done.3.base
  63.7 0.8 %shard_map.59.refs_1_ = f32[2048,128]{1,0:T(8,128)} custom-call(f32[4,256,128]{2,1,0:T(8,128)S(1)} %collective-permute-done.3.base, f32[2,256,128]{2,1,0:T(8,128)S(1)} %collective-permute-done.7.refs_0_, f32[2048,128]{1,0:T(8,128)} %shard_map.58.refs_1_), custom_call_target="tpu_custom_call", output_to_operand_aliasing={{}: (2, {})} | custom-call | tf_op jit(solution)/shard_map/pallas_call | solution.py:507
  64.5 0.0 collective-permute-done.5.refs_0_
  64.6 0.9 %shard_map.60 = f32[2048,128]{1,0:T(8,128)} custom-call(f32[4,256,128]{2,1,0:T(8,128)S(1)} %collective-permute-done.3.base, f32[2,256,128]{2,1,0:T(8,128)S(1)} %collective-permute-done.5.refs_0_, f32[2048,128]{1,0:T(8,128)} %shard_map.59.refs_1_), custom_call_target="tpu_custom_call", output_to_operand_aliasing={{}: (2, {})} | custom-call | tf_op jit(solution)/shard_map/pallas_call | solution.py:507
Async XLA Ops:
  1.9 5.1 %collective-permute-start = (f32[2312,128]{1,0:T(8,128)S(1)}, f32[2312,128]{1,0:T(8,128)S(1)}, u32[]{:S(2)}, u32[]{:S(2)}) collective-permute-start(f32[2312,128]{1,0:T(8,128)S(1)} %get-tuple-element.26.sent_ref), channel_id=1, source_target_pairs={{0,256},{256,0},{1,257},{257,1},{2,258},{258,2},{3,259},{259,3},{4... | collective-permute-start | bytes 3551240 | tf_op jit(solution)/shard_map/ppermute | solution.py:544
  11.8 18.4 %collective-permute-start.1 = (f32[2,2,256,128]{3,2,1,0:T(8,128)S(1)}, f32[2,2,256,128]{3,2,1,0:T(8,128)S(1)}, u32[]{:S(2)}, u32[]{:S(2)}) collective-permute-start(f32[2,2,256,128]{3,2,1,0:T(8,128)S(1)} %get-tuple-element.31), channel_id=1, source_target_pairs={{0,1},{2,3},{4,5},{6,7},{8,9},{10,11},{12,13},{14,15},{16,17},{18,... | collective-permute-start | bytes 1572872 | tf_op jit(solution)/shard_map/ppermute | solution.py:545
  14.9 20.2 %collective-permute-start.2 = (f32[2,2,256,128]{3,2,1,0:T(8,128)S(1)}, f32[2,2,256,128]{3,2,1,0:T(8,128)S(1)}, u32[]{:S(2)}, u32[]{:S(2)}) collective-permute-start(f32[2,2,256,128]{3,2,1,0:T(8,128)S(1)} %get-tuple-element.32), channel_id=1, source_target_pairs={{1,2},{3,4},{5,6},{7,8},{9,10},{11,12},{13,14},{15,16},{17,18},{19... | collective-permute-start | bytes 1572872 | tf_op jit(solution)/shard_map/ppermute | solution.py:545
  20.7 19.1 %collective-permute-start.6 = (f32[2,2,256,128]{3,2,1,0:T(8,128)S(1)}, f32[2,2,256,128]{3,2,1,0:T(8,128)S(1)}, u32[]{:S(2)}, u32[]{:S(2)}) collective-permute-start(f32[2,2,256,128]{3,2,1,0:T(8,128)S(1)} %get-tuple-element.38), channel_id=1, source_target_pairs={{0,1},{2,3},{4,5},{6,7},{8,9},{10,11},{12,13},{14,15},{16,17},{18,... | collective-permute-start | bytes 1572872 | tf_op jit(solution)/shard_map/ppermute | solution.py:556
  22.6 23.7 %collective-permute-start.4 = (f32[2,2,256,128]{3,2,1,0:T(8,128)S(1)}, f32[2,2,256,128]{3,2,1,0:T(8,128)S(1)}, u32[]{:S(2)}, u32[]{:S(2)}) collective-permute-start(f32[2,2,256,128]{3,2,1,0:T(8,128)S(1)} %get-tuple-element.35), channel_id=1, source_target_pairs={{1,2},{3,4},{5,6},{7,8},{9,10},{11,12},{13,14},{15,16},{17,18},{19... | collective-permute-start | bytes 1572872 | tf_op jit(solution)/shard_map/ppermute | solution.py:556
  35.2 28.5 %collective-permute-start.3 = (f32[4,256,128]{2,1,0:T(8,128)S(1)}, f32[4,256,128]{2,1,0:T(8,128)S(1)}, u32[]{:S(2)}, u32[]{:S(2)}) collective-permute-start(f32[4,256,128]{2,1,0:T(8,128)S(1)} %get-tuple-element.33), channel_id=1, source_target_pairs={{0,256},{256,0},{1,257},{257,1},{2,258},{258,2},{3,259},{259,3},{4... | collective-permute-start | bytes 1572872 | tf_op jit(solution)/shard_map/ppermute | solution.py:544
  39.8 17.5 %collective-permute-start.9 = (f32[2,256,128]{2,1,0:T(8,128)S(1)}, f32[2,256,128]{2,1,0:T(8,128)S(1)}, u32[]{:S(2)}, u32[]{:S(2)}) collective-permute-start(f32[2,256,128]{2,1,0:T(8,128)S(1)} %get-tuple-element.42), channel_id=1, source_target_pairs={{1,2},{3,4},{5,6},{7,8},{9,10},{11,12},{13,14},{15,16},{17,18},{19... | collective-permute-start | bytes 786440 | tf_op jit(solution)/shard_map/ppermute | solution.py:545
  46.4 11.0 %collective-permute-start.8 = (f32[2,256,128]{2,1,0:T(8,128)S(1)}, f32[2,256,128]{2,1,0:T(8,128)S(1)}, u32[]{:S(2)}, u32[]{:S(2)}) collective-permute-start(f32[2,256,128]{2,1,0:T(8,128)S(1)} %get-tuple-element.41), channel_id=1, source_target_pairs={{0,1},{2,3},{4,5},{6,7},{8,9},{10,11},{12,13},{14,15},{16,17},{18,... | collective-permute-start | bytes 786440 | tf_op jit(solution)/shard_map/ppermute | solution.py:545
  48.3 15.4 %collective-permute-start.7 = (f32[2,256,128]{2,1,0:T(8,128)S(1)}, f32[2,256,128]{2,1,0:T(8,128)S(1)}, u32[]{:S(2)}, u32[]{:S(2)}) collective-permute-start(f32[2,256,128]{2,1,0:T(8,128)S(1)} %get-tuple-element.39), channel_id=1, source_target_pairs={{1,258},{3,260},{5,262},{7,264},{9,266},{11,268},{13,270},{15,272}... | collective-permute-start | bytes 786440 | tf_op jit(solution)/shard_map/ppermute | solution.py:546
  55.4 9.1 %collective-permute-start.5 = (f32[2,256,128]{2,1,0:T(8,128)S(1)}, f32[2,256,128]{2,1,0:T(8,128)S(1)}, u32[]{:S(2)}, u32[]{:S(2)}) collective-permute-start(f32[2,256,128]{2,1,0:T(8,128)S(1)} %get-tuple-element.36), channel_id=1, source_target_pairs={{0,257},{2,259},{4,261},{6,263},{8,265},{10,267},{12,269},{14,271}... | collective-permute-start | bytes 786440 | tf_op jit(solution)/shard_map/ppermute | solution.py:546

commit v6 on v5

--- a/solution.py
+++ b/solution.py
@@ -11,7 +11,7 @@
 LANES = 128
 OVERLAP = 16
 PAD = 8
-GROUP = 4
+GROUP = 2
 FINISH = ((True,), (False,))
 VMEM = pl.BlockSpec(memory_space=pltpu.VMEM)
 SMEM = pl.BlockSpec(memory_space=pltpu.SMEM)
@@ -535,8 +535,6 @@
         [(i, i + 1) for i in range(start, lat_count - 1, 2)] + [(i + 1, i) for i in range(start, lat_count - 1, 2)]
         for start in (0, 1)
     ]
-    last = lat_count - 1
-    far_pairs = [[pair for pair in group if pair not in ((1, 0), (last - 1, last))] for group in pairs]
     crossed = [
         [(d * lat_count + a, (1 - d) * lat_count + b) for d in range(2) for a, b in group] for group in pairs
     ]
@@ -552,9 +550,7 @@
     far_first, far_second, mid_first, mid_second, near_first, near_second, own = sweeps(
         face_couple, mine, other, rows, half, lat_count
     )
-    far_first, far_second = (
-        lax.ppermute(value, "lat", far_pairs[group]) for group, value in enumerate((far_first, far_second))
-    )
+    far_first, far_second = exchange(far_first, 0), exchange(far_second, 1)
     mid_first, mid_second = exchange(mid_first, 0), exchange(mid_second, 1)
     joined = [piece(2), piece(2)]
     same_second, cross_second = call(join_body, joined, near_second, far_first)

time: 66.3 us -> 66.3 us (level)
    ppermute x2 -> x0, starting transfers between devices: 6.91 us -> none  [program(): lax.ppermute(value, 'lat', far_pairs[group])]
    ppermute x4 -> x6, starting transfers between devices: 16.5 us -> 23.4 us  [program(): exchange = lambda value, group: lax.ppermute(value, 'lat', pairs[group])]
    ppermute x4 -> x6, waiting for transfers between devices: 4.89 us -> 5.69 us  [program(): exchange = lambda value, group: lax.ppermute(value, 'lat', pairs[group])]
    ppermute x2 -> x0, waiting for transfers between devices: 0.78 us -> none  [program(): lax.ppermute(value, 'lat', far_pairs[group])]
where the time goes in v6:
time: 66.3 us; the launch traced here: 65.4 us
  starting transfers between devices  39.5 us (60%)
  Pallas kernels  13.7 us (21%)
  waiting for transfers between devices  11.3 us (17%)
  between operations  0.84 us (1%)
    ppermute x6, starting transfers between devices, program(): exchange = lambda value, group: lax.ppermute(value, 'lat', pairs[group])  23.4 us
    ppermute x2, starting transfers between devices, program(): lax.ppermute(value, ('depth', 'lat'), crossed[group])  9.03 us
    ppermute x2, starting transfers between devices, program(): swap = lambda value: lax.ppermute(value, 'depth', [(0, 1), (1, 0)])  7.11 us
    ppermute x6, waiting for transfers between devices, program(): exchange = lambda value, group: lax.ppermute(value, 'lat', pairs[group])  5.69 us
    ppermute x2, waiting for transfers between devices, program(): lax.ppermute(value, ('depth', 'lat'), crossed[group])  5.35 us
    pallas_call x3, Pallas kernels, finish(): pl.pallas_call(functools.partial(finish_body, crossed, tuple(pieces)), ou...  2.65 us
    pallas_call x1, Pallas kernels, sweeps(): pl.pallas_call(functools.partial(core_body, rows, width, lat_count), out_...  2.57 us
    pallas_call x1, Pallas kernels, sweeps(): pl.pallas_call(functools.partial(middle_body, rows, width, lat_count), ou...  2.51 us
  transfers between devices with their start and end apart: 10, of which 4 were waited for; matrix products, arithmetic and copies ran while one was open for 0% of the time, Pallas kernels for 9%

profile of v6, /device:TPU:257, one launch (start us, length us, event | category | flops | bytes accessed | tf_op | source)
XLA Modules:
  0.0 65.4 jit_solution(1357661748705309304)
XLA Ops:
  0.0 1.9 %pack_send.1 = (f32[2312,128]{1,0:T(8,128)S(1)}, f32[2064,128]{1,0:T(8,128)S(1)}, f32[2064,128]{1,0:T(8,128)S(1)}) custom-call(f32[2048,128]{1,0:T(8,128)} %bitcast.16, f32[2048,128]{1,0:T(8,128)} %bitcast.18, f32[128,128]{1,0:T(8,128)} %inverse_hbm.1, f32[1,128]{1,0:T(1,128)} %bitcast.20), custom_call_target="tpu_custom_call" | custom-call | tf_op jit(solution)/shard_map/pack_send/pallas_call | solution.py:164
  1.9 2.6 %collective-permute-start = (f32[2312,128]{1,0:T(8,128)S(1)}, f32[2312,128]{1,0:T(8,128)S(1)}, u32[]{:S(2)}, u32[]{:S(2)}) collective-permute-start(f32[2312,128]{1,0:T(8,128)S(1)} %get-tuple-element.26.sent_ref), channel_id=1, source_target_pairs={{0,256},{256,0},{1,257},{257,1},{2,258},{258,2},{3,259},{259,3},{4... | collective-permute-start | bytes 3551240 | tf_op jit(solution)/shard_map/ppermute | solution.py:542
  5.2 1.6 %pack_own.1.mine_ref = f32[2312,128]{1,0:T(8,128)S(1)} custom-call(f32[2048,128]{1,0:T(8,128)} %bitcast.17, f32[2048,128]{1,0:T(8,128)} %bitcast.19, f32[2064,128]{1,0:T(8,128)S(1)} %get-tuple-element.24.temp_ref, f32[2064,128]{1,0:T(8,128)S(1)} %get-tuple-element.25.source_ref, f32[2312,128]{1,0:T(8,128)S(1)} %get-tuple-element.26.sent_ref), custom_call_target="tpu_custom_call" | custom-call | tf_op jit(solution)/shard_map/pack_own/pallas_call | solution.py:148
  6.7 0.2 collective-permute-done.other_ref
  7.0 2.3 %strips.1 = (f32[2,2,256,128]{3,2,1,0:T(8,128)S(1)}, f32[2,2,256,128]{3,2,1,0:T(8,128)S(1)}, f32[6,4,2,288,128]{4,3,2,1,0:T(8,128)S(1)}) custom-call(f32[1]{0:T(128)S(6)} %copy.13.face_ref, f32[2312,128]{1,0:T(8,128)S(1)} %pack_own.1.mine_ref, f32[2312,128]{1,0:T(8,128)S(1)} %collective-permute-done.other_ref), custom_call_target="tpu_custom_call" | custom-call | tf_op jit(solution)/shard_map/strips/pallas_call | solution.py:410
  9.3 2.5 %middle.1 = (f32[2,2,256,128]{3,2,1,0:T(8,128)S(1)}, f32[2,2,256,128]{3,2,1,0:T(8,128)S(1)}, f32[5,4,2,288,128]{4,3,2,1,0:T(8,128)S(1)}, f32[2,4,272,128]{3,2,1,0:T(8,128)S(1)}) custom-call(f32[1]{0:T(128)S(6)} %copy.13.face_ref, f32[2312,128]{1,0:T(8,128)S(1)} %pack_own.1.mine_ref, f32[2312,128]{1,0:T(8,128)S(1)} %collective-permute-done.other_ref, ...), custom_call_target="tpu_custom_call" | custom-call | tf_op jit(solution)/shard_map/middle/pallas_call | solution.py:423
  11.8 3.1 %collective-permute-start.1 = (f32[2,2,256,128]{3,2,1,0:T(8,128)S(1)}, f32[2,2,256,128]{3,2,1,0:T(8,128)S(1)}, u32[]{:S(2)}, u32[]{:S(2)}) collective-permute-start(f32[2,2,256,128]{3,2,1,0:T(8,128)S(1)} %get-tuple-element.31), channel_id=1, source_target_pairs={{0,1},{2,3},{4,5},{6,7},{8,9},{10,11},{12,13},{14,15},{16,17},{18,... | collective-permute-start | bytes 1572872 | tf_op jit(solution)/shard_map/ppermute | solution.py:543
  14.9 5.7 %collective-permute-start.2 = (f32[2,2,256,128]{3,2,1,0:T(8,128)S(1)}, f32[2,2,256,128]{3,2,1,0:T(8,128)S(1)}, u32[]{:S(2)}, u32[]{:S(2)}) collective-permute-start(f32[2,2,256,128]{3,2,1,0:T(8,128)S(1)} %get-tuple-element.32), channel_id=1, source_target_pairs={{1,2},{3,4},{5,6},{7,8},{9,10},{11,12},{13,14},{15,16},{17,18},{19... | collective-permute-start | bytes 1572872 | tf_op jit(solution)/shard_map/ppermute | solution.py:543
  20.7 1.9 %collective-permute-start.6 = (f32[2,2,256,128]{3,2,1,0:T(8,128)S(1)}, f32[2,2,256,128]{3,2,1,0:T(8,128)S(1)}, u32[]{:S(2)}, u32[]{:S(2)}) collective-permute-start(f32[2,2,256,128]{3,2,1,0:T(8,128)S(1)} %get-tuple-element.38), channel_id=1, source_target_pairs={{0,1},{2,3},{4,5},{6,7},{8,9},{10,11},{12,13},{14,15},{16,17},{18,... | collective-permute-start | bytes 1572872 | tf_op jit(solution)/shard_map/ppermute | solution.py:543
  22.6 5.0 %collective-permute-start.4 = (f32[2,2,256,128]{3,2,1,0:T(8,128)S(1)}, f32[2,2,256,128]{3,2,1,0:T(8,128)S(1)}, u32[]{:S(2)}, u32[]{:S(2)}) collective-permute-start(f32[2,2,256,128]{3,2,1,0:T(8,128)S(1)} %get-tuple-element.35), channel_id=1, source_target_pairs={{1,2},{3,4},{5,6},{7,8},{9,10},{11,12},{13,14},{15,16},{17,18},{19... | collective-permute-start | bytes 1572872 | tf_op jit(solution)/shard_map/ppermute | solution.py:543
  27.6 2.6 %core.1 = (f32[2,2,256,128]{3,2,1,0:T(8,128)S(1)}, f32[2,2,256,128]{3,2,1,0:T(8,128)S(1)}, f32[4,2,256,128]{3,2,1,0:T(8,128)S(1)}) custom-call(f32[1]{0:T(128)S(6)} %copy.13.face_ref, f32[2312,128]{1,0:T(8,128)S(1)} %pack_own.1.mine_ref, f32[2312,128]{1,0:T(8,128)S(1)} %collective-permute-done.other_ref, f32[5,4,2,288,128]{4,3,2,1,0:T(8,128)S(1)} %get-tuple-element.28.inner, ...), custom_call_target="tpu_custom_call" | custom-call | tf_op jit(solution)/shard_map/core/pallas_call | solution.py:437
  30.2 0.0 collective-permute-done.1.mid_first
  30.2 4.9 %collective-permute-done.2.mid_second = f32[2,2,256,128]{3,2,1,0:T(8,128)S(1)} collective-permute-done((f32[2,2,256,128]{3,2,1,0:T(8,128)S(1)}, f32[2,2,256,128]{3,2,1,0:T(8,128)S(1)}, u32[]{:S(2)}, u32[]{:S(2)}) %collective-permute-start.2) | collective-permute-done | bytes 524320 | tf_op jit(solution)/shard_map/ppermute | solution.py:543
  35.1 0.1 shard_map.55
  35.2 4.5 %collective-permute-start.3 = (f32[4,256,128]{2,1,0:T(8,128)S(1)}, f32[4,256,128]{2,1,0:T(8,128)S(1)}, u32[]{:S(2)}, u32[]{:S(2)}) collective-permute-start(f32[4,256,128]{2,1,0:T(8,128)S(1)} %get-tuple-element.33), channel_id=1, source_target_pairs={{0,256},{256,0},{1,257},{257,1},{2,258},{258,2},{3,259},{259,3},{4... | collective-permute-start | bytes 1572872 | tf_op jit(solution)/shard_map/ppermute | solution.py:542
  39.7 0.0 collective-permute-done.6.far
  39.7 0.1 shard_map.57
  39.8 5.7 %collective-permute-start.9 = (f32[2,256,128]{2,1,0:T(8,128)S(1)}, f32[2,256,128]{2,1,0:T(8,128)S(1)}, u32[]{:S(2)}, u32[]{:S(2)}) collective-permute-start(f32[2,256,128]{2,1,0:T(8,128)S(1)} %get-tuple-element.42), channel_id=1, source_target_pairs={{1,2},{3,4},{5,6},{7,8},{9,10},{11,12},{13,14},{15,16},{17,18},{19... | collective-permute-start | bytes 786440 | tf_op jit(solution)/shard_map/ppermute | solution.py:543
  45.5 0.8 %collective-permute-done.4.far = f32[2,2,256,128]{3,2,1,0:T(8,128)S(1)} collective-permute-done((f32[2,2,256,128]{3,2,1,0:T(8,128)S(1)}, f32[2,2,256,128]{3,2,1,0:T(8,128)S(1)}, u32[]{:S(2)}, u32[]{:S(2)}) %collective-permute-start.4) | collective-permute-done | bytes 524320 | tf_op jit(solution)/shard_map/ppermute | solution.py:543
  46.3 0.1 shard_map.56
  46.4 1.9 %collective-permute-start.8 = (f32[2,256,128]{2,1,0:T(8,128)S(1)}, f32[2,256,128]{2,1,0:T(8,128)S(1)}, u32[]{:S(2)}, u32[]{:S(2)}) collective-permute-start(f32[2,256,128]{2,1,0:T(8,128)S(1)} %get-tuple-element.41), channel_id=1, source_target_pairs={{0,1},{2,3},{4,5},{6,7},{8,9},{10,11},{12,13},{14,15},{16,17},{18,... | collective-permute-start | bytes 786440 | tf_op jit(solution)/shard_map/ppermute | solution.py:543
  48.3 7.1 %collective-permute-start.7 = (f32[2,256,128]{2,1,0:T(8,128)S(1)}, f32[2,256,128]{2,1,0:T(8,128)S(1)}, u32[]{:S(2)}, u32[]{:S(2)}) collective-permute-start(f32[2,256,128]{2,1,0:T(8,128)S(1)} %get-tuple-element.39), channel_id=1, source_target_pairs={{1,258},{3,260},{5,262},{7,264},{9,266},{11,268},{13,270},{15,272}... | collective-permute-start | bytes 786440 | tf_op jit(solution)/shard_map/ppermute | solution.py:544
  55.4 1.9 %collective-permute-start.5 = (f32[2,256,128]{2,1,0:T(8,128)S(1)}, f32[2,256,128]{2,1,0:T(8,128)S(1)}, u32[]{:S(2)}, u32[]{:S(2)}) collective-permute-start(f32[2,256,128]{2,1,0:T(8,128)S(1)} %get-tuple-element.36), channel_id=1, source_target_pairs={{0,257},{2,259},{4,261},{6,263},{8,265},{10,267},{12,269},{14,271}... | collective-permute-start | bytes 786440 | tf_op jit(solution)/shard_map/ppermute | solution.py:544
  57.4 0.0 collective-permute-done.9.refs_1_
  57.4 0.0 collective-permute-done.8.refs_0_
  57.4 1.0 %shard_map.58.refs_1_ = f32[2048,128]{1,0:T(8,128)} custom-call(f32[4,256,128]{2,1,0:T(8,128)S(1)} %get-tuple-element.40.base, f32[2,256,128]{2,1,0:T(8,128)S(1)} %collective-permute-done.8.refs_0_, f32[2,256,128]{2,1,0:T(8,128)S(1)} %collective-permute-done.9.refs_1_), custom_call_target="tpu_custom_call" | custom-call | tf_op jit(solution)/shard_map/pallas_call | solution.py:507
  58.4 5.4 %collective-permute-done.7.refs_0_ = f32[2,256,128]{2,1,0:T(8,128)S(1)} collective-permute-done((f32[2,256,128]{2,1,0:T(8,128)S(1)}, f32[2,256,128]{2,1,0:T(8,128)S(1)}, u32[]{:S(2)}, u32[]{:S(2)}) %collective-permute-start.7) | collective-permute-done | bytes 262176 | tf_op jit(solution)/shard_map/ppermute | solution.py:544
  63.7 0.0 collective-permute-done.3.base
  63.7 0.8 %shard_map.59.refs_1_ = f32[2048,128]{1,0:T(8,128)} custom-call(f32[4,256,128]{2,1,0:T(8,128)S(1)} %collective-permute-done.3.base, f32[2,256,128]{2,1,0:T(8,128)S(1)} %collective-permute-done.7.refs_0_, f32[2048,128]{1,0:T(8,128)} %shard_map.58.refs_1_), custom_call_target="tpu_custom_call", output_to_operand_aliasing={{}: (2, {})} | custom-call | tf_op jit(solution)/shard_map/pallas_call | solution.py:507
  64.5 0.0 collective-permute-done.5.refs_0_
  64.6 0.9 %shard_map.60 = f32[2048,128]{1,0:T(8,128)} custom-call(f32[4,256,128]{2,1,0:T(8,128)S(1)} %collective-permute-done.3.base, f32[2,256,128]{2,1,0:T(8,128)S(1)} %collective-permute-done.5.refs_0_, f32[2048,128]{1,0:T(8,128)} %shard_map.59.refs_1_), custom_call_target="tpu_custom_call", output_to_operand_aliasing={{}: (2, {})} | custom-call | tf_op jit(solution)/shard_map/pallas_call | solution.py:507
Async XLA Ops:
  1.9 5.1 %collective-permute-start = (f32[2312,128]{1,0:T(8,128)S(1)}, f32[2312,128]{1,0:T(8,128)S(1)}, u32[]{:S(2)}, u32[]{:S(2)}) collective-permute-start(f32[2312,128]{1,0:T(8,128)S(1)} %get-tuple-element.26.sent_ref), channel_id=1, source_target_pairs={{0,256},{256,0},{1,257},{257,1},{2,258},{258,2},{3,259},{259,3},{4... | collective-permute-start | bytes 3551240 | tf_op jit(solution)/shard_map/ppermute | solution.py:542
  11.8 18.4 %collective-permute-start.1 = (f32[2,2,256,128]{3,2,1,0:T(8,128)S(1)}, f32[2,2,256,128]{3,2,1,0:T(8,128)S(1)}, u32[]{:S(2)}, u32[]{:S(2)}) collective-permute-start(f32[2,2,256,128]{3,2,1,0:T(8,128)S(1)} %get-tuple-element.31), channel_id=1, source_target_pairs={{0,1},{2,3},{4,5},{6,7},{8,9},{10,11},{12,13},{14,15},{16,17},{18,... | collective-permute-start | bytes 1572872 | tf_op jit(solution)/shard_map/ppermute | solution.py:543
  14.9 20.2 %collective-permute-start.2 = (f32[2,2,256,128]{3,2,1,0:T(8,128)S(1)}, f32[2,2,256,128]{3,2,1,0:T(8,128)S(1)}, u32[]{:S(2)}, u32[]{:S(2)}) collective-permute-start(f32[2,2,256,128]{3,2,1,0:T(8,128)S(1)} %get-tuple-element.32), channel_id=1, source_target_pairs={{1,2},{3,4},{5,6},{7,8},{9,10},{11,12},{13,14},{15,16},{17,18},{19... | collective-permute-start | bytes 1572872 | tf_op jit(solution)/shard_map/ppermute | solution.py:543
  20.7 19.1 %collective-permute-start.6 = (f32[2,2,256,128]{3,2,1,0:T(8,128)S(1)}, f32[2,2,256,128]{3,2,1,0:T(8,128)S(1)}, u32[]{:S(2)}, u32[]{:S(2)}) collective-permute-start(f32[2,2,256,128]{3,2,1,0:T(8,128)S(1)} %get-tuple-element.38), channel_id=1, source_target_pairs={{0,1},{2,3},{4,5},{6,7},{8,9},{10,11},{12,13},{14,15},{16,17},{18,... | collective-permute-start | bytes 1572872 | tf_op jit(solution)/shard_map/ppermute | solution.py:543
  22.6 23.7 %collective-permute-start.4 = (f32[2,2,256,128]{3,2,1,0:T(8,128)S(1)}, f32[2,2,256,128]{3,2,1,0:T(8,128)S(1)}, u32[]{:S(2)}, u32[]{:S(2)}) collective-permute-start(f32[2,2,256,128]{3,2,1,0:T(8,128)S(1)} %get-tuple-element.35), channel_id=1, source_target_pairs={{1,2},{3,4},{5,6},{7,8},{9,10},{11,12},{13,14},{15,16},{17,18},{19... | collective-permute-start | bytes 1572872 | tf_op jit(solution)/shard_map/ppermute | solution.py:543
  35.2 28.5 %collective-permute-start.3 = (f32[4,256,128]{2,1,0:T(8,128)S(1)}, f32[4,256,128]{2,1,0:T(8,128)S(1)}, u32[]{:S(2)}, u32[]{:S(2)}) collective-permute-start(f32[4,256,128]{2,1,0:T(8,128)S(1)} %get-tuple-element.33), channel_id=1, source_target_pairs={{0,256},{256,0},{1,257},{257,1},{2,258},{258,2},{3,259},{259,3},{4... | collective-permute-start | bytes 1572872 | tf_op jit(solution)/shard_map/ppermute | solution.py:542
  39.8 17.5 %collective-permute-start.9 = (f32[2,256,128]{2,1,0:T(8,128)S(1)}, f32[2,256,128]{2,1,0:T(8,128)S(1)}, u32[]{:S(2)}, u32[]{:S(2)}) collective-permute-start(f32[2,256,128]{2,1,0:T(8,128)S(1)} %get-tuple-element.42), channel_id=1, source_target_pairs={{1,2},{3,4},{5,6},{7,8},{9,10},{11,12},{13,14},{15,16},{17,18},{19... | collective-permute-start | bytes 786440 | tf_op jit(solution)/shard_map/ppermute | solution.py:543
  46.4 11.0 %collective-permute-start.8 = (f32[2,256,128]{2,1,0:T(8,128)S(1)}, f32[2,256,128]{2,1,0:T(8,128)S(1)}, u32[]{:S(2)}, u32[]{:S(2)}) collective-permute-start(f32[2,256,128]{2,1,0:T(8,128)S(1)} %get-tuple-element.41), channel_id=1, source_target_pairs={{0,1},{2,3},{4,5},{6,7},{8,9},{10,11},{12,13},{14,15},{16,17},{18,... | collective-permute-start | bytes 786440 | tf_op jit(solution)/shard_map/ppermute | solution.py:543
  48.3 15.4 %collective-permute-start.7 = (f32[2,256,128]{2,1,0:T(8,128)S(1)}, f32[2,256,128]{2,1,0:T(8,128)S(1)}, u32[]{:S(2)}, u32[]{:S(2)}) collective-permute-start(f32[2,256,128]{2,1,0:T(8,128)S(1)} %get-tuple-element.39), channel_id=1, source_target_pairs={{1,258},{3,260},{5,262},{7,264},{9,266},{11,268},{13,270},{15,272}... | collective-permute-start | bytes 786440 | tf_op jit(solution)/shard_map/ppermute | solution.py:544
  55.4 9.1 %collective-permute-start.5 = (f32[2,256,128]{2,1,0:T(8,128)S(1)}, f32[2,256,128]{2,1,0:T(8,128)S(1)}, u32[]{:S(2)}, u32[]{:S(2)}) collective-permute-start(f32[2,256,128]{2,1,0:T(8,128)S(1)} %get-tuple-element.36), channel_id=1, source_target_pairs={{0,257},{2,259},{4,261},{6,263},{8,265},{10,267},{12,269},{14,271}... | collective-permute-start | bytes 786440 | tf_op jit(solution)/shard_map/ppermute | solution.py:544
